TPU v7x, 256 devices: a whole 4x4x8 slice. The times are simulated.
256 devices in a mesh: rows: 32 (over z, x), feat: 8 (over y, core).
Axes of the slice: x: 4, y: 4, z: 8, core: 2. Of those that a mesh axis runs over, the one named last changes fastest.
Arguments:
- tile_values: bfloat16 [8192, 512, 128], P('rows', 'feat'), may hold values from -6 to 6
- tile_blocks: int32 [8192, 512], P('rows', 'feat'), may hold values from 0 to 1023
- tile_counts: int32 [8192, 8], P('rows', 'feat'), may hold values from 1 to 64, as said below
- labels: int32 [8192], P('rows'), may hold values 0 or 1
- owner_rank: int32 [8192], P('rows'), may hold values from 0 to 31, as said below
- weights: float32 [8192, 128], P(('feat', 'rows')), may hold values from -0.09375 to 0.09375
Outputs:
- owned_margins: float32 [8192], P('rows')
- gradient: float32 [8192, 128], P(('feat', 'rows'))
- loss: float32 [], replicated
Inputs may be any that keep to these rules, and one draw needn't show every extreme that they name: `owner_rank`: within each aligned block of 256 examples, every owner is named by exactly 8 examples. `tile_counts`: in every aligned block of 256 examples, each shard's column holds at least one example with exactly 64 used slots.
All inputs are finite; a program needn't handle non-finite values. No bound on the sum of `labels` on one device may be relied on, other than what follows from the above.
Results may differ from a plain program's by a relative error of at most 0.003.
Values may be sent and summed in bfloat16 or wider, within the bound.
No kernel may reach another device: no remote copies, remote signals or barrier semaphores. Data moves between devices by JAX's collectives and lax.ppermute only.
A program may use at most 64 MiB of HBM per device.

v0:
```python
import math

import jax
import jax.numpy as jnp
from jax import lax
from jax.sharding import PartitionSpec as P


def sent_to_all(value, axis):
    peers = lax.axis_size(axis)
    return lax.all_to_all(
        jnp.broadcast_to(value[None], (peers, *value.shape)), axis, 0, 0, tiled=True
    )


def joined_along(blocks, dim):
    lengths = list(blocks.shape[1:])
    lengths[dim] *= blocks.shape[0]
    return jnp.moveaxis(blocks, 0, dim).reshape(lengths)


def collect(value, axis, dim):
    blocks = sent_to_all(value, axis)
    return joined_along(blocks, dim)


def taken_together(value, axis):
    return sent_to_all(value, axis).sum(axis=0)


def in_blocks(value, dim, peers):
    lengths = value.shape
    blocks = value.reshape(*lengths[:dim], peers, lengths[dim] // peers, *lengths[dim + 1 :])
    return jnp.moveaxis(blocks, dim, 0)


def sum_at_owner(value, axis, dim):
    blocks = in_blocks(value, dim, lax.axis_size(axis))
    arrived = lax.all_to_all(blocks, axis, split_axis=0, concat_axis=0, tiled=True)
    return arrived.sum(axis=0)


def on_device(tile_values, tile_blocks, tile_counts, labels, owner_rank, weights):
    examples = tile_values.shape[0]
    slot_count = tile_values.shape[1]
    tile_width = tile_values.shape[2]
    peer_count = lax.axis_size("rows")
    per_owner = examples // peer_count
    w_half = weights.astype(jnp.bfloat16)
    weight_table = collect(w_half, "rows", 0)
    owner_hits = (owner_rank[:, None] == jnp.arange(peer_count, dtype=jnp.int32)[None, :]).astype(
        jnp.int32
    )
    earlier = jnp.cumsum(owner_hits, axis=0) - owner_hits
    local_rank = jnp.sum(earlier * owner_hits, axis=1)
    position = owner_rank * per_owner + local_rank
    send_order = (
        jnp.zeros((examples,), jnp.int32).at[position].set(jnp.arange(examples, dtype=jnp.int32))
    )
    counts_here = tile_counts[:, 0]
    live_slot = jnp.arange(slot_count, dtype=jnp.int32)[None, :] < counts_here[:, None]
    picked = weight_table[tile_blocks]
    products = jnp.sum(tile_values.astype(jnp.float32) * picked.astype(jnp.float32), axis=2)
    partial_value = jnp.sum(jnp.where(live_slot, products, jnp.float32(0.0)), axis=1)
    margin = taken_together(partial_value, "feat")
    label_float = labels.astype(jnp.float32)
    residual = jax.nn.sigmoid(margin) - label_float
    loss_terms = jnp.sum(jax.nn.softplus(margin) - label_float * margin)
    loss = taken_together(loss_terms, "rows") / (examples * peer_count)
    resid_half = residual.astype(jnp.bfloat16)
    coefficient = jnp.where(live_slot, resid_half[:, None], jnp.zeros((), jnp.bfloat16))
    total_tiles = examples * slot_count
    block_rows = math.gcd(total_tiles, 1024)
    turn_count = total_tiles // block_rows
    flat_values = tile_values.reshape(turn_count, block_rows, tile_width)
    flat_blocks = tile_blocks.reshape(turn_count, block_rows)
    flat_coefficient = coefficient.reshape(turn_count, block_rows)
    row_count = weights.shape[0] * lax.axis_size("rows")
    candidates = jnp.arange(row_count, dtype=jnp.int32)

    def add_block(running, pieces):
        block_values, block_ids, block_coefficient = pieces
        matches = block_ids[:, None] == candidates[None, :]
        spread = jnp.where(matches, block_coefficient[:, None], jnp.zeros((), jnp.bfloat16))
        update = lax.dot_general(
            spread, block_values, (((0,), (0,)), ((), ())), preferred_element_type=jnp.float32
        )
        return (running + update, None)

    start_sum = jnp.zeros((row_count, tile_width), jnp.float32)
    summed, unused = lax.scan(add_block, start_sum, (flat_values, flat_blocks, flat_coefficient))
    gradient = sum_at_owner(summed, "rows", 0)
    ordered = margin[send_order].reshape(peer_count, per_owner)
    owned_margins = lax.all_to_all(
        ordered, "rows", split_axis=0, concat_axis=0, tiled=True
    ).reshape(examples)
    return (owned_margins, gradient, loss)


def solution(mesh):
    in_specs = (
        P("rows", "feat", None),
        P("rows", "feat"),
        P("rows", "feat"),
        P("rows"),
        P("rows"),
        P(("feat", "rows"), None),
    )
    out_specs = (P("rows"), P(("feat", "rows"), None), P())
    return jax.shard_map(
        on_device, mesh=mesh, in_specs=in_specs, out_specs=out_specs, check_vma=False
    )
```

profile of v0, /device:TPU:32, one launch (start us, length us, event | category | flops | bytes accessed | tf_op | source)
XLA Modules:
  0.0 195.4 jit_solution(1007062431974473650)
XLA Ops:
  0.6 0.7 convert_element_type.23
  1.4 0.7 broadcast_in_dim.71
  2.1 11.2 %all-to-all-start = ((bf16[32,32,128]{2,1,0:T(8,128)(2,1)}), bf16[32,32,128]{2,1,0:T(8,128)(2,1)S(1)}, u32[]{:S(2)}, u32[]{:S(2)}) async-start(bf16[32,32,128]{2,1,0:T(8,128)(2,1)} %broadcast_in_dim.71), calls=%async_computation | async-start | bytes 524288 | tf_op jit(solution)/shard_map/all_to_all | solution.py:11
  13.3 0.9 compare_select_fusion
  14.1 0.7 fusion.19
  14.8 0.6 reduce-window.6
  15.6 0.8 fusion.18
  16.4 0.7 compare_select_fusion.4
  17.1 1.4 scatter_custom_fusion
  18.7 6.7 %all-to-all-done = bf16[32,32,128]{2,1,0:T(8,128)(2,1)S(1)} async-done(((bf16[32,32,128]{2,1,0:T(8,128)(2,1)}), bf16[32,32,128]{2,1,0:T(8,128)(2,1)S(1)}, u32[]{:S(2)}, u32[]{:S(2)}) %all-to-all-start) | async-done | bytes 262176 | tf_op jit(solution)/shard_map/all_to_all | solution.py:11
  25.4 57.4 %gather_fusion = bf16[16384,128]{1,0:T(8,128)(2,1)} fusion(bf16[1024,128]{1,0:T(8,128)(2,1)S(1)} %bitcast.36, s32[16384]{0:T(1024)S(1)} %broadcast_clamp_fusion), kind=kCustom, calls=%fused_computation | custom fusion | bytes 8454144 | tf_op jit(solution)/shard_map/gather | solution.py:62
  82.8 5.7 %fusion.15 = f32[256,64]{1,0:T(8,128)S(1)} fusion(bf16[256,64,128]{2,1,0:T(8,128)(2,1)} %bitcast.37, bf16[256,64,128]{2,1,0:T(8,128)(2,1)} %param.8), kind=kLoop, calls=%fused_computation.18 | loop fusion | flops 8372224 | bytes 8454144 | tf_op jit(solution)/shard_map/reduce_sum | solution.py:63
  88.8 0.6 broadcast_in_dim.74
  89.4 4.5 %all-to-all-start.1 = ((f32[8,1,256]{2,1,0:T(1,128)}), f32[8,1,256]{2,1,0:T(1,128)S(1)}, u32[]{:S(2)}, u32[]{:S(2)}) async-start(f32[8,1,256]{2,1,0:T(1,128)} %broadcast_in_dim.74), calls=%async_computation.1 | async-start | bytes 16384 | tf_op jit(solution)/shard_map/all_to_all | solution.py:11
  94.1 0.5 broadcast.73
  94.6 0.7 reduce.13
  95.6 3.5 %all-to-all-done.1 = f32[8,1,256]{2,1,0:T(1,128)S(1)} async-done(((f32[8,1,256]{2,1,0:T(1,128)}), f32[8,1,256]{2,1,0:T(1,128)S(1)}, u32[]{:S(2)}, u32[]{:S(2)}) %all-to-all-start.1) | async-done | bytes 8224 | tf_op jit(solution)/shard_map/all_to_all | solution.py:11
  99.2 0.6 fusion.21
  100.1 1.3 broadcast_in_dim.82
  101.4 4.6 %all-to-all-start.4 = ((f32[32,1,1]{2,1,0:T(1,128)}), f32[32,1,1]{2,1,0:T(1,128)S(1)}, u32[]{:S(2)}, u32[]{:S(2)}) async-start(f32[32,1,1]{2,1,0:T(1,128)} %broadcast_in_dim.82), calls=%async_computation.4 | async-start | bytes 32768 | tf_op jit(solution)/shard_map/all_to_all | solution.py:11
  106.0 1.9 gather_fusion.1
  108.0 0.7 all_to_all.22
  108.7 5.9 %all-to-all-done.4 = f32[32,1,1]{2,1,0:T(1,128)S(1)} async-done(((f32[32,1,1]{2,1,0:T(1,128)}), f32[32,1,1]{2,1,0:T(1,128)S(1)}, u32[]{:S(2)}, u32[]{:S(2)}) %all-to-all-start.4) | async-done | bytes 160 | tf_op jit(solution)/shard_map/all_to_all | solution.py:11
  114.6 4.9 %all-to-all-start.2 = ((f32[32,1,8]{2,1,0:T(1,128)}), f32[32,1,8]{2,1,0:T(1,128)S(1)}, u32[]{:S(2)}, u32[]{:S(2)}) async-start(f32[32,1,8]{2,1,0:T(1,128)} %bitcast.5), calls=%async_computation.2 | async-start | bytes 32768 | tf_op jit(solution)/shard_map/all_to_all | solution.py:94
  119.5 48.5 %while.11 = (s32[]{:T(128)}, f32[1024,128]{1,0:T(8,128)}, s32[16,1024]{1,0:T(8,128)S(1)}, bf16[16,1024]{1,0:T(8,128)(2,1)S(1)}, bf16[16,1024,128]{2,1,0:T(8,128)(2,1)}, /*index=5*/s32[]{:T(128)}, s32[]{:T(128)}) while((s32[]{:T(128)}, f32[1024,128]{1,0:T(8,128)}, s32[16,1024]{1,0:T(8,128)S(1)}, bf16[16,1024]{1,0:T(8,128)(2,1)S(1)}, ...), condition=%wide.region_8.9_spmd.clone, body=%wide.region_7.8_spmd.clone.sunk | while | flops 270794752 | bytes 1329259 | solution.py:91
  119.6 2.8 %fusion.30 = f32[1024,128]{1,0:T(8,128)} fusion(s32[1024]{0:T(1024)S(1)} %bitcast.39, bf16[1024]{0:T(1024)(128)(2,1)S(1)} %dynamic-slice_reduce_fusion.2, f32[1024,128]{1,0:T(8,128)} %get-tuple-element.107, bf16[16,1024,128]{2,1,0:T(8,128)(2,1)} %get-tuple-element.117, s32[]{:T(128)S(6)} %copy.35, pred[]{:T(512)S(6)} %compare.3), kind=kOutput, calls=%fused_computation.8.clone.1 | convolution fusion | flops 270794752 | bytes 1316869 | tf_op jit(solution)/shard_map/while/body/eval_jaxpr/dot_general | solution.py:85
  122.4 3.0 %fusion.30 = f32[1024,128]{1,0:T(8,128)} fusion(s32[1024]{0:T(1024)S(1)} %bitcast.39, bf16[1024]{0:T(1024)(128)(2,1)S(1)} %dynamic-slice_reduce_fusion.2, f32[1024,128]{1,0:T(8,128)} %get-tuple-element.107, bf16[16,1024,128]{2,1,0:T(8,128)(2,1)} %get-tuple-element.117, s32[]{:T(128)S(6)} %copy.35, pred[]{:T(512)S(6)} %compare.3), kind=kOutput, calls=%fused_computation.8.clone.1 | convolution fusion | flops 270794752 | bytes 1316869 | tf_op jit(solution)/shard_map/while/body/eval_jaxpr/dot_general | solution.py:85
  125.5 3.0 %fusion.30 = f32[1024,128]{1,0:T(8,128)} fusion(s32[1024]{0:T(1024)S(1)} %bitcast.39, bf16[1024]{0:T(1024)(128)(2,1)S(1)} %dynamic-slice_reduce_fusion.2, f32[1024,128]{1,0:T(8,128)} %get-tuple-element.107, bf16[16,1024,128]{2,1,0:T(8,128)(2,1)} %get-tuple-element.117, s32[]{:T(128)S(6)} %copy.35, pred[]{:T(512)S(6)} %compare.3), kind=kOutput, calls=%fused_computation.8.clone.1 | convolution fusion | flops 270794752 | bytes 1316869 | tf_op jit(solution)/shard_map/while/body/eval_jaxpr/dot_general | solution.py:85
  128.5 3.0 %fusion.30 = f32[1024,128]{1,0:T(8,128)} fusion(s32[1024]{0:T(1024)S(1)} %bitcast.39, bf16[1024]{0:T(1024)(128)(2,1)S(1)} %dynamic-slice_reduce_fusion.2, f32[1024,128]{1,0:T(8,128)} %get-tuple-element.107, bf16[16,1024,128]{2,1,0:T(8,128)(2,1)} %get-tuple-element.117, s32[]{:T(128)S(6)} %copy.35, pred[]{:T(512)S(6)} %compare.3), kind=kOutput, calls=%fused_computation.8.clone.1 | convolution fusion | flops 270794752 | bytes 1316869 | tf_op jit(solution)/shard_map/while/body/eval_jaxpr/dot_general | solution.py:85
  131.6 3.0 %fusion.30 = f32[1024,128]{1,0:T(8,128)} fusion(s32[1024]{0:T(1024)S(1)} %bitcast.39, bf16[1024]{0:T(1024)(128)(2,1)S(1)} %dynamic-slice_reduce_fusion.2, f32[1024,128]{1,0:T(8,128)} %get-tuple-element.107, bf16[16,1024,128]{2,1,0:T(8,128)(2,1)} %get-tuple-element.117, s32[]{:T(128)S(6)} %copy.35, pred[]{:T(512)S(6)} %compare.3), kind=kOutput, calls=%fused_computation.8.clone.1 | convolution fusion | flops 270794752 | bytes 1316869 | tf_op jit(solution)/shard_map/while/body/eval_jaxpr/dot_general | solution.py:85
  134.6 3.0 %fusion.30 = f32[1024,128]{1,0:T(8,128)} fusion(s32[1024]{0:T(1024)S(1)} %bitcast.39, bf16[1024]{0:T(1024)(128)(2,1)S(1)} %dynamic-slice_reduce_fusion.2, f32[1024,128]{1,0:T(8,128)} %get-tuple-element.107, bf16[16,1024,128]{2,1,0:T(8,128)(2,1)} %get-tuple-element.117, s32[]{:T(128)S(6)} %copy.35, pred[]{:T(512)S(6)} %compare.3), kind=kOutput, calls=%fused_computation.8.clone.1 | convolution fusion | flops 270794752 | bytes 1316869 | tf_op jit(solution)/shard_map/while/body/eval_jaxpr/dot_general | solution.py:85
  137.6 3.0 %fusion.30 = f32[1024,128]{1,0:T(8,128)} fusion(s32[1024]{0:T(1024)S(1)} %bitcast.39, bf16[1024]{0:T(1024)(128)(2,1)S(1)} %dynamic-slice_reduce_fusion.2, f32[1024,128]{1,0:T(8,128)} %get-tuple-element.107, bf16[16,1024,128]{2,1,0:T(8,128)(2,1)} %get-tuple-element.117, s32[]{:T(128)S(6)} %copy.35, pred[]{:T(512)S(6)} %compare.3), kind=kOutput, calls=%fused_computation.8.clone.1 | convolution fusion | flops 270794752 | bytes 1316869 | tf_op jit(solution)/shard_map/while/body/eval_jaxpr/dot_general | solution.py:85
  140.7 3.0 %fusion.30 = f32[1024,128]{1,0:T(8,128)} fusion(s32[1024]{0:T(1024)S(1)} %bitcast.39, bf16[1024]{0:T(1024)(128)(2,1)S(1)} %dynamic-slice_reduce_fusion.2, f32[1024,128]{1,0:T(8,128)} %get-tuple-element.107, bf16[16,1024,128]{2,1,0:T(8,128)(2,1)} %get-tuple-element.117, s32[]{:T(128)S(6)} %copy.35, pred[]{:T(512)S(6)} %compare.3), kind=kOutput, calls=%fused_computation.8.clone.1 | convolution fusion | flops 270794752 | bytes 1316869 | tf_op jit(solution)/shard_map/while/body/eval_jaxpr/dot_general | solution.py:85
  143.7 3.0 %fusion.30 = f32[1024,128]{1,0:T(8,128)} fusion(s32[1024]{0:T(1024)S(1)} %bitcast.39, bf16[1024]{0:T(1024)(128)(2,1)S(1)} %dynamic-slice_reduce_fusion.2, f32[1024,128]{1,0:T(8,128)} %get-tuple-element.107, bf16[16,1024,128]{2,1,0:T(8,128)(2,1)} %get-tuple-element.117, s32[]{:T(128)S(6)} %copy.35, pred[]{:T(512)S(6)} %compare.3), kind=kOutput, calls=%fused_computation.8.clone.1 | convolution fusion | flops 270794752 | bytes 1316869 | tf_op jit(solution)/shard_map/while/body/eval_jaxpr/dot_general | solution.py:85
  146.8 3.0 %fusion.30 = f32[1024,128]{1,0:T(8,128)} fusion(s32[1024]{0:T(1024)S(1)} %bitcast.39, bf16[1024]{0:T(1024)(128)(2,1)S(1)} %dynamic-slice_reduce_fusion.2, f32[1024,128]{1,0:T(8,128)} %get-tuple-element.107, bf16[16,1024,128]{2,1,0:T(8,128)(2,1)} %get-tuple-element.117, s32[]{:T(128)S(6)} %copy.35, pred[]{:T(512)S(6)} %compare.3), kind=kOutput, calls=%fused_computation.8.clone.1 | convolution fusion | flops 270794752 | bytes 1316869 | tf_op jit(solution)/shard_map/while/body/eval_jaxpr/dot_general | solution.py:85
  149.8 3.0 %fusion.30 = f32[1024,128]{1,0:T(8,128)} fusion(s32[1024]{0:T(1024)S(1)} %bitcast.39, bf16[1024]{0:T(1024)(128)(2,1)S(1)} %dynamic-slice_reduce_fusion.2, f32[1024,128]{1,0:T(8,128)} %get-tuple-element.107, bf16[16,1024,128]{2,1,0:T(8,128)(2,1)} %get-tuple-element.117, s32[]{:T(128)S(6)} %copy.35, pred[]{:T(512)S(6)} %compare.3), kind=kOutput, calls=%fused_computation.8.clone.1 | convolution fusion | flops 270794752 | bytes 1316869 | tf_op jit(solution)/shard_map/while/body/eval_jaxpr/dot_general | solution.py:85
  152.8 3.0 %fusion.30 = f32[1024,128]{1,0:T(8,128)} fusion(s32[1024]{0:T(1024)S(1)} %bitcast.39, bf16[1024]{0:T(1024)(128)(2,1)S(1)} %dynamic-slice_reduce_fusion.2, f32[1024,128]{1,0:T(8,128)} %get-tuple-element.107, bf16[16,1024,128]{2,1,0:T(8,128)(2,1)} %get-tuple-element.117, s32[]{:T(128)S(6)} %copy.35, pred[]{:T(512)S(6)} %compare.3), kind=kOutput, calls=%fused_computation.8.clone.1 | convolution fusion | flops 270794752 | bytes 1316869 | tf_op jit(solution)/shard_map/while/body/eval_jaxpr/dot_general | solution.py:85
  155.9 3.0 %fusion.30 = f32[1024,128]{1,0:T(8,128)} fusion(s32[1024]{0:T(1024)S(1)} %bitcast.39, bf16[1024]{0:T(1024)(128)(2,1)S(1)} %dynamic-slice_reduce_fusion.2, f32[1024,128]{1,0:T(8,128)} %get-tuple-element.107, bf16[16,1024,128]{2,1,0:T(8,128)(2,1)} %get-tuple-element.117, s32[]{:T(128)S(6)} %copy.35, pred[]{:T(512)S(6)} %compare.3), kind=kOutput, calls=%fused_computation.8.clone.1 | convolution fusion | flops 270794752 | bytes 1316869 | tf_op jit(solution)/shard_map/while/body/eval_jaxpr/dot_general | solution.py:85
  158.9 3.0 %fusion.30 = f32[1024,128]{1,0:T(8,128)} fusion(s32[1024]{0:T(1024)S(1)} %bitcast.39, bf16[1024]{0:T(1024)(128)(2,1)S(1)} %dynamic-slice_reduce_fusion.2, f32[1024,128]{1,0:T(8,128)} %get-tuple-element.107, bf16[16,1024,128]{2,1,0:T(8,128)(2,1)} %get-tuple-element.117, s32[]{:T(128)S(6)} %copy.35, pred[]{:T(512)S(6)} %compare.3), kind=kOutput, calls=%fused_computation.8.clone.1 | convolution fusion | flops 270794752 | bytes 1316869 | tf_op jit(solution)/shard_map/while/body/eval_jaxpr/dot_general | solution.py:85
  162.0 3.0 %fusion.30 = f32[1024,128]{1,0:T(8,128)} fusion(s32[1024]{0:T(1024)S(1)} %bitcast.39, bf16[1024]{0:T(1024)(128)(2,1)S(1)} %dynamic-slice_reduce_fusion.2, f32[1024,128]{1,0:T(8,128)} %get-tuple-element.107, bf16[16,1024,128]{2,1,0:T(8,128)(2,1)} %get-tuple-element.117, s32[]{:T(128)S(6)} %copy.35, pred[]{:T(512)S(6)} %compare.3), kind=kOutput, calls=%fused_computation.8.clone.1 | convolution fusion | flops 270794752 | bytes 1316869 | tf_op jit(solution)/shard_map/while/body/eval_jaxpr/dot_general | solution.py:85
  165.0 3.0 %fusion.30 = f32[1024,128]{1,0:T(8,128)} fusion(s32[1024]{0:T(1024)S(1)} %bitcast.39, bf16[1024]{0:T(1024)(128)(2,1)S(1)} %dynamic-slice_reduce_fusion.2, f32[1024,128]{1,0:T(8,128)} %get-tuple-element.107, bf16[16,1024,128]{2,1,0:T(8,128)(2,1)} %get-tuple-element.117, s32[]{:T(128)S(6)} %copy.35, pred[]{:T(512)S(6)} %compare.3), kind=kOutput, calls=%fused_computation.8.clone.1 | convolution fusion | flops 270794752 | bytes 1316869 | tf_op jit(solution)/shard_map/while/body/eval_jaxpr/dot_general | solution.py:85
  168.0 9.9 %all-to-all-start.3 = ((f32[32,32,128]{2,1,0:T(8,128)}), f32[32,32,128]{2,1,0:T(8,128)S(1)}, u32[]{:S(2)}, u32[]{:S(2)}) async-start(f32[32,32,128]{2,1,0:T(8,128)} %bitcast.7), calls=%async_computation.3 | async-start | bytes 1048576 | tf_op jit(solution)/shard_map/all_to_all | solution.py:39
  177.9 0.6 reduce_sum.69
  179.1 0.5 broadcast.72
  179.7 0.7 reduce.12
  180.4 0.7 reshape.68
  181.0 12.6 %all-to-all-done.3 = f32[32,32,128]{2,1,0:T(8,128)S(1)} async-done(((f32[32,32,128]{2,1,0:T(8,128)}), f32[32,32,128]{2,1,0:T(8,128)S(1)}, u32[]{:S(2)}, u32[]{:S(2)}) %all-to-all-start.3) | async-done | bytes 524320 | tf_op jit(solution)/shard_map/all_to_all | solution.py:39
  193.6 0.6 reduce_sum.67
  (62 shorter events, 2.1 us)
Async XLA Ops:
  2.1 23.4 %all-to-all-start = ((bf16[32,32,128]{2,1,0:T(8,128)(2,1)}), bf16[32,32,128]{2,1,0:T(8,128)(2,1)S(1)}, u32[]{:S(2)}, u32[]{:S(2)}) async-start(bf16[32,32,128]{2,1,0:T(8,128)(2,1)} %broadcast_in_dim.71), calls=%async_computation | async-start | bytes 524288 | tf_op jit(solution)/shard_map/all_to_all | solution.py:11
  82.8 5.8 %copy-start.1 = (s32[256,1]{0,1:T(1,128)S(1)}, s32[256,1]{0,1:T(1,128)}, u32[]{:S(2)}) copy-start(s32[256,1]{0,1:T(1,128)} %param.10) | copy-start | bytes 3076
  82.8 11.0 %copy-start = (s32[256,64]{0,1:T(8,128)S(1)}, s32[256,64]{0,1:T(8,128)}, u32[]{:S(2)}) copy-start(s32[256,64]{0,1:T(8,128)} %param.9) | copy-start | bytes 196612
  82.8 16.4 %copy-start.2 = (s32[256]{0:T(256)S(1)}, s32[256]{0:T(256)}, u32[]{:S(2)}) copy-start(s32[256]{0:T(256)} %param.11) | copy-start | bytes 3076
  89.4 9.8 %all-to-all-start.1 = ((f32[8,1,256]{2,1,0:T(1,128)}), f32[8,1,256]{2,1,0:T(1,128)S(1)}, u32[]{:S(2)}, u32[]{:S(2)}) async-start(f32[8,1,256]{2,1,0:T(1,128)} %broadcast_in_dim.74), calls=%async_computation.1 | async-start | bytes 16384 | tf_op jit(solution)/shard_map/all_to_all | solution.py:11
  101.4 13.2 %all-to-all-start.4 = ((f32[32,1,1]{2,1,0:T(1,128)}), f32[32,1,1]{2,1,0:T(1,128)S(1)}, u32[]{:S(2)}, u32[]{:S(2)}) async-start(f32[32,1,1]{2,1,0:T(1,128)} %broadcast_in_dim.82), calls=%async_computation.4 | async-start | bytes 32768 | tf_op jit(solution)/shard_map/all_to_all | solution.py:11
  114.6 53.4 %all-to-all-start.2 = ((f32[32,1,8]{2,1,0:T(1,128)}), f32[32,1,8]{2,1,0:T(1,128)S(1)}, u32[]{:S(2)}, u32[]{:S(2)}) async-start(f32[32,1,8]{2,1,0:T(1,128)} %bitcast.5), calls=%async_computation.2 | async-start | bytes 32768 | tf_op jit(solution)/shard_map/all_to_all | solution.py:94
  168.0 25.6 %all-to-all-start.3 = ((f32[32,32,128]{2,1,0:T(8,128)}), f32[32,32,128]{2,1,0:T(8,128)S(1)}, u32[]{:S(2)}, u32[]{:S(2)}) async-start(f32[32,32,128]{2,1,0:T(8,128)} %bitcast.7), calls=%async_computation.3 | async-start | bytes 1048576 | tf_op jit(solution)/shard_map/all_to_all | solution.py:39
where the time goes:
time: 196 us; the launch traced here: 195 us
  local copies, waits for them, and re-layouts  67.5 us (34%)
  matrix products  47.7 us (24%)
  starting transfers between devices  35 us (18%)
  waiting for transfers between devices  28.8 us (15%)
  other arithmetic  13.6 us (7%)
  between operations  2.58 us (1%)
    gather x1, local copies, waits for them, and re-layouts, on_device(): picked = weight_table[tile_blocks]  57.4 us
    dot_general x16, matrix products, add_block(): lax.dot_general(spread, block_values, (((0,), (0,)), ((), ())), preferred...  47.7 us
    all_to_all x3, starting transfers between devices, sent_to_all(): lax.all_to_all(jnp.broadcast_to(value[None], (peers, *value.shape)), axis...  20.3 us
    all_to_all x3, waiting for transfers between devices, sent_to_all(): lax.all_to_all(jnp.broadcast_to(value[None], (peers, *value.shape)), axis...  16.2 us
    all_to_all x1, waiting for transfers between devices, sum_at_owner(): lax.all_to_all(blocks, axis, split_axis=0, concat_axis=0, tiled=True)  12.6 us
    all_to_all x1, starting transfers between devices, sum_at_owner(): lax.all_to_all(blocks, axis, split_axis=0, concat_axis=0, tiled=True)  9.87 us
    reduce_sum x1, other arithmetic, on_device(): jnp.sum(tile_values.astype(jnp.float32) * picked.astype(jnp.float32), axi...  5.74 us
    all_to_all x1, starting transfers between devices, on_device(): lax.all_to_all(ordered, 'rows', split_axis=0, concat_axis=0, tiled=True)  4.9 us
  transfers between devices with their start and end apart: 5, of which 4 were waited for; matrix products, arithmetic and copies ran while one was open for 31% of the time, Pallas kernels for 0%

commit v1 on v0

v1 whole, which is shorter than its diff:
```python
import jax
import jax.numpy as jnp
from jax import lax
from jax.experimental import pallas as pl
from jax.experimental.pallas import tpu as pltpu
from jax.sharding import PartitionSpec as P

F32 = jnp.float32
BF16 = jnp.bfloat16
I32 = jnp.int32

E = 256
SLOT = 64
C = 128
B = 1024
R = 32
F = 8
OWN = 8
GR = 8
NG = E * SLOT // GR
CH = 256
GCH = CH // GR
NCH = NG // GCH
XR = 8
LOADS = 4

VMEM = pl.BlockSpec(memory_space=pltpu.VMEM)
SMEM = pl.BlockSpec(memory_space=pltpu.SMEM)
ANY = pl.BlockSpec(memory_space=pl.ANY)


def nt(a, b):
    return lax.dot_general(a, b, (((1,), (1,)), ((), ())), preferred_element_type=F32)


def nn(a, b):
    return lax.dot_general(a, b, (((1,), (0,)), ((), ())), preferred_element_type=F32)


def split3(x):
    hi = x.astype(BF16).astype(F32)
    mid = (x - hi).astype(BF16).astype(F32)
    lo = (x - hi - mid).astype(BF16).astype(F32)
    return hi, mid, lo


def iota(shape, dim):
    return lax.broadcasted_iota(I32, shape, dim)


def spread_weights(w_ref, out_ref):
    out_ref[...] = jnp.broadcast_to(w_ref[...].astype(BF16)[None], out_ref.shape)


def pack_tiles(
    counts_s, counts_ref, blocks_ref, owner_ref, values_hbm, packed_hbm, ids_ref, ex_ref, rank_ref,
    total_ref, values, packed_ref, sems, out_sem
):
    part = NG // LOADS

    def load(i):
        return pltpu.make_async_copy(
            values_hbm.at[pl.ds(i * part, part)], values.at[pl.ds(i * part, part)], sems.at[i]
        )

    for i in range(LOADS):
        load(i).start()

    counts = counts_ref[...]
    granules = lax.shift_right_logical(counts + (GR - 1), 3).astype(F32)
    spread = jnp.broadcast_to(granules, (E, E)).astype(BF16)
    up = iota((E, E), 0)
    across = iota((E, E), 1)
    first = nt((across < up).astype(F32).astype(BF16), spread)
    last = nt((across <= up).astype(F32).astype(BF16), spread)
    before = (up < across).astype(F32).astype(BF16)
    start = nn(spread[0:16], before)
    start_hi = jnp.floor(start * (1.0 / 64.0))
    start_lo = start - 64.0 * start_hi
    row16 = iota((16, E), 0)
    tail = jnp.where(row16 == 0, start_hi, jnp.where(row16 == 1, start_lo, iota((16, E), 1).astype(F32)))
    ids = jnp.where(iota((SLOT, E), 0) < counts, blocks_ref[...], 2047)
    both = jnp.concatenate([lax.shift_right_logical(ids, 5), ids & 31], axis=0).astype(F32)
    table = jnp.concatenate([both, tail], axis=0).astype(BF16)
    lane = iota((1, CH), 1)
    sub = iota((SLOT, CH), 0).astype(F32)
    total = jnp.sum(granules).astype(I32)
    total_ref[0] = total

    def place(k, carry):
        pos = k * CH + lane
        gran = lax.shift_right_logical(pos, 3).astype(F32)
        hit = (first <= gran) & (gran < last)
        x = nn(table, jnp.where(hit, 1.0, 0.0).astype(BF16))
        slot = pos.astype(F32) - 8.0 * (64.0 * x[128:129] + x[129:130])
        code = 32.0 * x[0:64] + x[64:128]
        here = jnp.sum(jnp.where(sub == slot, code, 0.0), axis=0, keepdims=True).astype(I32)
        live = (pos < total * GR) & (here < B)
        ids_ref[k] = jnp.where(live, here, -1)
        ex_ref[k] = x[130:131].astype(I32)
        return carry

    chunks = lax.shift_right_logical(total + (GCH - 1), 5)
    lax.fori_loop(0, chunks, place, 0)

    hits = (iota((R, E), 0) == owner_ref[...]).astype(F32)
    earlier = nn(hits.astype(BF16), before)
    rank_ref[...] = jnp.sum(hits * earlier, axis=0, keepdims=True).astype(I32)

    def put(e, off):
        packed_ref[pl.ds(off, 8)] = values[pl.ds(e * 8, 8)]
        return off + lax.shift_right_logical(counts_s[e] + (GR - 1), 3)

    off = 0
    for i in range(LOADS):
        load(i).wait()
        off = lax.fori_loop(i * (E // LOADS), (i + 1) * (E // LOADS), put, off, unroll=8)
    packed_ref[pl.ds(off, GCH)] = jnp.zeros((GCH, GR, C), BF16)

    def send(k, carry):
        span = pl.ds(k * GCH, GCH)
        pltpu.make_async_copy(packed_ref.at[span], packed_hbm.at[span], out_sem).start()
        return carry

    lax.fori_loop(0, chunks, send, 0)
    whole = pl.ds(0, chunks * GCH)
    pltpu.make_async_copy(packed_ref.at[whole], packed_hbm.at[whole], out_sem).wait()


def start_chunks(packed_hbm, buf, sems, chunks):
    def go(k, carry):
        span = pl.ds(k * GCH, GCH)
        pltpu.make_async_copy(packed_hbm.at[span], buf.at[span], sems.at[k]).start()
        return carry

    lax.fori_loop(0, chunks, go, 0)


def wait_chunk(packed_hbm, buf, sems, k):
    span = pl.ds(k * GCH, GCH)
    pltpu.make_async_copy(packed_hbm.at[span], buf.at[span], sems.at[k]).wait()
    return buf[span].reshape(CH, C)


def margins_kernel(total_ref, w_ref, ids_ref, ex_ref, packed_hbm, out_ref, buf, acc, sems):
    chunks = lax.shift_right_logical(total_ref[0] + (GCH - 1), 5)
    start_chunks(packed_hbm, buf, sems, chunks)
    acc[...] = jnp.zeros_like(acc)
    rows = iota((E, CH), 0)
    sub8 = iota((8, CH), 0)

    def step(k, carry):
        v = wait_chunk(packed_hbm, buf, sems, k)
        ids = ids_ref[k]
        score = nt(w_ref[...], v)
        half = B // 2
        while half >= 8:
            bit = jnp.broadcast_to((ids & half) != 0, (half, CH))
            score = jnp.where(bit, score[half:], score[:half])
            half //= 2
        pick = jnp.sum(jnp.where(sub8 == (ids & 7), score, 0.0), axis=0, keepdims=True)
        pick = jnp.where(ids >= 0, pick, 0.0)
        acc[...] += jnp.where(rows == ex_ref[k], pick, 0.0)
        return carry

    lax.fori_loop(0, chunks, step, 0)
    row = jnp.sum(acc[...].T, axis=0, keepdims=True)
    out_ref[...] = jnp.broadcast_to(row[None], out_ref.shape)


def gradient_kernel(
    total_ref, parts_ref, labels_ref, owner_ref, rank_ref, ids_ref, ex_ref, packed_hbm, out_ref,
    buf, acc, sems
):
    chunks = lax.shift_right_logical(total_ref[0] + (GCH - 1), 5)
    start_chunks(packed_hbm, buf, sems, chunks)
    margin = jnp.sum(parts_ref[...].reshape(F, E), axis=0, keepdims=True)
    label = labels_ref[...].astype(F32)
    resid = jax.nn.sigmoid(margin) - label
    small = jnp.exp(-jnp.abs(margin))
    loss = jnp.sum(jnp.maximum(margin, 0.0) + jnp.log1p(small) - label * margin)
    half = resid.astype(BF16).astype(F32)
    column = jnp.broadcast_to(half, (C, E)).T
    column = jnp.concatenate([column, column], axis=1)
    rows = iota((E, CH), 0)
    lo_rows = iota((32, CH), 0)
    acc[...] = jnp.zeros_like(acc)

    def step(k, carry):
        v = wait_chunk(packed_hbm, buf, sems, k)
        ids = ids_ref[k]
        coef = jnp.sum(jnp.where(rows == ex_ref[k], column, 0.0), axis=0, keepdims=True)
        coef = jnp.where(ids >= 0, coef, 0.0)
        low = jnp.where(lo_rows == (ids & 31), coef, 0.0).astype(BF16)
        high = lax.shift_right_arithmetic(ids, 5)
        pieces = []
        for h in range(32):
            mask = jnp.broadcast_to(jnp.where(high == h, 1.0, 0.0), (32, CH)).astype(BF16)
            pieces.append(low * mask)
        spread = jnp.concatenate(pieces, axis=0)
        acc[...] += nn(spread, v)
        return carry

    lax.fori_loop(0, chunks, step, 0)
    out_ref[:, 0:32, :] = acc[...].reshape(R, 32, C).astype(BF16)

    owner_hit = iota((R, E), 0) == owner_ref[...]
    rank = rank_ref[...]
    lane_row = iota((C, E), 0)
    extra = jnp.zeros((R, C), F32)
    for i, piece in enumerate(split3(margin)):
        a = jnp.where(owner_hit, piece, 0.0).astype(BF16)
        b = jnp.where(lane_row == rank + OWN * i, 1.0, 0.0).astype(BF16)
        extra = extra + nt(a, b)
    lane = iota((R, C), 1)
    for i, piece in enumerate(split3(jnp.full((R, C), loss, F32))):
        extra = jnp.where(lane == 3 * OWN + i, piece, extra)
    out_ref[:, 32 : 32 + XR, :] = jnp.broadcast_to(extra[:, None, :], (R, XR, C)).astype(BF16)


def finish_kernel(in_ref, grad_ref, owned_ref, loss_ref):
    total = in_ref[0, 0:32, :].astype(F32)
    for r in range(1, R):
        total = total + in_ref[r, 0:32, :].astype(F32)
    grad_ref[...] = total
    extra = in_ref[:, 32 : 32 + XR, :].astype(F32)[:, 0, :]
    src = iota((C, E), 0)
    pick = jnp.where((src < 3 * OWN) & ((src & 7) == (iota((C, E), 1) & 7)), 1.0, 0.0)
    wide = nn(extra.astype(BF16), pick.astype(BF16))
    own = lax.shift_right_logical(iota((R, E), 1), 3) == iota((R, E), 0)
    owned_ref[...] = jnp.sum(jnp.where(own, wide, 0.0), axis=0, keepdims=True)
    lane = iota((R, C), 1)
    keep = (lane >= 3 * OWN) & (lane < 3 * OWN + 3)
    total_loss = jnp.sum(jnp.where(keep, extra, 0.0), keepdims=True)
    loss_ref[...] = total_loss * (1.0 / (E * R))


def local(body, out_shapes, in_specs, out_specs, scratch, limit, *args):
    return pl.pallas_call(
        body,
        out_shape=out_shapes,
        in_specs=in_specs,
        out_specs=out_specs,
        scratch_shapes=scratch,
        compiler_params=pltpu.CompilerParams(vmem_limit_bytes=limit << 20),
    )(*args)


def near(x):
    return pltpu.with_memory_space_constraint(x, pltpu.VMEM)


def far(x):
    return pltpu.with_memory_space_constraint(x, pltpu.HBM)


def on_device(tile_values, tile_blocks, tile_counts, labels, owner_rank, weights):
    shape = jax.ShapeDtypeStruct
    spread = local(
        spread_weights, pltpu.VMEM((R, B // R, C), BF16), [VMEM], VMEM, (), 8, weights
    )
    table = lax.all_to_all(spread, "rows", 0, 0, tiled=True).reshape(B, C)
    owner_row = owner_rank.reshape(1, E)
    label_row = labels.reshape(1, E)
    packed, ids, ex, rank, total = local(
        pack_tiles,
        (
            pltpu.HBM((NG, GR, C), BF16),
            pltpu.VMEM((NCH, 1, CH), I32),
            pltpu.VMEM((NCH, 1, CH), I32),
            pltpu.VMEM((1, E), I32),
            shape((1,), I32),
        ),
        [SMEM, VMEM, VMEM, VMEM, ANY],
        (ANY, VMEM, VMEM, VMEM, SMEM),
        [
            pltpu.VMEM((NG, GR, C), BF16),
            pltpu.VMEM((NG + GCH, GR, C), BF16),
            pltpu.SemaphoreType.DMA((LOADS,)),
            pltpu.SemaphoreType.DMA(()),
        ],
        20,
        tile_counts.reshape(E), tile_counts.T, tile_blocks.T, owner_row,
        far(tile_values.reshape(NG, GR, C)),
    )
    partial = local(
        margins_kernel, pltpu.VMEM((F, 1, E), F32), [SMEM, VMEM, VMEM, VMEM, ANY], VMEM,
        [pltpu.VMEM((NG, GR, C), BF16), pltpu.VMEM((E, CH), F32), pltpu.SemaphoreType.DMA((NCH,))], 16,
        total, near(table), near(ids), near(ex), far(packed),
    )
    parts = lax.all_to_all(partial, "feat", 0, 0, tiled=True)
    payload = local(
        gradient_kernel, pltpu.VMEM((R, B // R + XR, C), BF16),
        [SMEM, VMEM, VMEM, VMEM, VMEM, VMEM, VMEM, ANY], VMEM,
        [pltpu.VMEM((NG, GR, C), BF16), pltpu.VMEM((B, C), F32), pltpu.SemaphoreType.DMA((NCH,))], 16,
        total, near(parts), label_row, owner_row, near(rank), near(ids), near(ex), far(packed),
    )
    arrived = lax.all_to_all(payload, "rows", 0, 0, tiled=True)
    gradient, owned, loss = local(
        finish_kernel,
        (shape((B // R, C), F32), shape((1, E), F32), shape((1, 1), F32)),
        [VMEM], (VMEM, VMEM, VMEM), (), 8, near(arrived),
    )
    return owned.reshape(E), gradient, loss.reshape(())


def solution(mesh):
    in_specs = (
        P("rows", "feat", None),
        P("rows", "feat"),
        P("rows", "feat"),
        P("rows"),
        P("rows"),
        P(("feat", "rows"), None),
    )
    out_specs = (P("rows"), P(("feat", "rows"), None), P())
    return jax.shard_map(
        on_device, mesh=mesh, in_specs=in_specs, out_specs=out_specs, check_vma=False
    )
```

time: 196 us -> 73 us (0.37)
  local copies, waits for them, and re-layouts: 67.5 us -> 2.91 us
  matrix products: 47.7 us -> 0 us
  blocking collectives: 0 us -> 33.1 us
  waiting for transfers between devices: 28.8 us -> 4.41 us
  starting transfers between devices: 35 us -> 11.2 us
  Pallas kernels: 0 us -> 19.9 us
  other arithmetic: 13.6 us -> 0 us
    gather x2 -> x0, local copies, waits for them, and re-layouts: 59.3 us -> none  [the longest x1 57.4 us: on_device(): picked = weight_table[tile_blocks]]
    dot_general x16 -> x0, matrix products: 47.7 us -> none  [add_block(): lax.dot_general(spread, block_values, (((0,), (0,)), ((), ())), preferred...]
    all_to_all x0 -> x2, blocking collectives: none -> 33.1 us  [the longest x1 23.5 us: on_device(): arrived = lax.all_to_all(payload, 'rows', 0, 0, tiled=True)]
    all_to_all x5 -> x1, waiting for transfers between devices: 28.8 us -> 4.41 us  [on_device(): table = lax.all_to_all(spread, 'rows', 0, 0, tiled=True).reshape(B, C)]
    all_to_all x5 -> x1, starting transfers between devices: 35 us -> 11.2 us  [on_device(): table = lax.all_to_all(spread, 'rows', 0, 0, tiled=True).reshape(B, C)]
    pallas_call x0 -> x5, Pallas kernels: none -> 19.9 us  [local(): pl.pallas_call(body, out_shape=out_shapes, in_specs=in_specs, out_specs=o...]
    reduce_sum x7 -> x0, other arithmetic: 8.63 us -> none  [the longest x1 5.74 us: on_device(): jnp.sum(tile_values.astype(jnp.float32) * picked.astype(jnp.float32), axi...]
    broadcast_in_dim x7 -> x0, local copies, waits for them, and re-layouts: 2.98 us -> none  [the longest x3 2.6 us: sent_to_all(): jnp.broadcast_to(value[None], (peers, *value.shape))]
  transfers between devices with their start and end apart: 5 -> 1, of which waited for: 4 -> 1; matrix products, arithmetic and copies ran while one was open for 31% -> 0% of each run, Pallas kernels for 0% -> 8%
where the time goes in v1:
time: 73 us; the launch traced here: 72.2 us
  blocking collectives  33.1 us (45%)
  Pallas kernels  19.9 us (27%)
  starting transfers between devices  11.2 us (15%)
  waiting for transfers between devices  4.41 us (6%)
  local copies, waits for them, and re-layouts  2.91 us (4%)
    all_to_all x1, blocking collectives, on_device(): arrived = lax.all_to_all(payload, 'rows', 0, 0, tiled=True)  23.5 us
    pallas_call x5, Pallas kernels, local(): pl.pallas_call(body, out_shape=out_shapes, in_specs=in_specs, out_specs=o...  19.9 us
    all_to_all x1, starting transfers between devices, on_device(): table = lax.all_to_all(spread, 'rows', 0, 0, tiled=True).reshape(B, C)  11.2 us
    all_to_all x1, blocking collectives, on_device(): parts = lax.all_to_all(partial, 'feat', 0, 0, tiled=True)  9.59 us
    all_to_all x1, waiting for transfers between devices, on_device(): table = lax.all_to_all(spread, 'rows', 0, 0, tiled=True).reshape(B, C)  4.41 us
    unnamed x12, local copies, waits for them, and re-layouts  2.91 us
  transfers between devices with their start and end apart: 1, of which 1 were waited for; matrix products, arithmetic and copies ran while one was open for 0% of the time, Pallas kernels for 8%

profile of v1, /device:TPU:32, one launch (start us, length us, event | category | flops | bytes accessed | tf_op | source)
XLA Modules:
  0.0 72.2 jit_solution(3621019254331290867)
XLA Ops:
  0.6 0.0 copy-start.1
  0.6 0.7 copy-done.1
  1.3 0.7 shard_map.86
  2.1 11.2 %all-to-all-start = ((bf16[32,32,128]{2,1,0:T(8,128)(2,1)}), bf16[32,32,128]{2,1,0:T(8,128)(2,1)S(1)}, u32[]{:S(2)}, u32[]{:S(2)}) async-start(bf16[32,32,128]{2,1,0:T(8,128)(2,1)} %shard_map.86), calls=%async_computation | async-start | bytes 524288 | tf_op jit(solution)/shard_map/all_to_all | solution.py:262
  13.3 0.0 copy-start
  13.3 0.8 %copy-done = s32[256,64]{0,1:T(8,128)S(1)} copy-done((s32[256,64]{0,1:T(8,128)S(1)}, s32[256,64]{0,1:T(8,128)}, u32[]{:S(2)}) %copy-start) | copy-done | bytes 65560
  14.1 0.0 copy-start.2
  14.1 0.7 copy-done.2
  14.8 0.0 copy-start.3
  14.8 0.7 copy-done.3
  15.5 0.0 copy-start.4
  15.5 0.0 copy-start.5
  15.5 5.5 %shard_map.85 = (bf16[2048,8,128]{2,1,0:T(8,128)(2,1)}, s32[64,1,256]{2,1,0:T(1,128)S(1)}, s32[64,1,256]{2,1,0:T(1,128)S(1)}, s32[1,256]{1,0:T(1,128)S(1)}, s32[1]{0:T(128)}) custom-call(s32[256]{0:T(256)S(1)} %bitcast.11, s32[1,256]{1,0:T(1,128)S(1)} %bitcast.12, s32[64,256]{1,0:T(8,128)S(1)} %bitcast.10, s32[1,256]{1,0:T(1,128)S(1)} %bitcast.13, ...), custom_call_target="tpu_custom_call" | custom-call | tf_op jit(solution)/shard_map/pallas_call | solution.py:239
  21.0 4.4 %all-to-all-done = bf16[32,32,128]{2,1,0:T(8,128)(2,1)S(1)} async-done(((bf16[32,32,128]{2,1,0:T(8,128)(2,1)}), bf16[32,32,128]{2,1,0:T(8,128)(2,1)S(1)}, u32[]{:S(2)}, u32[]{:S(2)}) %all-to-all-start) | async-done | bytes 262176 | tf_op jit(solution)/shard_map/all_to_all | solution.py:262
  25.4 6.5 %shard_map.87 = f32[8,1,256]{2,1,0:T(1,128)S(1)} custom-call(s32[1]{0:T(128)} %get-tuple-element.11.total_ref, bf16[1024,128]{1,0:T(8,128)(2,1)S(1)} %bitcast.9, s32[64,1,256]{2,1,0:T(1,128)S(1)} %get-tuple-element.12.ids_ref, s32[64,1,256]{2,1,0:T(1,128)S(1)} %get-tuple-element.13.ex_ref, bf16[2048,8,128]{2,1,0:T(8,128)(2,1)} %get-tuple-element.14.packed_hbm), custom_call_target="tpu_custom_call" | custom-call | tf_op jit(solution)/shard_map/pallas_call | solution.py:239
  31.9 9.6 %all_to_all.15.parts_ref = f32[8,1,256]{2,1,0:T(1,128)S(1)} all-to-all(f32[8,1,256]{2,1,0:T(1,128)S(1)} %shard_map.87), channel_id=1, replica_groups=mesh['rows'=32,'feat'=8] {'feat'}, dimensions={0} | all-to-all | bytes 16384 | tf_op jit(solution)/shard_map/all_to_all | solution.py:291
  41.5 0.0 copy-done.4
  41.5 0.0 copy-done.5
  41.5 6.4 %shard_map.88 = bf16[32,40,128]{2,1,0:T(8,128)(2,1)S(1)} custom-call(s32[1]{0:T(128)} %get-tuple-element.11.total_ref, f32[8,1,256]{2,1,0:T(1,128)S(1)} %all_to_all.15.parts_ref, s32[1,256]{1,0:T(1,128)S(1)} %bitcast.15, s32[1,256]{1,0:T(1,128)S(1)} %bitcast.14, s32[1,256]{1,0:T(1,128)S(1)} %get-tuple-element.15.rank_ref, ...), custom_call_target="tpu_custom_call" | custom-call | tf_op jit(solution)/shard_map/pallas_call | solution.py:239
  47.9 23.5 %all_to_all.16.in_ref = bf16[32,40,128]{2,1,0:T(8,128)(2,1)S(1)} all-to-all(bf16[32,40,128]{2,1,0:T(8,128)(2,1)S(1)} %shard_map.88), channel_id=1, replica_groups=mesh['rows'=32,'feat'=8] {'rows'}, dimensions={0} | all-to-all | bytes 655360 | tf_op jit(solution)/shard_map/all_to_all | solution.py:298
  71.5 0.7 shard_map.89
Async XLA Ops:
  0.6 0.7 copy-start.1
  2.1 23.4 %all-to-all-start = ((bf16[32,32,128]{2,1,0:T(8,128)(2,1)}), bf16[32,32,128]{2,1,0:T(8,128)(2,1)S(1)}, u32[]{:S(2)}, u32[]{:S(2)}) async-start(bf16[32,32,128]{2,1,0:T(8,128)(2,1)} %shard_map.86), calls=%async_computation | async-start | bytes 524288 | tf_op jit(solution)/shard_map/all_to_all | solution.py:262
  13.3 0.8 %copy-start = (s32[256,64]{0,1:T(8,128)S(1)}, s32[256,64]{0,1:T(8,128)}, u32[]{:S(2)}) copy-start(s32[256,64]{0,1:T(8,128)} %param.7) | copy-start | bytes 196612
  14.1 0.7 copy-start.2
  14.8 0.7 copy-start.3
  15.5 26.1 %copy-start.4 = (s32[256]{0:T(256)S(1)}, s32[256]{0:T(256)}, u32[]{:S(2)}) copy-start(s32[256]{0:T(256)} %param.10) | copy-start | bytes 3076
  15.5 26.1 %copy-start.5 = (s32[256]{0:T(256)S(1)}, s32[256]{0:T(256)}, u32[]{:S(2)}) copy-start(s32[256]{0:T(256)} %param.9) | copy-start | bytes 3076

commit v2 on v1

v2 whole, which is shorter than its diff:
```python
import jax
import jax.numpy as jnp
from jax import lax
from jax.experimental import pallas as pl
from jax.experimental.pallas import tpu as pltpu
from jax.sharding import PartitionSpec as P

F32 = jnp.float32
BF16 = jnp.bfloat16
I32 = jnp.int32

E = 256
SLOT = 64
C = 128
B = 1024
R = 32
F = 8
OWN = 8
GR = 8
NG = E * SLOT // GR
CH = 512
GCH = CH // GR
NCH = NG // GCH
KA = 18
KAG = KA * GCH
LEAD = 2 * GCH
XR = 8
WIN = GCH + 8
LOADS = 4

VMEM = pl.BlockSpec(memory_space=pltpu.VMEM)
SMEM = pl.BlockSpec(memory_space=pltpu.SMEM)
ANY = pl.BlockSpec(memory_space=pl.ANY)


def nt(a, b):
    return lax.dot_general(a, b, (((1,), (1,)), ((), ())), preferred_element_type=F32)


def nn(a, b):
    return lax.dot_general(a, b, (((1,), (0,)), ((), ())), preferred_element_type=F32)


def split3(x):
    hi = x.astype(BF16).astype(F32)
    mid = (x - hi).astype(BF16).astype(F32)
    lo = (x - hi - mid).astype(BF16).astype(F32)
    return hi, mid, lo


def iota(shape, dim):
    return lax.broadcasted_iota(I32, shape, dim)


def spread_weights(w_hbm, out_ref, w_ref, sem):
    pltpu.make_async_copy(w_hbm, w_ref, sem).start()
    pltpu.make_async_copy(w_hbm, w_ref, sem).wait()
    out_ref[...] = jnp.broadcast_to(w_ref[...].astype(BF16)[None], out_ref.shape)


def pack_tiles(
    counts_s, counts_hbm, blocks_hbm, owner_hbm, values_hbm, near_ref, far_hbm, ids_ref, ex_ref,
    rank_ref, meta_ref, counts_ref, blocks_ref, owner_ref, values, spill, small_sems, sems, out_sem
):
    part = NG // LOADS
    small = [
        pltpu.make_async_copy(src, dst, small_sems.at[i])
        for i, (src, dst) in enumerate(
            [(counts_hbm, counts_ref), (blocks_hbm, blocks_ref), (owner_hbm, owner_ref)]
        )
    ]
    loads = [
        pltpu.make_async_copy(
            values_hbm.at[pl.ds(i * part, part)], values.at[pl.ds(i * part, part)], sems.at[i]
        )
        for i in range(LOADS)
    ]
    for copy in small + loads:
        copy.start()
    for copy in small:
        copy.wait()

    counts = counts_ref[...]
    granules = lax.shift_right_logical(counts + (GR - 1), 3).astype(F32)
    spread = jnp.broadcast_to(granules, (E, E)).astype(BF16)
    up = iota((E, E), 0)
    across = iota((E, E), 1)
    first = nt((across < up).astype(F32).astype(BF16), spread)
    last = nt((across <= up).astype(F32).astype(BF16), spread)
    first = jnp.concatenate([first] * (CH // E), axis=1)
    last = jnp.concatenate([last] * (CH // E), axis=1)
    before = (up < across).astype(F32).astype(BF16)
    start = nn(spread[0:16], before)
    start_hi = jnp.floor(start * (1.0 / 64.0))
    start_lo = start - 64.0 * start_hi
    row16 = iota((16, E), 0)
    tail = jnp.where(row16 == 0, start_hi, jnp.where(row16 == 1, start_lo, iota((16, E), 1).astype(F32)))
    ids = jnp.where(iota((SLOT, E), 0) < counts, blocks_ref[...], 2047)
    both = jnp.concatenate([lax.shift_right_logical(ids, 5), ids & 31], axis=0).astype(F32)
    table = jnp.concatenate([both, tail], axis=0).astype(BF16)
    lane = iota((1, CH), 1)
    sub = iota((SLOT, CH), 0).astype(F32)
    total = jnp.sum(granules).astype(I32)
    meta_ref[NCH + 1] = total
    meta_ref[0] = 0
    chunks = lax.shift_right_logical(total + (GCH - 1), 6)

    hits = (iota((R, E), 0) == owner_ref[...]).astype(F32)
    earlier = nn(hits.astype(BF16), before)
    rank_ref[...] = jnp.sum(hits * earlier, axis=0, keepdims=True).astype(I32)

    inside = jnp.sum(jnp.where(start[0:1] + 8.0 <= KAG, 1.0, 0.0)).astype(I32)
    reach = jnp.sum(jnp.where(start[0:1] < KAG, 1.0, 0.0)).astype(I32)
    blocks_inside = lax.shift_right_logical(inside, 3)

    def after(e, off):
        off = off + lax.shift_right_logical(counts_s[e] + (GR - 1), 3)
        meta_ref[lax.shift_right_logical(off + (GCH - 1), 6)] = e + 1
        return off

    def put_eight(i, off):
        for j in range(8):
            e = i * 8 + j
            near_ref[pl.ds(off, 8)] = values[pl.ds(e * 8, 8)]
            off = after(e, off)
        return off

    def put_both(e, off):
        tiles = values[pl.ds(e * 8, 8)]
        near_ref[pl.ds(off, 8)] = tiles
        spill[pl.ds(off - KAG + LEAD, 8)] = tiles
        return after(e, off)

    def put_far(e, off):
        spill[pl.ds(off - KAG + LEAD, 8)] = values[pl.ds(e * 8, 8)]
        return after(e, off)

    for copy in loads:
        copy.wait()
    off = lax.fori_loop(0, blocks_inside, put_eight, 0)
    off = lax.fori_loop(blocks_inside * 8, reach, put_both, off)
    lax.fori_loop(reach, E, put_far, off)
    zeros = jnp.zeros((GCH, GR, C), BF16)

    @pl.when(total <= KAG)
    def _():
        near_ref[pl.ds(total, GCH)] = zeros

    @pl.when(total > KAG)
    def _():
        spill[pl.ds(total - KAG + LEAD, GCH)] = zeros

    def send(k):
        return pltpu.make_async_copy(
            spill.at[pl.ds(LEAD + k * GCH, GCH)], far_hbm.at[pl.ds(k * GCH, GCH)], out_sem
        )

    def place(k, carry):
        pos = k * CH + lane
        gran = lax.shift_right_logical(pos, 3).astype(F32)
        hit = (first <= gran) & (gran < last)
        x = nn(table, jnp.where(hit, 1.0, 0.0).astype(BF16))
        slot = pos.astype(F32) - 8.0 * (64.0 * x[128:129] + x[129:130])
        code = 32.0 * x[0:64] + x[64:128]
        here = jnp.sum(jnp.where(sub == slot, code, 0.0), axis=0, keepdims=True).astype(I32)
        live = (pos < total * GR) & (here < B)
        ids_ref[k] = jnp.where(live, here, -1)
        ex_ref[k] = x[130:131].astype(I32)
        return carry

    lax.fori_loop(0, chunks, place, 0)

    def over(k, carry):
        send(k).start()
        send(k).wait()
        return carry

    lax.fori_loop(0, chunks - KA, over, 0)


def doubled(v, ids):
    top = jnp.broadcast_to(jnp.where(ids >= B // 2, 1.0, 0.0), (8, CH)).T
    mask = jnp.broadcast_to(top[:, 0:1], (CH, C)).astype(BF16)
    high = v * mask
    return v - high, high


def window(meta_ref, k):
    return pl.multiple_of(lax.shift_right_logical(meta_ref[k], 3) * 8, 8)


def margins_kernel(
    meta_ref, w_ref, ids_ref, ex_ref, near_ref, far_hbm, out_ref, buf, acc, wide, tiles0, tiles1,
    score0, score1, sem
):
    chunks = lax.shift_right_logical(meta_ref[NCH + 1] + (GCH - 1), 6)
    acc[...] = jnp.zeros_like(acc)
    wide[:, 0:C] = w_ref[0 : B // 2]
    wide[:, C : 2 * C] = w_ref[B // 2 : B]
    rows = iota((WIN, CH), 0)
    sub8 = iota((8, CH), 0)

    def prepare(k, tiles, source):
        low, high = doubled(source.reshape(CH, C), ids_ref[k])
        tiles[:, 0:C] = low
        tiles[:, C : 2 * C] = high

    def multiply(tiles, score):
        score[...] = nt(wide[...], tiles[...])

    def choose(k, score, live):
        ids = ids_ref[k]
        ids8 = jnp.broadcast_to(ids, (8, CH))
        pieces = [score[8 * i : 8 * i + 8, :] for i in range(B // 16)]
        half = B // 4
        while half >= 8:
            bit = (ids8 & half) != 0
            n = len(pieces) // 2
            pieces = [jnp.where(bit, pieces[n + i], pieces[i]) for i in range(n)]
            half //= 2
        pick = jnp.sum(jnp.where(sub8 == (ids8 & 7), pieces[0], 0.0), axis=0, keepdims=True)
        pick = jnp.where((ids >= 0) & live, pick, 0.0)
        base = window(meta_ref, k)
        span = pl.ds(base, WIN)
        acc[span, :] += jnp.where(rows + base == ex_ref[k], pick, 0.0)

    near = jnp.minimum(chunks, KA)
    final = near - 1

    def fetch(k):
        k = jnp.minimum(k, final)
        return k, near_ref[pl.ds(k * GCH, GCH)]

    k0, first = fetch(0)
    prepare(k0, tiles0, first)

    def pair(i, carry):
        k = 2 * i
        k1, v1 = fetch(k + 1)
        choose(jnp.clip(k - 1, 0, final), score1, (k >= 1) & (k <= near))
        multiply(tiles0, score0)
        prepare(k1, tiles1, v1)
        k2, v2 = fetch(k + 2)
        choose(jnp.minimum(k, final), score0, k < near)
        multiply(tiles1, score1)
        prepare(k2, tiles0, v2)
        return carry

    lax.fori_loop(0, lax.shift_right_logical(near + 2, 1), pair, 0)

    def outer(k, carry):
        copy = pltpu.make_async_copy(far_hbm.at[pl.ds((k - KA) * GCH, GCH)], buf, sem)
        copy.start()
        copy.wait()
        prepare(k, tiles0, buf[...])
        multiply(tiles0, score0)
        choose(k, score0, k < chunks)
        return carry

    lax.fori_loop(KA, chunks, outer, 0)
    row = jnp.sum(acc[0:E, :].T, axis=0, keepdims=True)
    out_ref[...] = jnp.broadcast_to(row[None], out_ref.shape)


def gradient_kernel(
    meta_ref, parts_ref, labels_hbm, owner_hbm, rank_ref, ids_ref, ex_ref, near_ref, far_hbm, out_ref,
    labels_ref, owner_ref, buf, acc, column_ref, tiles0, tiles1, hot0, hot1, small_sems, sem
):
    chunks = lax.shift_right_logical(meta_ref[NCH + 1] + (GCH - 1), 6)
    small = [
        pltpu.make_async_copy(labels_hbm, labels_ref, small_sems.at[0]),
        pltpu.make_async_copy(owner_hbm, owner_ref, small_sems.at[1]),
    ]
    for copy in small:
        copy.start()
    acc[...] = jnp.zeros_like(acc)
    margin = jnp.sum(parts_ref[...].reshape(F, E), axis=0, keepdims=True)
    small_exp = jnp.exp(-jnp.abs(margin))
    for copy in small:
        copy.wait()
    label = labels_ref[...].astype(F32)
    resid = jax.nn.sigmoid(margin) - label
    loss = jnp.sum(jnp.maximum(margin, 0.0) + jnp.log1p(small_exp) - label * margin)
    half = resid.astype(BF16).astype(F32)
    column_ref[0:E, :] = jnp.broadcast_to(half, (C, E)).T
    column_ref[E : E + WIN, :] = jnp.zeros((WIN, C), F32)
    rows = iota((WIN, CH), 0)
    lo_rows = iota((32, CH), 0)

    def prepare(k, tiles, hot, source, live):
        ids = ids_ref[k]
        base = window(meta_ref, k)
        column = column_ref[pl.ds(base, WIN), :]
        column = jnp.concatenate([column] * (CH // C), axis=1)
        coef = jnp.sum(jnp.where(rows + base == ex_ref[k], column, 0.0), axis=0, keepdims=True)
        coef = jnp.where((ids >= 0) & live, coef, 0.0)
        low = jnp.where(lo_rows == (ids & 31), coef, 0.0).astype(BF16)
        high = jnp.broadcast_to(lax.shift_right_arithmetic(ids, 5) & 15, (8, CH))
        for h in range(16):
            one = jnp.where(high == h, 1.0, 0.0)
            mask = jnp.concatenate([one, one, one, one], axis=0).astype(BF16)
            hot[32 * h : 32 * h + 32, :] = low * mask
        lower, upper = doubled(source.reshape(CH, C), ids)
        tiles[:, 0:C] = lower
        tiles[:, C : 2 * C] = upper

    def multiply(tiles, hot):
        acc[...] += nn(hot[...], tiles[...])

    near = jnp.minimum(chunks, KA)
    final = near - 1

    def fetch(k):
        live = k < near
        k = jnp.minimum(k, final)
        return k, near_ref[pl.ds(k * GCH, GCH)], live

    k0, v0, live0 = fetch(0)
    prepare(k0, tiles0, hot0, v0, live0)

    def pair(i, carry):
        k1, v1, live1 = fetch(2 * i + 1)
        multiply(tiles0, hot0)
        prepare(k1, tiles1, hot1, v1, live1)
        k2, v2, live2 = fetch(2 * i + 2)
        multiply(tiles1, hot1)
        prepare(k2, tiles0, hot0, v2, live2)
        return carry

    lax.fori_loop(0, lax.shift_right_logical(near + 1, 1), pair, 0)

    def outer(k, carry):
        copy = pltpu.make_async_copy(far_hbm.at[pl.ds((k - KA) * GCH, GCH)], buf, sem)
        copy.start()
        copy.wait()
        prepare(k, tiles0, hot0, buf[...], k < chunks)
        multiply(tiles0, hot0)
        return carry

    lax.fori_loop(KA, chunks, outer, 0)
    for i in range(2):
        out_ref[16 * i : 16 * i + 16, 0:32, :] = (
            acc[:, C * i : C * i + C].reshape(R // 2, 32, C).astype(BF16)
        )

    owner_hit = iota((R, E), 0) == owner_ref[...]
    rank = rank_ref[...]
    lane_row = iota((C, E), 0)
    extra = jnp.zeros((R, C), F32)
    for i, piece in enumerate(split3(margin)):
        a = jnp.where(owner_hit, piece, 0.0).astype(BF16)
        b = jnp.where(lane_row == rank + OWN * i, 1.0, 0.0).astype(BF16)
        extra = extra + nt(a, b)
    lane = iota((R, C), 1)
    for i, piece in enumerate(split3(jnp.full((R, C), loss, F32))):
        extra = jnp.where(lane == 3 * OWN + i, piece, extra)
    out_ref[:, 32 : 32 + XR, :] = jnp.broadcast_to(extra[:, None, :], (R, XR, C)).astype(BF16)


def finish_kernel(in_ref, grad_ref, owned_ref, loss_ref):
    total = in_ref[0, 0:32, :].astype(F32)
    for r in range(1, R):
        total = total + in_ref[r, 0:32, :].astype(F32)
    grad_ref[...] = total
    extra = in_ref[:, 32 : 32 + XR, :].astype(F32)[:, 0, :]
    src = iota((C, E), 0)
    pick = jnp.where((src < 3 * OWN) & ((src & 7) == (iota((C, E), 1) & 7)), 1.0, 0.0)
    wide = nn(extra.astype(BF16), pick.astype(BF16))
    own = lax.shift_right_logical(iota((R, E), 1), 3) == iota((R, E), 0)
    owned_ref[...] = jnp.sum(jnp.where(own, wide, 0.0), axis=0, keepdims=True)
    lane = iota((R, C), 1)
    keep = (lane >= 3 * OWN) & (lane < 3 * OWN + 3)
    total_loss = jnp.sum(jnp.where(keep, extra, 0.0), keepdims=True)
    loss_ref[...] = total_loss * (1.0 / (E * R))


def local(body, out_shapes, in_specs, out_specs, scratch, limit, *args):
    return pl.pallas_call(
        body,
        out_shape=out_shapes,
        in_specs=in_specs,
        out_specs=out_specs,
        scratch_shapes=scratch,
        compiler_params=pltpu.CompilerParams(vmem_limit_bytes=limit << 20),
    )(*args)


def near(x):
    return pltpu.with_memory_space_constraint(x, pltpu.VMEM)


def far(x):
    return pltpu.with_memory_space_constraint(x, pltpu.HBM)


def on_device(tile_values, tile_blocks, tile_counts, labels, owner_rank, weights):
    shape = jax.ShapeDtypeStruct
    dma = pltpu.SemaphoreType.DMA
    spread = local(
        spread_weights, pltpu.VMEM((R, B // R, C), BF16), [ANY], VMEM,
        [pltpu.VMEM((B // R, C), F32), dma(())], 4, far(weights),
    )
    table = lax.all_to_all(spread, "rows", 0, 0, tiled=True).reshape(B, C)
    owner_row = far(owner_rank.reshape(1, E))
    label_row = far(labels.reshape(1, E))
    packed, over, ids, ex, rank, meta = local(
        pack_tiles,
        (
            pltpu.VMEM((KAG + GCH, GR, C), BF16),
            pltpu.HBM((NG - KAG, GR, C), BF16),
            pltpu.VMEM((NCH, 1, CH), I32),
            pltpu.VMEM((NCH, 1, CH), I32),
            pltpu.VMEM((1, E), I32),
            shape((NCH + 2,), I32),
        ),
        [SMEM, ANY, ANY, ANY, ANY],
        (VMEM, ANY, VMEM, VMEM, VMEM, SMEM),
        [
            pltpu.VMEM((1, E), I32),
            pltpu.VMEM((SLOT, E), I32),
            pltpu.VMEM((1, E), I32),
            pltpu.VMEM((NG, GR, C), BF16),
            pltpu.VMEM((NG - KAG + LEAD + GCH, GR, C), BF16),
            dma((3,)),
            dma((LOADS,)),
            dma(()),
        ],
        16,
        tile_counts.reshape(E), far(tile_counts.T), far(tile_blocks.T), owner_row,
        far(tile_values.reshape(NG, GR, C)),
    )
    partial = local(
        margins_kernel, pltpu.VMEM((F, 1, E), F32), [SMEM, VMEM, VMEM, VMEM, VMEM, ANY], VMEM,
        [
            pltpu.VMEM((GCH, GR, C), BF16),
            pltpu.VMEM((E + WIN, CH), F32),
            pltpu.VMEM((B // 2, 2 * C), BF16),
            pltpu.VMEM((CH, 2 * C), BF16),
            pltpu.VMEM((CH, 2 * C), BF16),
            pltpu.VMEM((B // 2, CH), F32),
            pltpu.VMEM((B // 2, CH), F32),
            dma(()),
        ],
        16,
        meta, near(table), near(ids), near(ex), near(packed), far(over),
    )
    parts = lax.all_to_all(partial, "feat", 0, 0, tiled=True)
    payload = local(
        gradient_kernel, pltpu.VMEM((R, B // R + XR, C), BF16),
        [SMEM, VMEM, ANY, ANY, VMEM, VMEM, VMEM, VMEM, ANY], VMEM,
        [
            pltpu.VMEM((1, E), I32),
            pltpu.VMEM((1, E), I32),
            pltpu.VMEM((GCH, GR, C), BF16),
            pltpu.VMEM((B // 2, 2 * C), F32),
            pltpu.VMEM((E + WIN, C), F32),
            pltpu.VMEM((CH, 2 * C), BF16),
            pltpu.VMEM((CH, 2 * C), BF16),
            pltpu.VMEM((B // 2, CH), BF16),
            pltpu.VMEM((B // 2, CH), BF16),
            dma((2,)),
            dma(()),
        ],
        16,
        meta, near(parts), label_row, owner_row, near(rank), near(ids), near(ex), near(packed),
        far(over),
    )
    arrived = lax.all_to_all(payload, "rows", 0, 0, tiled=True)
    gradient, owned, loss = local(
        finish_kernel,
        (shape((B // R, C), F32), shape((1, E), F32), shape((1, 1), F32)),
        [VMEM], (VMEM, VMEM, VMEM), (), 8, near(arrived),
    )
    return owned.reshape(E), gradient, loss.reshape(())


def solution(mesh):
    in_specs = (
        P("rows", "feat", None),
        P("rows", "feat"),
        P("rows", "feat"),
        P("rows"),
        P("rows"),
        P(("feat", "rows"), None),
    )
    out_specs = (P("rows"), P(("feat", "rows"), None), P())
    return jax.shard_map(
        on_device, mesh=mesh, in_specs=in_specs, out_specs=out_specs, check_vma=False
    )
```

time: 73 us -> 63.5 us (0.87)
  Pallas kernels: 19.9 us -> 15.8 us
  blocking collectives: 33.1 us -> 29.4 us
  local copies, waits for them, and re-layouts: 2.91 us -> 0 us
  waiting for transfers between devices: 4.41 us -> 6.02 us
    pallas_call x5, Pallas kernels: 19.9 us -> 15.8 us  [local(): pl.pallas_call(body, out_shape=out_shapes, in_specs=in_specs, out_specs=o...]
    all_to_all x1, blocking collectives: 23.5 us -> 19.9 us  [on_device(): arrived = lax.all_to_all(payload, 'rows', 0, 0, tiled=True)]
    unnamed x12 -> x0, local copies, waits for them, and re-layouts: 2.91 us -> none
    all_to_all x1, waiting for transfers between devices: 4.41 us -> 6.02 us  [on_device(): table = lax.all_to_all(spread, 'rows', 0, 0, tiled=True).reshape(B, C)]
  transfers between devices with their start and end apart: 1 -> 1, of which waited for: 1 -> 1; matrix products, arithmetic and copies ran while one was open for 0% -> 0% of each run, Pallas kernels for 8% -> 10%
where the time goes in v2:
time: 63.5 us; the launch traced here: 63.1 us
  blocking collectives  29.4 us (46%)
  Pallas kernels  15.8 us (25%)
  starting transfers between devices  11.2 us (18%)
  waiting for transfers between devices  6.02 us (9%)
  between operations  0.67 us (1%)
    all_to_all x1, blocking collectives, on_device(): arrived = lax.all_to_all(payload, 'rows', 0, 0, tiled=True)  19.9 us
    pallas_call x5, Pallas kernels, local(): pl.pallas_call(body, out_shape=out_shapes, in_specs=in_specs, out_specs=o...  15.8 us
    all_to_all x1, starting transfers between devices, on_device(): table = lax.all_to_all(spread, 'rows', 0, 0, tiled=True).reshape(B, C)  11.2 us
    all_to_all x1, blocking collectives, on_device(): parts = lax.all_to_all(partial, 'feat', 0, 0, tiled=True)  9.58 us
    all_to_all x1, waiting for transfers between devices, on_device(): table = lax.all_to_all(spread, 'rows', 0, 0, tiled=True).reshape(B, C)  6.02 us
  transfers between devices with their start and end apart: 1, of which 1 were waited for; matrix products, arithmetic and copies ran while one was open for 0% of the time, Pallas kernels for 10%

profile of v2, /device:TPU:32, one launch (start us, length us, event | category | flops | bytes accessed | tf_op | source)
XLA Modules:
  0.0 63.1 jit_solution(4818024510559903181)
XLA Ops:
  0.6 1.4 %shard_map.86 = bf16[32,32,128]{2,1,0:T(8,128)(2,1)} custom-call(f32[32,128]{1,0:T(8,128)} %w_hbm.1), custom_call_target="tpu_custom_call" | custom-call | tf_op jit(solution)/shard_map/pallas_call | solution.py:378
  2.1 11.2 %all-to-all-start = ((bf16[32,32,128]{2,1,0:T(8,128)(2,1)}), bf16[32,32,128]{2,1,0:T(8,128)(2,1)S(1)}, u32[]{:S(2)}, u32[]{:S(2)}) async-start(bf16[32,32,128]{2,1,0:T(8,128)(2,1)} %shard_map.86), calls=%async_computation | async-start | bytes 524288 | tf_op jit(solution)/shard_map/all_to_all | solution.py:403
  13.3 6.1 %shard_map.85 = (bf16[1216,8,128]{2,1,0:T(8,128)(2,1)S(1)}, bf16[896,8,128]{2,1,0:T(8,128)(2,1)}, s32[32,1,512]{2,1,0:T(1,128)S(1)}, s32[32,1,512]{2,1,0:T(1,128...) custom-call(s32[256]{0:T(256)} %bitcast.12, s32[1,256]{1,0:T(1,128)} %bitcast.13, s32[64,256]{1,0:T(8,128)} %bitcast.11, ...), custom_call_target="tpu_custom_call" | custom-call | tf_op jit(solution)/shard_map/pallas_call | solution.py:378
  19.4 6.0 %all-to-all-done = bf16[32,32,128]{2,1,0:T(8,128)(2,1)S(1)} async-done(((bf16[32,32,128]{2,1,0:T(8,128)(2,1)}), bf16[32,32,128]{2,1,0:T(8,128)(2,1)S(1)}, u32[]{:S(2)}, u32[]{:S(2)}) %all-to-all-start) | async-done | bytes 262176 | tf_op jit(solution)/shard_map/all_to_all | solution.py:403
  25.5 3.6 %shard_map.87 = f32[8,1,256]{2,1,0:T(1,128)S(1)} custom-call(s32[34]{0:T(128)S(1)} %get-tuple-element.12.meta_ref, bf16[1024,128]{1,0:T(8,128)(2,1)S(1)} %bitcast.9, s32[32,1,512]{2,1,0:T(1,128)S(1)} %get-tuple-element.13.ids_ref, s32[32,1,512]{2,1,0:T(1,128)S(1)} %get-tuple-element.14.ex_ref, bf16[1216,8,128]{2,1,0:T(8,128)(2,1)S(1)} %get-tuple-element.15.near_ref, ...), custom_call_target="tpu_custom_call" | custom-call | tf_op jit(solution)/shard_map/pallas_call | solution.py:378
  29.1 9.6 %all_to_all.15.parts_ref = f32[8,1,256]{2,1,0:T(1,128)S(1)} all-to-all(f32[8,1,256]{2,1,0:T(1,128)S(1)} %shard_map.87), channel_id=1, replica_groups=mesh['rows'=32,'feat'=8] {'feat'}, dimensions={0} | all-to-all | bytes 16384 | tf_op jit(solution)/shard_map/all_to_all | solution.py:447
  38.6 3.9 %shard_map.88 = bf16[32,40,128]{2,1,0:T(8,128)(2,1)S(1)} custom-call(s32[34]{0:T(128)S(1)} %get-tuple-element.12.meta_ref, f32[8,1,256]{2,1,0:T(1,128)S(1)} %all_to_all.15.parts_ref, s32[1,256]{1,0:T(1,128)} %bitcast.16, s32[1,256]{1,0:T(1,128)} %bitcast.15, s32[1,256]{1,0:T(1,128)S(1)} %get-tuple-element.17.rank_ref, ...), custom_call_target="tpu_custom_call" | custom-call | tf_op jit(solution)/shard_map/pallas_call | solution.py:378
  42.6 19.9 %all_to_all.16.in_ref = bf16[32,40,128]{2,1,0:T(8,128)(2,1)S(1)} all-to-all(bf16[32,40,128]{2,1,0:T(8,128)(2,1)S(1)} %shard_map.88), channel_id=1, replica_groups=mesh['rows'=32,'feat'=8] {'rows'}, dimensions={0} | all-to-all | bytes 655360 | tf_op jit(solution)/shard_map/all_to_all | solution.py:468
  62.4 0.7 %shard_map.89 = (f32[32,128]{1,0:T(8,128)}, f32[1,256]{1,0:T(1,128)}, f32[1,1]{1,0:T(1,128)}) custom-call(bf16[32,40,128]{2,1,0:T(8,128)(2,1)S(1)} %all_to_all.16.in_ref), custom_call_target="tpu_custom_call" | custom-call | tf_op jit(solution)/shard_map/pallas_call | solution.py:378
Async XLA Ops:
  2.1 23.4 %all-to-all-start = ((bf16[32,32,128]{2,1,0:T(8,128)(2,1)}), bf16[32,32,128]{2,1,0:T(8,128)(2,1)S(1)}, u32[]{:S(2)}, u32[]{:S(2)}) async-start(bf16[32,32,128]{2,1,0:T(8,128)(2,1)} %shard_map.86), calls=%async_computation | async-start | bytes 524288 | tf_op jit(solution)/shard_map/all_to_all | solution.py:403

commit v3 on v2

--- a/solution.py
+++ b/solution.py
@@ -26,10 +26,10 @@
 LEAD = 2 * GCH
 XR = 8
 WIN = GCH + 8
+FUSED = 4
 LOADS = 4
 
 VMEM = pl.BlockSpec(memory_space=pltpu.VMEM)
-SMEM = pl.BlockSpec(memory_space=pltpu.SMEM)
 ANY = pl.BlockSpec(memory_space=pl.ANY)
 
 
@@ -59,14 +59,19 @@
 
 
 def pack_tiles(
-    counts_s, counts_hbm, blocks_hbm, owner_hbm, values_hbm, near_ref, far_hbm, ids_ref, ex_ref,
-    rank_ref, meta_ref, counts_ref, blocks_ref, owner_ref, values, spill, small_sems, sems, out_sem
+    flat_hbm, counts_hbm, blocks_hbm, owner_hbm, values_hbm, near_ref, far_hbm, ids_ref, ex_ref,
+    info_ref, counts_s, counts_ref, blocks_ref, owner_ref, values, spill, small_sems, sems, out_sem
 ):
     part = NG // LOADS
     small = [
         pltpu.make_async_copy(src, dst, small_sems.at[i])
         for i, (src, dst) in enumerate(
-            [(counts_hbm, counts_ref), (blocks_hbm, blocks_ref), (owner_hbm, owner_ref)]
+            [
+                (counts_hbm, counts_ref),
+                (blocks_hbm, blocks_ref),
+                (owner_hbm, owner_ref),
+                (flat_hbm, counts_s),
+            ]
         )
     ]
     loads = [
@@ -86,9 +91,7 @@
     up = iota((E, E), 0)
     across = iota((E, E), 1)
     first = nt((across < up).astype(F32).astype(BF16), spread)
-    last = nt((across <= up).astype(F32).astype(BF16), spread)
     first = jnp.concatenate([first] * (CH // E), axis=1)
-    last = jnp.concatenate([last] * (CH // E), axis=1)
     before = (up < across).astype(F32).astype(BF16)
     start = nn(spread[0:16], before)
     start_hi = jnp.floor(start * (1.0 / 64.0))
@@ -97,69 +100,23 @@
     tail = jnp.where(row16 == 0, start_hi, jnp.where(row16 == 1, start_lo, iota((16, E), 1).astype(F32)))
     ids = jnp.where(iota((SLOT, E), 0) < counts, blocks_ref[...], 2047)
     both = jnp.concatenate([lax.shift_right_logical(ids, 5), ids & 31], axis=0).astype(F32)
-    table = jnp.concatenate([both, tail], axis=0).astype(BF16)
+    table = jnp.concatenate([both, tail], axis=0)
+    shifted = jnp.where(iota(table.shape, 1) == 0, 0.0, pltpu.roll(table, 1, 1))
+    table = (table - shifted).astype(BF16)
     lane = iota((1, CH), 1)
     sub = iota((SLOT, CH), 0).astype(F32)
     total = jnp.sum(granules).astype(I32)
-    meta_ref[NCH + 1] = total
-    meta_ref[0] = 0
     chunks = lax.shift_right_logical(total + (GCH - 1), 6)
 
     hits = (iota((R, E), 0) == owner_ref[...]).astype(F32)
     earlier = nn(hits.astype(BF16), before)
-    rank_ref[...] = jnp.sum(hits * earlier, axis=0, keepdims=True).astype(I32)
-
-    inside = jnp.sum(jnp.where(start[0:1] + 8.0 <= KAG, 1.0, 0.0)).astype(I32)
-    reach = jnp.sum(jnp.where(start[0:1] < KAG, 1.0, 0.0)).astype(I32)
-    blocks_inside = lax.shift_right_logical(inside, 3)
-
-    def after(e, off):
-        off = off + lax.shift_right_logical(counts_s[e] + (GR - 1), 3)
-        meta_ref[lax.shift_right_logical(off + (GCH - 1), 6)] = e + 1
-        return off
-
-    def put_eight(i, off):
-        for j in range(8):
-            e = i * 8 + j
-            near_ref[pl.ds(off, 8)] = values[pl.ds(e * 8, 8)]
-            off = after(e, off)
-        return off
-
-    def put_both(e, off):
-        tiles = values[pl.ds(e * 8, 8)]
-        near_ref[pl.ds(off, 8)] = tiles
-        spill[pl.ds(off - KAG + LEAD, 8)] = tiles
-        return after(e, off)
-
-    def put_far(e, off):
-        spill[pl.ds(off - KAG + LEAD, 8)] = values[pl.ds(e * 8, 8)]
-        return after(e, off)
-
-    for copy in loads:
-        copy.wait()
-    off = lax.fori_loop(0, blocks_inside, put_eight, 0)
-    off = lax.fori_loop(blocks_inside * 8, reach, put_both, off)
-    lax.fori_loop(reach, E, put_far, off)
-    zeros = jnp.zeros((GCH, GR, C), BF16)
-
-    @pl.when(total <= KAG)
-    def _():
-        near_ref[pl.ds(total, GCH)] = zeros
-
-    @pl.when(total > KAG)
-    def _():
-        spill[pl.ds(total - KAG + LEAD, GCH)] = zeros
-
-    def send(k):
-        return pltpu.make_async_copy(
-            spill.at[pl.ds(LEAD + k * GCH, GCH)], far_hbm.at[pl.ds(k * GCH, GCH)], out_sem
-        )
+    info_ref[0:1, :] = jnp.sum(hits * earlier, axis=0, keepdims=True).astype(I32)
+    info_ref[1:2, :] = jnp.full((1, E), total, I32)
 
     def place(k, carry):
         pos = k * CH + lane
         gran = lax.shift_right_logical(pos, 3).astype(F32)
-        hit = (first <= gran) & (gran < last)
-        x = nn(table, jnp.where(hit, 1.0, 0.0).astype(BF16))
+        x = nn(table, jnp.where(first <= gran, 1.0, 0.0).astype(BF16))
         slot = pos.astype(F32) - 8.0 * (64.0 * x[128:129] + x[129:130])
         code = 32.0 * x[0:64] + x[64:128]
         here = jnp.sum(jnp.where(sub == slot, code, 0.0), axis=0, keepdims=True).astype(I32)
@@ -168,7 +125,67 @@
         ex_ref[k] = x[130:131].astype(I32)
         return carry
 
-    lax.fori_loop(0, chunks, place, 0)
+
+    inside = jnp.sum(jnp.where(start[0:1] + 8.0 <= KAG, 1.0, 0.0)).astype(I32)
+    reach = jnp.sum(jnp.where(start[0:1] < KAG, 1.0, 0.0)).astype(I32)
+    blocks_inside = lax.shift_right_logical(inside, 3)
+
+    def after(e, off):
+        return off + lax.shift_right_logical(counts_s[e] + (GR - 1), 3)
+
+    def put_eight(i, off):
+        for j in range(8):
+            e = i * 8 + j
+            near_ref[pl.ds(off, 8)] = values[pl.ds(e * 8, 8)]
+            off = after(e, off)
+        return off
+
+    def put_both(e, off):
+        tiles = values[pl.ds(e * 8, 8)]
+        near_ref[pl.ds(off, 8)] = tiles
+        spill[pl.ds(off - KAG + LEAD, 8)] = tiles
+        return after(e, off)
+
+    def put_far(e, off):
+        spill[pl.ds(off - KAG + LEAD, 8)] = values[pl.ds(e * 8, 8)]
+        return after(e, off)
+
+    for copy in loads:
+        copy.wait()
+
+    def place_and_put(i, off):
+        place(2 * i, 0)
+        place(2 * i + 1, 0)
+        for j in range(FUSED):
+            off = put_eight(FUSED * i + j, off)
+        return off
+
+    @pl.when(inside == E)
+    def _():
+        lax.fori_loop(0, E // (8 * FUSED), place_and_put, 0)
+        lax.fori_loop(2 * E // (8 * FUSED), chunks, place, 0)
+
+    @pl.when(inside < E)
+    def _():
+        lax.fori_loop(0, chunks, place, 0)
+        off = lax.fori_loop(0, blocks_inside, put_eight, 0)
+        off = lax.fori_loop(blocks_inside * 8, reach, put_both, off)
+        lax.fori_loop(reach, E, put_far, off)
+
+    zeros = jnp.zeros((GCH, GR, C), BF16)
+
+    @pl.when(total <= KAG)
+    def _():
+        near_ref[pl.ds(total, GCH)] = zeros
+
+    @pl.when(total > KAG)
+    def _():
+        spill[pl.ds(total - KAG + LEAD, GCH)] = zeros
+
+    def send(k):
+        return pltpu.make_async_copy(
+            spill.at[pl.ds(LEAD + k * GCH, GCH)], far_hbm.at[pl.ds(k * GCH, GCH)], out_sem
+        )
 
     def over(k, carry):
         send(k).start()
@@ -185,15 +202,18 @@
     return v - high, high
 
 
-def window(meta_ref, k):
-    return pl.multiple_of(lax.shift_right_logical(meta_ref[k], 3) * 8, 8)
+def scalar(row):
+    return jnp.min(row[:, 0:128].astype(F32)).astype(I32)
+
+
+def window(ex_ref, k):
+    return pl.multiple_of(lax.shift_right_logical(scalar(ex_ref[k]), 3) * 8, 8)
 
 
 def margins_kernel(
-    meta_ref, w_ref, ids_ref, ex_ref, near_ref, far_hbm, out_ref, buf, acc, wide, tiles0, tiles1,
-    score0, score1, sem
+    info_ref, w_ref, ids_ref, ex_ref, near_ref, far_hbm, out_ref, buf, acc, wide, tiles0, tiles1, sem
 ):
-    chunks = lax.shift_right_logical(meta_ref[NCH + 1] + (GCH - 1), 6)
+    chunks = lax.shift_right_logical(scalar(info_ref[1:2, :]) + (GCH - 1), 6)
     acc[...] = jnp.zeros_like(acc)
     wide[:, 0:C] = w_ref[0 : B // 2]
     wide[:, C : 2 * C] = w_ref[B // 2 : B]
@@ -205,22 +225,21 @@
         tiles[:, 0:C] = low
         tiles[:, C : 2 * C] = high
 
-    def multiply(tiles, score):
-        score[...] = nt(wide[...], tiles[...])
+    def multiply(tiles):
+        return nt(wide[...], tiles[...])
 
     def choose(k, score, live):
         ids = ids_ref[k]
         ids8 = jnp.broadcast_to(ids, (8, CH))
         pieces = [score[8 * i : 8 * i + 8, :] for i in range(B // 16)]
-        half = B // 4
-        while half >= 8:
+        half = 8
+        while len(pieces) > 1:
             bit = (ids8 & half) != 0
-            n = len(pieces) // 2
-            pieces = [jnp.where(bit, pieces[n + i], pieces[i]) for i in range(n)]
-            half //= 2
+            pieces = [jnp.where(bit, b, a) for a, b in zip(pieces[0::2], pieces[1::2])]
+            half *= 2
         pick = jnp.sum(jnp.where(sub8 == (ids8 & 7), pieces[0], 0.0), axis=0, keepdims=True)
         pick = jnp.where((ids >= 0) & live, pick, 0.0)
-        base = window(meta_ref, k)
+        base = window(ex_ref, k)
         span = pl.ds(base, WIN)
         acc[span, :] += jnp.where(rows + base == ex_ref[k], pick, 0.0)
 
@@ -237,24 +256,21 @@
     def pair(i, carry):
         k = 2 * i
         k1, v1 = fetch(k + 1)
-        choose(jnp.clip(k - 1, 0, final), score1, (k >= 1) & (k <= near))
-        multiply(tiles0, score0)
+        choose(k, multiply(tiles0), k < near)
         prepare(k1, tiles1, v1)
         k2, v2 = fetch(k + 2)
-        choose(jnp.minimum(k, final), score0, k < near)
-        multiply(tiles1, score1)
+        choose(k1, multiply(tiles1), k + 1 < near)
         prepare(k2, tiles0, v2)
         return carry
 
-    lax.fori_loop(0, lax.shift_right_logical(near + 2, 1), pair, 0)
+    lax.fori_loop(0, lax.shift_right_logical(near + 1, 1), pair, 0)
 
     def outer(k, carry):
         copy = pltpu.make_async_copy(far_hbm.at[pl.ds((k - KA) * GCH, GCH)], buf, sem)
         copy.start()
         copy.wait()
         prepare(k, tiles0, buf[...])
-        multiply(tiles0, score0)
-        choose(k, score0, k < chunks)
+        choose(k, multiply(tiles0), k < chunks)
         return carry
 
     lax.fori_loop(KA, chunks, outer, 0)
@@ -263,10 +279,10 @@
 
 
 def gradient_kernel(
-    meta_ref, parts_ref, labels_hbm, owner_hbm, rank_ref, ids_ref, ex_ref, near_ref, far_hbm, out_ref,
+    info_ref, parts_ref, labels_hbm, owner_hbm, ids_ref, ex_ref, near_ref, far_hbm, out_ref,
     labels_ref, owner_ref, buf, acc, column_ref, tiles0, tiles1, hot0, hot1, small_sems, sem
 ):
-    chunks = lax.shift_right_logical(meta_ref[NCH + 1] + (GCH - 1), 6)
+    chunks = lax.shift_right_logical(scalar(info_ref[1:2, :]) + (GCH - 1), 6)
     small = [
         pltpu.make_async_copy(labels_hbm, labels_ref, small_sems.at[0]),
         pltpu.make_async_copy(owner_hbm, owner_ref, small_sems.at[1]),
@@ -289,7 +305,7 @@
 
     def prepare(k, tiles, hot, source, live):
         ids = ids_ref[k]
-        base = window(meta_ref, k)
+        base = window(ex_ref, k)
         column = column_ref[pl.ds(base, WIN), :]
         column = jnp.concatenate([column] * (CH // C), axis=1)
         coef = jnp.sum(jnp.where(rows + base == ex_ref[k], column, 0.0), axis=0, keepdims=True)
@@ -344,7 +360,7 @@
         )
 
     owner_hit = iota((R, E), 0) == owner_ref[...]
-    rank = rank_ref[...]
+    rank = info_ref[0:1, :]
     lane_row = iota((C, E), 0)
     extra = jnp.zeros((R, C), F32)
     for i, piece in enumerate(split3(margin)):
@@ -403,51 +419,49 @@
     table = lax.all_to_all(spread, "rows", 0, 0, tiled=True).reshape(B, C)
     owner_row = far(owner_rank.reshape(1, E))
     label_row = far(labels.reshape(1, E))
-    packed, over, ids, ex, rank, meta = local(
+    packed, over, ids, ex, info = local(
         pack_tiles,
         (
             pltpu.VMEM((KAG + GCH, GR, C), BF16),
             pltpu.HBM((NG - KAG, GR, C), BF16),
             pltpu.VMEM((NCH, 1, CH), I32),
             pltpu.VMEM((NCH, 1, CH), I32),
-            pltpu.VMEM((1, E), I32),
-            shape((NCH + 2,), I32),
+            pltpu.VMEM((2, E), I32),
         ),
-        [SMEM, ANY, ANY, ANY, ANY],
-        (VMEM, ANY, VMEM, VMEM, VMEM, SMEM),
+        [ANY, ANY, ANY, ANY, ANY],
+        (VMEM, ANY, VMEM, VMEM, VMEM),
         [
+            pltpu.SMEM((E,), I32),
             pltpu.VMEM((1, E), I32),
             pltpu.VMEM((SLOT, E), I32),
             pltpu.VMEM((1, E), I32),
             pltpu.VMEM((NG, GR, C), BF16),
             pltpu.VMEM((NG - KAG + LEAD + GCH, GR, C), BF16),
-            dma((3,)),
+            dma((4,)),
             dma((LOADS,)),
             dma(()),
         ],
         16,
-        tile_counts.reshape(E), far(tile_counts.T), far(tile_blocks.T), owner_row,
+        far(tile_counts.reshape(E)), far(tile_counts.T), far(tile_blocks.T), owner_row,
         far(tile_values.reshape(NG, GR, C)),
     )
     partial = local(
-        margins_kernel, pltpu.VMEM((F, 1, E), F32), [SMEM, VMEM, VMEM, VMEM, VMEM, ANY], VMEM,
+        margins_kernel, pltpu.VMEM((F, 1, E), F32), [VMEM, VMEM, VMEM, VMEM, VMEM, ANY], VMEM,
         [
             pltpu.VMEM((GCH, GR, C), BF16),
             pltpu.VMEM((E + WIN, CH), F32),
             pltpu.VMEM((B // 2, 2 * C), BF16),
             pltpu.VMEM((CH, 2 * C), BF16),
             pltpu.VMEM((CH, 2 * C), BF16),
-            pltpu.VMEM((B // 2, CH), F32),
-            pltpu.VMEM((B // 2, CH), F32),
             dma(()),
         ],
         16,
-        meta, near(table), near(ids), near(ex), near(packed), far(over),
+        near(info), near(table), near(ids), near(ex), near(packed), far(over),
     )
     parts = lax.all_to_all(partial, "feat", 0, 0, tiled=True)
     payload = local(
         gradient_kernel, pltpu.VMEM((R, B // R + XR, C), BF16),
-        [SMEM, VMEM, ANY, ANY, VMEM, VMEM, VMEM, VMEM, ANY], VMEM,
+        [VMEM, VMEM, ANY, ANY, VMEM, VMEM, VMEM, ANY], VMEM,
         [
             pltpu.VMEM((1, E), I32),
             pltpu.VMEM((1, E), I32),
@@ -462,7 +476,7 @@
             dma(()),
         ],
         16,
-        meta, near(parts), label_row, owner_row, near(rank), near(ids), near(ex), near(packed),
+        near(info), near(parts), label_row, owner_row, near(ids), near(ex), near(packed),
         far(over),
     )
     arrived = lax.all_to_all(payload, "rows", 0, 0, tiled=True)

time: 63.5 us -> 62.6 us (0.986)
  Pallas kernels: 15.8 us -> 12.9 us
  waiting for transfers between devices: 6.02 us -> 7.33 us
    pallas_call x5, Pallas kernels: 15.8 us -> 12.9 us  [local(): pl.pallas_call(body, out_shape=out_shapes, in_specs=in_specs, out_specs=o...]
    all_to_all x1, waiting for transfers between devices: 6.02 us -> 7.33 us  [on_device(): table = lax.all_to_all(spread, 'rows', 0, 0, tiled=True).reshape(B, C)]
  transfers between devices with their start and end apart: 1 -> 1, of which waited for: 1 -> 1; matrix products, arithmetic and copies ran while one was open for 0% -> 0% of each run, Pallas kernels for 10% -> 8%
where the time goes in v3:
time: 62.6 us; the launch traced here: 61.9 us
  blocking collectives  29.8 us (48%)
  Pallas kernels  12.9 us (21%)
  starting transfers between devices  11.2 us (18%)
  waiting for transfers between devices  7.33 us (12%)
  between operations  0.67 us (1%)
    all_to_all x1, blocking collectives, on_device(): arrived = lax.all_to_all(payload, 'rows', 0, 0, tiled=True)  20.2 us
    pallas_call x5, Pallas kernels, local(): pl.pallas_call(body, out_shape=out_shapes, in_specs=in_specs, out_specs=o...  12.9 us
    all_to_all x1, starting transfers between devices, on_device(): table = lax.all_to_all(spread, 'rows', 0, 0, tiled=True).reshape(B, C)  11.2 us
    all_to_all x1, blocking collectives, on_device(): parts = lax.all_to_all(partial, 'feat', 0, 0, tiled=True)  9.59 us
    all_to_all x1, waiting for transfers between devices, on_device(): table = lax.all_to_all(spread, 'rows', 0, 0, tiled=True).reshape(B, C)  7.33 us
  transfers between devices with their start and end apart: 1, of which 1 were waited for; matrix products, arithmetic and copies ran while one was open for 0% of the time, Pallas kernels for 8%

profile of v3, /device:TPU:32, one launch (start us, length us, event | category | flops | bytes accessed | tf_op | source)
XLA Modules:
  0.0 61.9 jit_solution(14283818537163124229)
XLA Ops:
  0.6 1.4 %shard_map.86 = bf16[32,32,128]{2,1,0:T(8,128)(2,1)} custom-call(f32[32,128]{1,0:T(8,128)} %w_hbm.1), custom_call_target="tpu_custom_call" | custom-call | tf_op jit(solution)/shard_map/pallas_call | solution.py:394
  2.1 11.2 %all-to-all-start = ((bf16[32,32,128]{2,1,0:T(8,128)(2,1)}), bf16[32,32,128]{2,1,0:T(8,128)(2,1)S(1)}, u32[]{:S(2)}, u32[]{:S(2)}) async-start(bf16[32,32,128]{2,1,0:T(8,128)(2,1)} %shard_map.86), calls=%async_computation | async-start | bytes 524288 | tf_op jit(solution)/shard_map/all_to_all | solution.py:419
  13.3 4.8 %shard_map.85 = (bf16[1216,8,128]{2,1,0:T(8,128)(2,1)S(1)}, bf16[896,8,128]{2,1,0:T(8,128)(2,1)}, s32[32,1,512]{2,1,0:T(1,128)S(1)}, s32[32,1,512]{2,1,0:T(1,128)S(1)}, s32[2,256]{1,0:T(2,128)S(1)}) custom-call(s32[256]{0:T(256)} %bitcast.12, s32[1,256]{1,0:T(1,128)} %bitcast.13, s32[64,256]{1,0:T(8,128)} %bitcast.11, s32[1,256]{1,0:T(1,128)} %bitcast.14, ...), custom_call_target="tpu_custom_call" | custom-call | tf_op jit(solution)/shard_map/pallas_call | solution.py:394
  18.1 7.3 %all-to-all-done = bf16[32,32,128]{2,1,0:T(8,128)(2,1)S(1)} async-done(((bf16[32,32,128]{2,1,0:T(8,128)(2,1)}), bf16[32,32,128]{2,1,0:T(8,128)(2,1)S(1)}, u32[]{:S(2)}, u32[]{:S(2)}) %all-to-all-start) | async-done | bytes 262176 | tf_op jit(solution)/shard_map/all_to_all | solution.py:419
  25.5 2.5 %shard_map.87 = f32[8,1,256]{2,1,0:T(1,128)S(1)} custom-call(s32[2,256]{1,0:T(2,128)S(1)} %get-tuple-element.11.info_ref, bf16[1024,128]{1,0:T(8,128)(2,1)S(1)} %bitcast.9, s32[32,1,512]{2,1,0:T(1,128)S(1)} %get-tuple-element.12.ids_ref, s32[32,1,512]{2,1,0:T(1,128)S(1)} %get-tuple-element.13.ex_ref, bf16[1216,8,128]{2,1,0:T(8,128)(2,1)S(1)} %get-tuple-element.14.near_ref, ...), custom_call_target="tpu_custom_call" | custom-call | tf_op jit(solution)/shard_map/pallas_call | solution.py:394
  27.9 9.6 %all_to_all.15.parts_ref = f32[8,1,256]{2,1,0:T(1,128)S(1)} all-to-all(f32[8,1,256]{2,1,0:T(1,128)S(1)} %shard_map.87), channel_id=1, replica_groups=mesh['rows'=32,'feat'=8] {'feat'}, dimensions={0} | all-to-all | bytes 16384 | tf_op jit(solution)/shard_map/all_to_all | solution.py:461
  37.5 3.5 %shard_map.88 = bf16[32,40,128]{2,1,0:T(8,128)(2,1)S(1)} custom-call(s32[2,256]{1,0:T(2,128)S(1)} %get-tuple-element.11.info_ref, f32[8,1,256]{2,1,0:T(1,128)S(1)} %all_to_all.15.parts_ref, s32[1,256]{1,0:T(1,128)} %bitcast.16, s32[1,256]{1,0:T(1,128)} %bitcast.15, s32[32,1,512]{2,1,0:T(1,128)S(1)} %get-tuple-element.12.ids_ref, ...), custom_call_target="tpu_custom_call" | custom-call | tf_op jit(solution)/shard_map/pallas_call | solution.py:394
  41.0 20.2 %all_to_all.16.in_ref = bf16[32,40,128]{2,1,0:T(8,128)(2,1)S(1)} all-to-all(bf16[32,40,128]{2,1,0:T(8,128)(2,1)S(1)} %shard_map.88), channel_id=1, replica_groups=mesh['rows'=32,'feat'=8] {'rows'}, dimensions={0} | all-to-all | bytes 655360 | tf_op jit(solution)/shard_map/all_to_all | solution.py:482
  61.2 0.7 %shard_map.89 = (f32[32,128]{1,0:T(8,128)}, f32[1,256]{1,0:T(1,128)}, f32[1,1]{1,0:T(1,128)}) custom-call(bf16[32,40,128]{2,1,0:T(8,128)(2,1)S(1)} %all_to_all.16.in_ref), custom_call_target="tpu_custom_call" | custom-call | tf_op jit(solution)/shard_map/pallas_call | solution.py:394
Async XLA Ops:
  2.1 23.4 %all-to-all-start = ((bf16[32,32,128]{2,1,0:T(8,128)(2,1)}), bf16[32,32,128]{2,1,0:T(8,128)(2,1)S(1)}, u32[]{:S(2)}, u32[]{:S(2)}) async-start(bf16[32,32,128]{2,1,0:T(8,128)(2,1)} %shard_map.86), calls=%async_computation | async-start | bytes 524288 | tf_op jit(solution)/shard_map/all_to_all | solution.py:419

commit v4 on v3

--- a/solution.py
+++ b/solution.py
@@ -59,8 +59,8 @@
 
 
 def pack_tiles(
-    flat_hbm, counts_hbm, blocks_hbm, owner_hbm, values_hbm, near_ref, far_hbm, ids_ref, ex_ref,
-    info_ref, counts_s, counts_ref, blocks_ref, owner_ref, values, spill, small_sems, sems, out_sem
+    flat_hbm, counts_hbm, blocks_hbm, owner_hbm, labels_hbm, values_hbm, near_ref, far_hbm, ids_ref, ex_ref,
+    info_ref, counts_s, counts_ref, blocks_ref, owner_ref, labels_ref, values, spill, small_sems, sems, out_sem
 ):
     part = NG // LOADS
     small = [
@@ -71,6 +71,7 @@
                 (blocks_hbm, blocks_ref),
                 (owner_hbm, owner_ref),
                 (flat_hbm, counts_s),
+                (labels_hbm, labels_ref),
             ]
         )
     ]
@@ -112,6 +113,8 @@
     earlier = nn(hits.astype(BF16), before)
     info_ref[0:1, :] = jnp.sum(hits * earlier, axis=0, keepdims=True).astype(I32)
     info_ref[1:2, :] = jnp.full((1, E), total, I32)
+    info_ref[2:3, :] = owner_ref[...]
+    info_ref[3:4, :] = labels_ref[...]
 
     def place(k, carry):
         pos = k * CH + lane
@@ -250,17 +253,18 @@
         k = jnp.minimum(k, final)
         return k, near_ref[pl.ds(k * GCH, GCH)]
 
-    k0, first = fetch(0)
-    prepare(k0, tiles0, first)
+    def ahead(k):
+        for tiles, j in ((tiles0, k), (tiles1, k + 1)):
+            j, v = fetch(j)
+            prepare(j, tiles, v)
+
+    ahead(0)
 
     def pair(i, carry):
         k = 2 * i
-        k1, v1 = fetch(k + 1)
         choose(k, multiply(tiles0), k < near)
-        prepare(k1, tiles1, v1)
-        k2, v2 = fetch(k + 2)
-        choose(k1, multiply(tiles1), k + 1 < near)
-        prepare(k2, tiles0, v2)
+        choose(jnp.minimum(k + 1, final), multiply(tiles1), k + 1 < near)
+        ahead(k + 2)
         return carry
 
     lax.fori_loop(0, lax.shift_right_logical(near + 1, 1), pair, 0)
@@ -279,22 +283,14 @@
 
 
 def gradient_kernel(
-    info_ref, parts_ref, labels_hbm, owner_hbm, ids_ref, ex_ref, near_ref, far_hbm, out_ref,
-    labels_ref, owner_ref, buf, acc, column_ref, tiles0, tiles1, hot0, hot1, small_sems, sem
+    info_ref, parts_ref, ids_ref, ex_ref, near_ref, far_hbm, out_ref, buf, acc, column_ref,
+    tiles0, tiles1, hot0, hot1, sem
 ):
     chunks = lax.shift_right_logical(scalar(info_ref[1:2, :]) + (GCH - 1), 6)
-    small = [
-        pltpu.make_async_copy(labels_hbm, labels_ref, small_sems.at[0]),
-        pltpu.make_async_copy(owner_hbm, owner_ref, small_sems.at[1]),
-    ]
-    for copy in small:
-        copy.start()
     acc[...] = jnp.zeros_like(acc)
     margin = jnp.sum(parts_ref[...].reshape(F, E), axis=0, keepdims=True)
     small_exp = jnp.exp(-jnp.abs(margin))
-    for copy in small:
-        copy.wait()
-    label = labels_ref[...].astype(F32)
+    label = info_ref[3:4, :].astype(F32)
     resid = jax.nn.sigmoid(margin) - label
     loss = jnp.sum(jnp.maximum(margin, 0.0) + jnp.log1p(small_exp) - label * margin)
     half = resid.astype(BF16).astype(F32)
@@ -331,16 +327,16 @@
         k = jnp.minimum(k, final)
         return k, near_ref[pl.ds(k * GCH, GCH)], live
 
-    k0, v0, live0 = fetch(0)
-    prepare(k0, tiles0, hot0, v0, live0)
+    def ahead(k):
+        for tiles, hot, j in ((tiles0, hot0, k), (tiles1, hot1, k + 1)):
+            j, v, live = fetch(j)
+            prepare(j, tiles, hot, v, live)
+
+    ahead(0)
 
     def pair(i, carry):
-        k1, v1, live1 = fetch(2 * i + 1)
-        multiply(tiles0, hot0)
-        prepare(k1, tiles1, hot1, v1, live1)
-        k2, v2, live2 = fetch(2 * i + 2)
-        multiply(tiles1, hot1)
-        prepare(k2, tiles0, hot0, v2, live2)
+        acc[...] += nn(hot0[...], tiles0[...]) + nn(hot1[...], tiles1[...])
+        ahead(2 * i + 2)
         return carry
 
     lax.fori_loop(0, lax.shift_right_logical(near + 1, 1), pair, 0)
@@ -359,7 +355,7 @@
             acc[:, C * i : C * i + C].reshape(R // 2, 32, C).astype(BF16)
         )
 
-    owner_hit = iota((R, E), 0) == owner_ref[...]
+    owner_hit = iota((R, E), 0) == info_ref[2:3, :]
     rank = info_ref[0:1, :]
     lane_row = iota((C, E), 0)
     extra = jnp.zeros((R, C), F32)
@@ -426,23 +422,24 @@
             pltpu.HBM((NG - KAG, GR, C), BF16),
             pltpu.VMEM((NCH, 1, CH), I32),
             pltpu.VMEM((NCH, 1, CH), I32),
-            pltpu.VMEM((2, E), I32),
+            pltpu.VMEM((4, E), I32),
         ),
-        [ANY, ANY, ANY, ANY, ANY],
+        [ANY, ANY, ANY, ANY, ANY, ANY],
         (VMEM, ANY, VMEM, VMEM, VMEM),
         [
             pltpu.SMEM((E,), I32),
             pltpu.VMEM((1, E), I32),
             pltpu.VMEM((SLOT, E), I32),
             pltpu.VMEM((1, E), I32),
+            pltpu.VMEM((1, E), I32),
             pltpu.VMEM((NG, GR, C), BF16),
             pltpu.VMEM((NG - KAG + LEAD + GCH, GR, C), BF16),
-            dma((4,)),
+            dma((5,)),
             dma((LOADS,)),
             dma(()),
         ],
         16,
-        far(tile_counts.reshape(E)), far(tile_counts.T), far(tile_blocks.T), owner_row,
+        far(tile_counts.reshape(E)), far(tile_counts.T), far(tile_blocks.T), owner_row, label_row,
         far(tile_values.reshape(NG, GR, C)),
     )
     partial = local(
@@ -461,10 +458,8 @@
     parts = lax.all_to_all(partial, "feat", 0, 0, tiled=True)
     payload = local(
         gradient_kernel, pltpu.VMEM((R, B // R + XR, C), BF16),
-        [VMEM, VMEM, ANY, ANY, VMEM, VMEM, VMEM, ANY], VMEM,
+        [VMEM, VMEM, VMEM, VMEM, VMEM, ANY], VMEM,
         [
-            pltpu.VMEM((1, E), I32),
-            pltpu.VMEM((1, E), I32),
             pltpu.VMEM((GCH, GR, C), BF16),
             pltpu.VMEM((B // 2, 2 * C), F32),
             pltpu.VMEM((E + WIN, C), F32),
@@ -472,11 +467,10 @@
             pltpu.VMEM((CH, 2 * C), BF16),
             pltpu.VMEM((B // 2, CH), BF16),
             pltpu.VMEM((B // 2, CH), BF16),
-            dma((2,)),
             dma(()),
         ],
         16,
-        near(info), near(parts), label_row, owner_row, near(ids), near(ex), near(packed),
+        near(info), near(parts), near(ids), near(ex), near(packed),
         far(over),
     )
     arrived = lax.all_to_all(payload, "rows", 0, 0, tiled=True)

time: 62.6 us -> 61.1 us (0.976)
  Pallas kernels: 12.9 us -> 12.1 us
    pallas_call x5, Pallas kernels: 12.9 us -> 12.1 us  [local(): pl.pallas_call(body, out_shape=out_shapes, in_specs=in_specs, out_specs=o...]
where the time goes in v4:
time: 61.1 us; the launch traced here: 60.9 us
  blocking collectives  29.6 us (48%)
  Pallas kernels  12.1 us (20%)
  starting transfers between devices  11.2 us (18%)
  waiting for transfers between devices  7.29 us (12%)
  between operations  0.67 us (1%)
    all_to_all x1, blocking collectives, on_device(): arrived = lax.all_to_all(payload, 'rows', 0, 0, tiled=True)  20 us
    pallas_call x5, Pallas kernels, local(): pl.pallas_call(body, out_shape=out_shapes, in_specs=in_specs, out_specs=o...  12.1 us
    all_to_all x1, starting transfers between devices, on_device(): table = lax.all_to_all(spread, 'rows', 0, 0, tiled=True).reshape(B, C)  11.2 us
    all_to_all x1, blocking collectives, on_device(): parts = lax.all_to_all(partial, 'feat', 0, 0, tiled=True)  9.59 us
    all_to_all x1, waiting for transfers between devices, on_device(): table = lax.all_to_all(spread, 'rows', 0, 0, tiled=True).reshape(B, C)  7.29 us
  transfers between devices with their start and end apart: 1, of which 1 were waited for; matrix products, arithmetic and copies ran while one was open for 0% of the time, Pallas kernels for 8%

profile of v4, /device:TPU:32, one launch (start us, length us, event | category | flops | bytes accessed | tf_op | source)
XLA Modules:
  0.0 60.9 jit_solution(8528269494212460823)
XLA Ops:
  0.6 1.4 %shard_map.86 = bf16[32,32,128]{2,1,0:T(8,128)(2,1)} custom-call(f32[32,128]{1,0:T(8,128)} %w_hbm.1), custom_call_target="tpu_custom_call" | custom-call | tf_op jit(solution)/shard_map/pallas_call | solution.py:390
  2.1 11.2 %all-to-all-start = ((bf16[32,32,128]{2,1,0:T(8,128)(2,1)}), bf16[32,32,128]{2,1,0:T(8,128)(2,1)S(1)}, u32[]{:S(2)}, u32[]{:S(2)}) async-start(bf16[32,32,128]{2,1,0:T(8,128)(2,1)} %shard_map.86), calls=%async_computation | async-start | bytes 524288 | tf_op jit(solution)/shard_map/all_to_all | solution.py:415
  13.3 4.9 %shard_map.85 = (bf16[1216,8,128]{2,1,0:T(8,128)(2,1)S(1)}, bf16[896,8,128]{2,1,0:T(8,128)(2,1)}, s32[32,1,512]{2,1,0:T(1,128)S(1)}, s32[32,1,512]{2,1,0:T(1,128)S(1)}, s32[4,256]{1,0:T(4,128)S(1)}) custom-call(s32[256]{0:T(256)} %bitcast.12, s32[1,256]{1,0:T(1,128)} %bitcast.13, s32[64,256]{1,0:T(8,128)} %bitcast.11, s32[1,256]{1,0:T(1,128)} %bitcast.14, ...), custom_call_target="tpu_custom_call" | custom-call | tf_op jit(solution)/shard_map/pallas_call | solution.py:390
  18.2 7.3 %all-to-all-done = bf16[32,32,128]{2,1,0:T(8,128)(2,1)S(1)} async-done(((bf16[32,32,128]{2,1,0:T(8,128)(2,1)}), bf16[32,32,128]{2,1,0:T(8,128)(2,1)S(1)}, u32[]{:S(2)}, u32[]{:S(2)}) %all-to-all-start) | async-done | bytes 262176 | tf_op jit(solution)/shard_map/all_to_all | solution.py:415
  25.5 2.3 %shard_map.87 = f32[8,1,256]{2,1,0:T(1,128)S(1)} custom-call(s32[4,256]{1,0:T(4,128)S(1)} %get-tuple-element.11.info_ref, bf16[1024,128]{1,0:T(8,128)(2,1)S(1)} %bitcast.9, s32[32,1,512]{2,1,0:T(1,128)S(1)} %get-tuple-element.12.ids_ref, s32[32,1,512]{2,1,0:T(1,128)S(1)} %get-tuple-element.13.ex_ref, bf16[1216,8,128]{2,1,0:T(8,128)(2,1)S(1)} %get-tuple-element.14.near_ref, ...), custom_call_target="tpu_custom_call" | custom-call | tf_op jit(solution)/shard_map/pallas_call | solution.py:390
  27.7 9.6 %all_to_all.15.parts_ref = f32[8,1,256]{2,1,0:T(1,128)S(1)} all-to-all(f32[8,1,256]{2,1,0:T(1,128)S(1)} %shard_map.87), channel_id=1, replica_groups=mesh['rows'=32,'feat'=8] {'feat'}, dimensions={0} | all-to-all | bytes 16384 | tf_op jit(solution)/shard_map/all_to_all | solution.py:458
  37.3 2.8 %shard_map.88 = bf16[32,40,128]{2,1,0:T(8,128)(2,1)S(1)} custom-call(s32[4,256]{1,0:T(4,128)S(1)} %get-tuple-element.11.info_ref, f32[8,1,256]{2,1,0:T(1,128)S(1)} %all_to_all.15.parts_ref, s32[32,1,512]{2,1,0:T(1,128)S(1)} %get-tuple-element.12.ids_ref, s32[32,1,512]{2,1,0:T(1,128)S(1)} %get-tuple-element.13.ex_ref, ...), custom_call_target="tpu_custom_call" | custom-call | tf_op jit(solution)/shard_map/pallas_call | solution.py:390
  40.1 20.0 %all_to_all.16.in_ref = bf16[32,40,128]{2,1,0:T(8,128)(2,1)S(1)} all-to-all(bf16[32,40,128]{2,1,0:T(8,128)(2,1)S(1)} %shard_map.88), channel_id=1, replica_groups=mesh['rows'=32,'feat'=8] {'rows'}, dimensions={0} | all-to-all | bytes 655360 | tf_op jit(solution)/shard_map/all_to_all | solution.py:476
  60.1 0.7 %shard_map.89 = (f32[32,128]{1,0:T(8,128)}, f32[1,256]{1,0:T(1,128)}, f32[1,1]{1,0:T(1,128)}) custom-call(bf16[32,40,128]{2,1,0:T(8,128)(2,1)S(1)} %all_to_all.16.in_ref), custom_call_target="tpu_custom_call" | custom-call | tf_op jit(solution)/shard_map/pallas_call | solution.py:390
Async XLA Ops:
  2.1 23.4 %all-to-all-start = ((bf16[32,32,128]{2,1,0:T(8,128)(2,1)}), bf16[32,32,128]{2,1,0:T(8,128)(2,1)S(1)}, u32[]{:S(2)}, u32[]{:S(2)}) async-start(bf16[32,32,128]{2,1,0:T(8,128)(2,1)} %shard_map.86), calls=%async_computation | async-start | bytes 524288 | tf_op jit(solution)/shard_map/all_to_all | solution.py:415

commit v5 on v4

--- a/solution.py
+++ b/solution.py
@@ -224,7 +224,7 @@
     sub8 = iota((8, CH), 0)
 
     def prepare(k, tiles, source):
-        low, high = doubled(source.reshape(CH, C), ids_ref[k])
+        low, high = doubled(source, ids_ref[k])
         tiles[:, 0:C] = low
         tiles[:, C : 2 * C] = high
 
@@ -251,7 +251,7 @@
 
     def fetch(k):
         k = jnp.minimum(k, final)
-        return k, near_ref[pl.ds(k * GCH, GCH)]
+        return k, near_ref[pl.ds(pl.multiple_of(k * CH, CH), CH), :]
 
     def ahead(k):
         for tiles, j in ((tiles0, k), (tiles1, k + 1)):
@@ -270,7 +270,7 @@
     lax.fori_loop(0, lax.shift_right_logical(near + 1, 1), pair, 0)
 
     def outer(k, carry):
-        copy = pltpu.make_async_copy(far_hbm.at[pl.ds((k - KA) * GCH, GCH)], buf, sem)
+        copy = pltpu.make_async_copy(far_hbm.at[pl.ds(pl.multiple_of((k - KA) * CH, CH), CH)], buf, sem)
         copy.start()
         copy.wait()
         prepare(k, tiles0, buf[...])
@@ -307,17 +307,23 @@
         coef = jnp.sum(jnp.where(rows + base == ex_ref[k], column, 0.0), axis=0, keepdims=True)
         coef = jnp.where((ids >= 0) & live, coef, 0.0)
         low = jnp.where(lo_rows == (ids & 31), coef, 0.0).astype(BF16)
-        high = jnp.broadcast_to(lax.shift_right_arithmetic(ids, 5) & 15, (8, CH))
-        for h in range(16):
-            one = jnp.where(high == h, 1.0, 0.0)
-            mask = jnp.concatenate([one, one, one, one], axis=0).astype(BF16)
-            hot[32 * h : 32 * h + 32, :] = low * mask
-        lower, upper = doubled(source.reshape(CH, C), ids)
+        high = lax.shift_right_arithmetic(ids, 5) & 15
+        hot[0:32, :] = low
+        hot[32:48, :] = jnp.broadcast_to(high.astype(F32), (16, CH)).astype(BF16)
+        lower, upper = doubled(source, ids)
         tiles[:, 0:C] = lower
         tiles[:, C : 2 * C] = upper
 
+    def spread(hot):
+        low = [hot[0:16, :], hot[16:32, :]]
+        high = hot[32:48, :]
+        zero = jnp.zeros((), BF16)
+        return jnp.concatenate(
+            [jnp.where(high == h, part, zero) for h in range(16) for part in low], axis=0
+        )
+
     def multiply(tiles, hot):
-        acc[...] += nn(hot[...], tiles[...])
+        acc[...] += nn(spread(hot), tiles[...])
 
     near = jnp.minimum(chunks, KA)
     final = near - 1
@@ -325,7 +331,7 @@
     def fetch(k):
         live = k < near
         k = jnp.minimum(k, final)
-        return k, near_ref[pl.ds(k * GCH, GCH)], live
+        return k, near_ref[pl.ds(pl.multiple_of(k * CH, CH), CH), :], live
 
     def ahead(k):
         for tiles, hot, j in ((tiles0, hot0, k), (tiles1, hot1, k + 1)):
@@ -335,14 +341,14 @@
     ahead(0)
 
     def pair(i, carry):
-        acc[...] += nn(hot0[...], tiles0[...]) + nn(hot1[...], tiles1[...])
+        acc[...] += nn(spread(hot0), tiles0[...]) + nn(spread(hot1), tiles1[...])
         ahead(2 * i + 2)
         return carry
 
     lax.fori_loop(0, lax.shift_right_logical(near + 1, 1), pair, 0)
 
     def outer(k, carry):
-        copy = pltpu.make_async_copy(far_hbm.at[pl.ds((k - KA) * GCH, GCH)], buf, sem)
+        copy = pltpu.make_async_copy(far_hbm.at[pl.ds(pl.multiple_of((k - KA) * CH, CH), CH)], buf, sem)
         copy.start()
         copy.wait()
         prepare(k, tiles0, hot0, buf[...], k < chunks)
@@ -442,10 +448,12 @@
         far(tile_counts.reshape(E)), far(tile_counts.T), far(tile_blocks.T), owner_row, label_row,
         far(tile_values.reshape(NG, GR, C)),
     )
+    packed = packed.reshape(-1, C)
+    over = over.reshape(-1, C)
     partial = local(
         margins_kernel, pltpu.VMEM((F, 1, E), F32), [VMEM, VMEM, VMEM, VMEM, VMEM, ANY], VMEM,
         [
-            pltpu.VMEM((GCH, GR, C), BF16),
+            pltpu.VMEM((CH, C), BF16),
             pltpu.VMEM((E + WIN, CH), F32),
             pltpu.VMEM((B // 2, 2 * C), BF16),
             pltpu.VMEM((CH, 2 * C), BF16),
@@ -460,13 +468,13 @@
         gradient_kernel, pltpu.VMEM((R, B // R + XR, C), BF16),
         [VMEM, VMEM, VMEM, VMEM, VMEM, ANY], VMEM,
         [
-            pltpu.VMEM((GCH, GR, C), BF16),
+            pltpu.VMEM((CH, C), BF16),
             pltpu.VMEM((B // 2, 2 * C), F32),
             pltpu.VMEM((E + WIN, C), F32),
             pltpu.VMEM((CH, 2 * C), BF16),
             pltpu.VMEM((CH, 2 * C), BF16),
-            pltpu.VMEM((B // 2, CH), BF16),
-            pltpu.VMEM((B // 2, CH), BF16),
+            pltpu.VMEM((48, CH), BF16),
+            pltpu.VMEM((48, CH), BF16),
             dma(()),
         ],
         16,

time: 61.1 us -> 60.4 us (0.989)
  no operation moved by 1% of the time
where the time goes in v5:
time: 60.4 us; the launch traced here: 59.9 us
  blocking collectives  29.2 us (48%)
  Pallas kernels  11.6 us (19%)
  starting transfers between devices  11.2 us (19%)
  waiting for transfers between devices  7.29 us (12%)
  between operations  0.67 us (1%)
    all_to_all x1, blocking collectives, on_device(): arrived = lax.all_to_all(payload, 'rows', 0, 0, tiled=True)  19.6 us
    pallas_call x5, Pallas kernels, local(): pl.pallas_call(body, out_shape=out_shapes, in_specs=in_specs, out_specs=o...  11.6 us
    all_to_all x1, starting transfers between devices, on_device(): table = lax.all_to_all(spread, 'rows', 0, 0, tiled=True).reshape(B, C)  11.2 us
    all_to_all x1, blocking collectives, on_device(): parts = lax.all_to_all(partial, 'feat', 0, 0, tiled=True)  9.59 us
    all_to_all x1, waiting for transfers between devices, on_device(): table = lax.all_to_all(spread, 'rows', 0, 0, tiled=True).reshape(B, C)  7.29 us
  transfers between devices with their start and end apart: 1, of which 1 were waited for; matrix products, arithmetic and copies ran while one was open for 0% of the time, Pallas kernels for 8%

profile of v5, /device:TPU:32, one launch (start us, length us, event | category | flops | bytes accessed | tf_op | source)
XLA Modules:
  0.0 59.9 jit_solution(8261272568833872418)
XLA Ops:
  0.6 1.4 %shard_map.86 = bf16[32,32,128]{2,1,0:T(8,128)(2,1)} custom-call(f32[32,128]{1,0:T(8,128)} %w_hbm.1), custom_call_target="tpu_custom_call" | custom-call | tf_op jit(solution)/shard_map/pallas_call | solution.py:396
  2.1 11.2 %all-to-all-start = ((bf16[32,32,128]{2,1,0:T(8,128)(2,1)}), bf16[32,32,128]{2,1,0:T(8,128)(2,1)S(1)}, u32[]{:S(2)}, u32[]{:S(2)}) async-start(bf16[32,32,128]{2,1,0:T(8,128)(2,1)} %shard_map.86), calls=%async_computation | async-start | bytes 524288 | tf_op jit(solution)/shard_map/all_to_all | solution.py:421
  13.3 4.9 %shard_map.85 = (bf16[1216,8,128]{2,1,0:T(8,128)(2,1)S(1)}, bf16[896,8,128]{2,1,0:T(8,128)(2,1)}, s32[32,1,512]{2,1,0:T(1,128)S(1)}, s32[32,1,512]{2,1,0:T(1,128)S(1)}, s32[4,256]{1,0:T(4,128)S(1)}) custom-call(s32[256]{0:T(256)} %bitcast.18, s32[1,256]{1,0:T(1,128)} %bitcast.19, s32[64,256]{1,0:T(8,128)} %bitcast.17, s32[1,256]{1,0:T(1,128)} %bitcast.20, ...), custom_call_target="tpu_custom_call" | custom-call | tf_op jit(solution)/shard_map/pallas_call | solution.py:396
  18.2 7.3 %all-to-all-done = bf16[32,32,128]{2,1,0:T(8,128)(2,1)S(1)} async-done(((bf16[32,32,128]{2,1,0:T(8,128)(2,1)}), bf16[32,32,128]{2,1,0:T(8,128)(2,1)S(1)}, u32[]{:S(2)}, u32[]{:S(2)}) %all-to-all-start) | async-done | bytes 262176 | tf_op jit(solution)/shard_map/all_to_all | solution.py:421
  25.5 2.3 %shard_map.87 = f32[8,1,256]{2,1,0:T(1,128)S(1)} custom-call(s32[4,256]{1,0:T(4,128)S(1)} %get-tuple-element.11.info_ref, bf16[1024,128]{1,0:T(8,128)(2,1)S(1)} %bitcast.13, s32[32,1,512]{2,1,0:T(1,128)S(1)} %get-tuple-element.12.ids_ref, s32[32,1,512]{2,1,0:T(1,128)S(1)} %get-tuple-element.13.ex_ref, bf16[9728,128]{1,0:T(8,128)(2,1)S(1)} %bitcast.11, ...), custom_call_target="tpu_custom_call" | custom-call | tf_op jit(solution)/shard_map/pallas_call | solution.py:396
  27.7 9.6 %all_to_all.15.parts_ref = f32[8,1,256]{2,1,0:T(1,128)S(1)} all-to-all(f32[8,1,256]{2,1,0:T(1,128)S(1)} %shard_map.87), channel_id=1, replica_groups=mesh['rows'=32,'feat'=8] {'feat'}, dimensions={0} | all-to-all | bytes 16384 | tf_op jit(solution)/shard_map/all_to_all | solution.py:466
  37.3 2.3 %shard_map.88 = bf16[32,40,128]{2,1,0:T(8,128)(2,1)S(1)} custom-call(s32[4,256]{1,0:T(4,128)S(1)} %get-tuple-element.11.info_ref, f32[8,1,256]{2,1,0:T(1,128)S(1)} %all_to_all.15.parts_ref, s32[32,1,512]{2,1,0:T(1,128)S(1)} %get-tuple-element.12.ids_ref, s32[32,1,512]{2,1,0:T(1,128)S(1)} %get-tuple-element.13.ex_ref, bf16[9728,128]{1,0:T(8,128)(2,1)S(1)} %bitcast.12, ...), custom_call_target="tpu_custom_call" | custom-call | tf_op jit(solution)/shard_map/pallas_call | solution.py:396
  39.6 19.6 %all_to_all.16.in_ref = bf16[32,40,128]{2,1,0:T(8,128)(2,1)S(1)} all-to-all(bf16[32,40,128]{2,1,0:T(8,128)(2,1)S(1)} %shard_map.88), channel_id=1, replica_groups=mesh['rows'=32,'feat'=8] {'rows'}, dimensions={0} | all-to-all | bytes 655360 | tf_op jit(solution)/shard_map/all_to_all | solution.py:484
  59.2 0.7 %shard_map.89 = (f32[32,128]{1,0:T(8,128)}, f32[1,256]{1,0:T(1,128)}, f32[1,1]{1,0:T(1,128)}) custom-call(bf16[32,40,128]{2,1,0:T(8,128)(2,1)S(1)} %all_to_all.16.in_ref), custom_call_target="tpu_custom_call" | custom-call | tf_op jit(solution)/shard_map/pallas_call | solution.py:396
Async XLA Ops:
  2.1 23.4 %all-to-all-start = ((bf16[32,32,128]{2,1,0:T(8,128)(2,1)}), bf16[32,32,128]{2,1,0:T(8,128)(2,1)S(1)}, u32[]{:S(2)}, u32[]{:S(2)}) async-start(bf16[32,32,128]{2,1,0:T(8,128)(2,1)} %shard_map.86), calls=%async_computation | async-start | bytes 524288 | tf_op jit(solution)/shard_map/all_to_all | solution.py:421

commit v6 on v4

--- a/solution.py
+++ b/solution.py
@@ -21,12 +21,12 @@
 CH = 512
 GCH = CH // GR
 NCH = NG // GCH
-KA = 18
-KAG = KA * GCH
-LEAD = 2 * GCH
+KA = 10
+KF = NCH - KA
 XR = 8
 WIN = GCH + 8
 FUSED = 4
+EARLY = 2
 LOADS = 4
 
 VMEM = pl.BlockSpec(memory_space=pltpu.VMEM)
@@ -55,12 +55,15 @@
 def spread_weights(w_hbm, out_ref, w_ref, sem):
     pltpu.make_async_copy(w_hbm, w_ref, sem).start()
     pltpu.make_async_copy(w_hbm, w_ref, sem).wait()
-    out_ref[...] = jnp.broadcast_to(w_ref[...].astype(BF16)[None], out_ref.shape)
+    half = w_ref[...].astype(BF16)
+    both = jnp.concatenate([half[0:16], half[16:32]], axis=1)
+    out_ref[...] = jnp.broadcast_to(both[None], out_ref.shape)
 
 
 def pack_tiles(
-    flat_hbm, counts_hbm, blocks_hbm, owner_hbm, labels_hbm, values_hbm, near_ref, far_hbm, ids_ref, ex_ref,
-    info_ref, counts_s, counts_ref, blocks_ref, owner_ref, labels_ref, values, spill, small_sems, sems, out_sem
+    flat_hbm, counts_hbm, blocks_hbm, owner_hbm, labels_hbm, values_hbm, near_ref, far_hbm, ids_ref,
+    ex_ref, info_ref, counts_s, counts_ref, blocks_ref, owner_ref, labels_ref, values, packed, spill,
+    small_sems, sems, out_sem
 ):
     part = NG // LOADS
     small = [
@@ -129,77 +132,64 @@
         return carry
 
 
-    inside = jnp.sum(jnp.where(start[0:1] + 8.0 <= KAG, 1.0, 0.0)).astype(I32)
-    reach = jnp.sum(jnp.where(start[0:1] < KAG, 1.0, 0.0)).astype(I32)
-    blocks_inside = lax.shift_right_logical(inside, 3)
-
-    def after(e, off):
-        return off + lax.shift_right_logical(counts_s[e] + (GR - 1), 3)
-
     def put_eight(i, off):
         for j in range(8):
             e = i * 8 + j
-            near_ref[pl.ds(off, 8)] = values[pl.ds(e * 8, 8)]
-            off = after(e, off)
+            packed[pl.ds(off, 8)] = values[pl.ds(e * 8, 8)]
+            off = off + lax.shift_right_logical(counts_s[e] + (GR - 1), 3)
         return off
 
-    def put_both(e, off):
-        tiles = values[pl.ds(e * 8, 8)]
-        near_ref[pl.ds(off, 8)] = tiles
-        spill[pl.ds(off - KAG + LEAD, 8)] = tiles
-        return after(e, off)
-
-    def put_far(e, off):
-        spill[pl.ds(off - KAG + LEAD, 8)] = values[pl.ds(e * 8, 8)]
-        return after(e, off)
-
-    for copy in loads:
-        copy.wait()
+    def place_two(i, carry):
+        place(2 * i, 0)
+        return place(2 * i + 1, carry)
 
     def place_and_put(i, off):
-        place(2 * i, 0)
-        place(2 * i + 1, 0)
+        place(EARLY + i, 0)
         for j in range(FUSED):
             off = put_eight(FUSED * i + j, off)
         return off
 
-    @pl.when(inside == E)
-    def _():
-        lax.fori_loop(0, E // (8 * FUSED), place_and_put, 0)
-        lax.fori_loop(2 * E // (8 * FUSED), chunks, place, 0)
-
-    @pl.when(inside < E)
-    def _():
-        lax.fori_loop(0, chunks, place, 0)
-        off = lax.fori_loop(0, blocks_inside, put_eight, 0)
-        off = lax.fori_loop(blocks_inside * 8, reach, put_both, off)
-        lax.fori_loop(reach, E, put_far, off)
-
-    zeros = jnp.zeros((GCH, GR, C), BF16)
-
-    @pl.when(total <= KAG)
-    def _():
-        near_ref[pl.ds(total, GCH)] = zeros
-
-    @pl.when(total > KAG)
-    def _():
-        spill[pl.ds(total - KAG + LEAD, GCH)] = zeros
+    lax.fori_loop(0, EARLY // 2, place_two, 0)
+    for copy in loads:
+        copy.wait()
+    lax.fori_loop(0, E // (8 * FUSED), place_and_put, 0)
+    lax.fori_loop(EARLY + E // (8 * FUSED), chunks, place, 0)
+    packed[pl.ds(total, GCH)] = jnp.zeros((GCH, GR, C), BF16)
+
+    def widen(k, out, at):
+        low, high = doubled(packed[pl.ds(k * GCH, GCH)].reshape(CH, C), ids_ref[k])
+        span = pl.ds(pl.multiple_of(at * CH, CH), CH)
+        out[span, 0:C] = low
+        out[span, C : 2 * C] = high
+
+    near = jnp.minimum(chunks, KA)
+
+    def widen_pair(i, carry):
+        for k in (2 * i, jnp.minimum(2 * i + 1, near - 1)):
+            widen(k, near_ref, k)
+        return carry
+
+    lax.fori_loop(0, lax.shift_right_logical(near + 1, 1), widen_pair, 0)
 
     def send(k):
-        return pltpu.make_async_copy(
-            spill.at[pl.ds(LEAD + k * GCH, GCH)], far_hbm.at[pl.ds(k * GCH, GCH)], out_sem
-        )
+        span = pl.ds(pl.multiple_of(k * CH, CH), CH)
+        return pltpu.make_async_copy(spill.at[span], far_hbm.at[span], out_sem.at[k])
 
     def over(k, carry):
+        widen(k + KA, spill, k)
         send(k).start()
+        return carry
+
+    def arrive(k, carry):
         send(k).wait()
         return carry
 
     lax.fori_loop(0, chunks - KA, over, 0)
+    lax.fori_loop(0, chunks - KA, arrive, 0)
 
 
 def doubled(v, ids):
-    top = jnp.broadcast_to(jnp.where(ids >= B // 2, 1.0, 0.0), (8, CH)).T
+    top = jnp.broadcast_to(jnp.where((ids & 16) != 0, 1.0, 0.0), (8, CH)).T
     mask = jnp.broadcast_to(top[:, 0:1], (CH, C)).astype(BF16)
     high = v * mask
     return v - high, high
@@ -213,23 +203,45 @@
     return pl.multiple_of(lax.shift_right_logical(scalar(ex_ref[k]), 3) * 8, 8)
 
 
+def each_chunk(info_ref, near_ref, far_hbm, buf, sems, pair, single):
+    chunks = lax.shift_right_logical(scalar(info_ref[1:2, :]) + (GCH - 1), 6)
+    near = jnp.minimum(chunks, KA)
+
+    def fetch(k):
+        span = pl.ds(pl.multiple_of(k * CH, CH), CH)
+        return pltpu.make_async_copy(far_hbm.at[span], buf.at[span], sems.at[k])
+
+    def start(k, carry):
+        fetch(k).start()
+        return carry
+
+    lax.fori_loop(0, chunks - KA, start, 0)
+
+    def tiles(ref, k):
+        return ref[pl.ds(pl.multiple_of(k * CH, CH), CH), :]
+
+    def inner(i, carry):
+        k0 = 2 * i
+        k1 = jnp.minimum(k0 + 1, near - 1)
+        pair(k0, tiles(near_ref, k0), k1, tiles(near_ref, k1), k0 + 1 < near)
+        return carry
+
+    lax.fori_loop(0, lax.shift_right_logical(near + 1, 1), inner, 0)
+
+    def outer(k, carry):
+        fetch(k).wait()
+        single(k + KA, tiles(buf, k))
+        return carry
+
+    lax.fori_loop(0, chunks - KA, outer, 0)
+
+
 def margins_kernel(
-    info_ref, w_ref, ids_ref, ex_ref, near_ref, far_hbm, out_ref, buf, acc, wide, tiles0, tiles1, sem
+    info_ref, w_ref, ids_ref, ex_ref, near_ref, far_hbm, out_ref, buf, acc, sems
 ):
-    chunks = lax.shift_right_logical(scalar(info_ref[1:2, :]) + (GCH - 1), 6)
     acc[...] = jnp.zeros_like(acc)
-    wide[:, 0:C] = w_ref[0 : B // 2]
-    wide[:, C : 2 * C] = w_ref[B // 2 : B]
     rows = iota((WIN, CH), 0)
     sub8 = iota((8, CH), 0)
-
-    def prepare(k, tiles, source):
-        low, high = doubled(source.reshape(CH, C), ids_ref[k])
-        tiles[:, 0:C] = low
-        tiles[:, C : 2 * C] = high
-
-    def multiply(tiles):
-        return nt(wide[...], tiles[...])
 
     def choose(k, score, live):
         ids = ids_ref[k]
@@ -239,54 +251,32 @@
         while len(pieces) > 1:
             bit = (ids8 & half) != 0
             pieces = [jnp.where(bit, b, a) for a, b in zip(pieces[0::2], pieces[1::2])]
-            half *= 2
+            half = 32 if half == 8 else 2 * half
         pick = jnp.sum(jnp.where(sub8 == (ids8 & 7), pieces[0], 0.0), axis=0, keepdims=True)
         pick = jnp.where((ids >= 0) & live, pick, 0.0)
         base = window(ex_ref, k)
         span = pl.ds(base, WIN)
         acc[span, :] += jnp.where(rows + base == ex_ref[k], pick, 0.0)
 
-    near = jnp.minimum(chunks, KA)
-    final = near - 1
-
-    def fetch(k):
-        k = jnp.minimum(k, final)
-        return k, near_ref[pl.ds(k * GCH, GCH)]
-
-    def ahead(k):
-        for tiles, j in ((tiles0, k), (tiles1, k + 1)):
-            j, v = fetch(j)
-            prepare(j, tiles, v)
-
-    ahead(0)
-
-    def pair(i, carry):
-        k = 2 * i
-        choose(k, multiply(tiles0), k < near)
-        choose(jnp.minimum(k + 1, final), multiply(tiles1), k + 1 < near)
-        ahead(k + 2)
-        return carry
-
-    lax.fori_loop(0, lax.shift_right_logical(near + 1, 1), pair, 0)
-
-    def outer(k, carry):
-        copy = pltpu.make_async_copy(far_hbm.at[pl.ds((k - KA) * GCH, GCH)], buf, sem)
-        copy.start()
-        copy.wait()
-        prepare(k, tiles0, buf[...])
-        choose(k, multiply(tiles0), k < chunks)
-        return carry
-
-    lax.fori_loop(KA, chunks, outer, 0)
-    row = jnp.sum(acc[0:E, :].T, axis=0, keepdims=True)
+    def single(k, v):
+        choose(k, nt(w_ref[...], v), True)
+
+    def pair(k0, v0, k1, v1, live):
+        choose(k0, nt(w_ref[...], v0), True)
+        choose(k1, nt(w_ref[...], v1), live)
+
+    each_chunk(info_ref, near_ref, far_hbm, buf, sems, pair, single)
+    folded = acc[0:E, 0:C]
+    for i in range(1, CH // C):
+        folded = folded + acc[0:E, C * i : C * i + C]
+    row = jnp.sum(folded.T, axis=0, keepdims=True)
     out_ref[...] = jnp.broadcast_to(row[None], out_ref.shape)
 
 
 def gradient_kernel(
-    info_ref, parts_ref, ids_ref, ex_ref, near_ref, far_hbm, out_ref, buf, acc, column_ref,
-    tiles0, tiles1, hot0, hot1, sem
+    info_ref, parts_ref, ids_ref, ex_ref, near_ref, far_hbm, out_ref, buf, acc, column_ref, hot0, hot1,
+    sems
 ):
-    chunks = lax.shift_right_logical(scalar(info_ref[1:2, :]) + (GCH - 1), 6)
     acc[...] = jnp.zeros_like(acc)
     margin = jnp.sum(parts_ref[...].reshape(F, E), axis=0, keepdims=True)
     small_exp = jnp.exp(-jnp.abs(margin))
@@ -297,62 +287,46 @@
     column_ref[0:E, :] = jnp.broadcast_to(half, (C, E)).T
     column_ref[E : E + WIN, :] = jnp.zeros((WIN, C), F32)
     rows = iota((WIN, CH), 0)
-    lo_rows = iota((32, CH), 0)
-
-    def prepare(k, tiles, hot, source, live):
+    lo_rows = iota((16, CH), 0)
+
+    def prepare(k, hot, live):
         ids = ids_ref[k]
         base = window(ex_ref, k)
         column = column_ref[pl.ds(base, WIN), :]
         column = jnp.concatenate([column] * (CH // C), axis=1)
         coef = jnp.sum(jnp.where(rows + base == ex_ref[k], column, 0.0), axis=0, keepdims=True)
         coef = jnp.where((ids >= 0) & live, coef, 0.0)
-        low = jnp.where(lo_rows == (ids & 31), coef, 0.0).astype(BF16)
-        high = jnp.broadcast_to(lax.shift_right_arithmetic(ids, 5) & 15, (8, CH))
-        for h in range(16):
-            one = jnp.where(high == h, 1.0, 0.0)
-            mask = jnp.concatenate([one, one, one, one], axis=0).astype(BF16)
-            hot[32 * h : 32 * h + 32, :] = low * mask
-        lower, upper = doubled(source.reshape(CH, C), ids)
-        tiles[:, 0:C] = lower
-        tiles[:, C : 2 * C] = upper
-
-    def multiply(tiles, hot):
-        acc[...] += nn(hot[...], tiles[...])
-
+        hot[0:16, :] = jnp.where(lo_rows == (ids & 15), coef, 0.0).astype(BF16)
+        high = lax.shift_right_arithmetic(ids, 5).astype(F32)
+        hot[16:32, :] = jnp.broadcast_to(high, (16, CH)).astype(BF16)
+
+    def spread(hot):
+        low = hot[0:16, :]
+        high = hot[16:32, :]
+        zero = jnp.zeros((), BF16)
+        return jnp.concatenate([jnp.where(high == h, low, zero) for h in range(32)], axis=0)
+
+    def single(k, v):
+        prepare(k, hot0, True)
+        acc[...] += nn(spread(hot0), v)
+
+    chunks = lax.shift_right_logical(scalar(info_ref[1:2, :]) + (GCH - 1), 6)
     near = jnp.minimum(chunks, KA)
-    final = near - 1
-
-    def fetch(k):
-        live = k < near
-        k = jnp.minimum(k, final)
-        return k, near_ref[pl.ds(k * GCH, GCH)], live
 
     def ahead(k):
-        for tiles, hot, j in ((tiles0, hot0, k), (tiles1, hot1, k + 1)):
-            j, v, live = fetch(j)
-            prepare(j, tiles, hot, v, live)
+        for hot, j in ((hot0, k), (hot1, k + 1)):
+            prepare(jnp.minimum(j, near - 1), hot, j < near)
 
     ahead(0)
 
-    def pair(i, carry):
-        acc[...] += nn(hot0[...], tiles0[...]) + nn(hot1[...], tiles1[...])
-        ahead(2 * i + 2)
-        return carry
-
-    lax.fori_loop(0, lax.shift_right_logical(near + 1, 1), pair, 0)
-
-    def outer(k, carry):
-        copy = pltpu.make_async_copy(far_hbm.at[pl.ds((k - KA) * GCH, GCH)], buf, sem)
-        copy.start()
-        copy.wait()
-        prepare(k, tiles0, hot0, buf[...], k < chunks)
-        multiply(tiles0, hot0)
-        return carry
-
-    lax.fori_loop(KA, chunks, outer, 0)
+    def pair(k0, v0, k1, v1, live):
+        acc[...] += nn(spread(hot0), v0) + nn(spread(hot1), v1)
+        ahead(k0 + 2)
+
+    each_chunk(info_ref, near_ref, far_hbm, buf, sems, pair, single)
     for i in range(2):
-        out_ref[16 * i : 16 * i + 16, 0:32, :] = (
-            acc[:, C * i : C * i + C].reshape(R // 2, 32, C).astype(BF16)
+        out_ref[:, 16 * i : 16 * i + 16, :] = (
+            acc[:, C * i : C * i + C].reshape(R, 16, C).astype(BF16)
         )
 
     owner_hit = iota((R, E), 0) == info_ref[2:3, :]
@@ -409,17 +383,17 @@
     shape = jax.ShapeDtypeStruct
     dma = pltpu.SemaphoreType.DMA
     spread = local(
-        spread_weights, pltpu.VMEM((R, B // R, C), BF16), [ANY], VMEM,
+        spread_weights, pltpu.VMEM((R, B // (2 * R), 2 * C), BF16), [ANY], VMEM,
         [pltpu.VMEM((B // R, C), F32), dma(())], 4, far(weights),
     )
-    table = lax.all_to_all(spread, "rows", 0, 0, tiled=True).reshape(B, C)
+    table = lax.all_to_all(spread, "rows", 0, 0, tiled=True).reshape(B // 2, 2 * C)
     owner_row = far(owner_rank.reshape(1, E))
     label_row = far(labels.reshape(1, E))
     packed, over, ids, ex, info = local(
         pack_tiles,
         (
-            pltpu.VMEM((KAG + GCH, GR, C), BF16),
-            pltpu.HBM((NG - KAG, GR, C), BF16),
+            pltpu.VMEM((KA * CH, 2 * C), BF16),
+            pltpu.HBM((KF * CH, 2 * C), BF16),
             pltpu.VMEM((NCH, 1, CH), I32),
             pltpu.VMEM((NCH, 1, CH), I32),
             pltpu.VMEM((4, E), I32),
@@ -433,24 +407,22 @@
             pltpu.VMEM((1, E), I32),
             pltpu.VMEM((1, E), I32),
             pltpu.VMEM((NG, GR, C), BF16),
-            pltpu.VMEM((NG - KAG + LEAD + GCH, GR, C), BF16),
+            pltpu.VMEM((NG + GCH, GR, C), BF16),
+            pltpu.VMEM((KF * CH, 2 * C), BF16),
             dma((5,)),
             dma((LOADS,)),
-            dma(()),
+            dma((KF,)),
         ],
-        16,
+        24,
         far(tile_counts.reshape(E)), far(tile_counts.T), far(tile_blocks.T), owner_row, label_row,
         far(tile_values.reshape(NG, GR, C)),
     )
     partial = local(
         margins_kernel, pltpu.VMEM((F, 1, E), F32), [VMEM, VMEM, VMEM, VMEM, VMEM, ANY], VMEM,
         [
-            pltpu.VMEM((GCH, GR, C), BF16),
+            pltpu.VMEM((KF * CH, 2 * C), BF16),
             pltpu.VMEM((E + WIN, CH), F32),
-            pltpu.VMEM((B // 2, 2 * C), BF16),
-            pltpu.VMEM((CH, 2 * C), BF16),
-            pltpu.VMEM((CH, 2 * C), BF16),
-            dma(()),
+            dma((KF,)),
         ],
         16,
         near(info), near(table), near(ids), near(ex), near(packed), far(over),
@@ -460,14 +432,12 @@
         gradient_kernel, pltpu.VMEM((R, B // R + XR, C), BF16),
         [VMEM, VMEM, VMEM, VMEM, VMEM, ANY], VMEM,
         [
-            pltpu.VMEM((GCH, GR, C), BF16),
+            pltpu.VMEM((KF * CH, 2 * C), BF16),
             pltpu.VMEM((B // 2, 2 * C), F32),
             pltpu.VMEM((E + WIN, C), F32),
-            pltpu.VMEM((CH, 2 * C), BF16),
-            pltpu.VMEM((CH, 2 * C), BF16),
-            pltpu.VMEM((B // 2, CH), BF16),
-            pltpu.VMEM((B // 2, CH), BF16),
-            dma(()),
+            pltpu.VMEM((32, CH), BF16),
+            pltpu.VMEM((32, CH), BF16),
+            dma((KF,)),
         ],
         16,
         near(info), near(parts), near(ids), near(ex), near(packed),

time: 61.1 us -> 59.9 us (0.980)
  waiting for transfers between devices: 7.29 us -> 6.64 us
    all_to_all x1, waiting for transfers between devices: 7.29 us -> 6.64 us  [on_device(): lax.all_to_all(spread, 'rows', 0, 0, tiled=True).reshape(B // 2, 2 * C)]
  transfers between devices with their start and end apart: 1 -> 1, of which waited for: 1 -> 1; matrix products, arithmetic and copies ran while one was open for 0% -> 0% of each run, Pallas kernels for 8% -> 9%
where the time goes in v6:
time: 59.9 us; the launch traced here: 59.5 us
  blocking collectives  29.1 us (49%)
  Pallas kernels  11.8 us (20%)
  starting transfers between devices  11.2 us (19%)
  waiting for transfers between devices  6.64 us (11%)
  between operations  0.67 us (1%)
    all_to_all x1, blocking collectives, on_device(): arrived = lax.all_to_all(payload, 'rows', 0, 0, tiled=True)  19.6 us
    pallas_call x5, Pallas kernels, local(): pl.pallas_call(body, out_shape=out_shapes, in_specs=in_specs, out_specs=o...  11.8 us
    all_to_all x1, starting transfers between devices, on_device(): lax.all_to_all(spread, 'rows', 0, 0, tiled=True).reshape(B // 2, 2 * C)  11.2 us
    all_to_all x1, blocking collectives, on_device(): parts = lax.all_to_all(partial, 'feat', 0, 0, tiled=True)  9.57 us
    all_to_all x1, waiting for transfers between devices, on_device(): lax.all_to_all(spread, 'rows', 0, 0, tiled=True).reshape(B // 2, 2 * C)  6.64 us
  transfers between devices with their start and end apart: 1, of which 1 were waited for; matrix products, arithmetic and copies ran while one was open for 0% of the time, Pallas kernels for 9%

profile of v6, /device:TPU:32, one launch (start us, length us, event | category | flops | bytes accessed | tf_op | source)
XLA Modules:
  0.0 59.5 jit_solution(5177140135346310898)
XLA Ops:
  0.6 1.5 %shard_map.86 = bf16[32,16,256]{2,1,0:T(8,128)(2,1)} custom-call(f32[32,128]{1,0:T(8,128)} %w_hbm.1), custom_call_target="tpu_custom_call" | custom-call | tf_op jit(solution)/shard_map/pallas_call | solution.py:364
  2.1 11.2 %all-to-all-start = ((bf16[32,16,256]{2,1,0:T(8,128)(2,1)}), bf16[32,16,256]{2,1,0:T(8,128)(2,1)S(1)}, u32[]{:S(2)}, u32[]{:S(2)}) async-start(bf16[32,16,256]{2,1,0:T(8,128)(2,1)} %shard_map.86), calls=%async_computation | async-start | bytes 524288 | tf_op jit(solution)/shard_map/all_to_all | solution.py:389
  13.3 5.5 %shard_map.85 = (bf16[5120,256]{1,0:T(8,128)(2,1)S(1)}, bf16[11264,256]{1,0:T(8,128)(2,1)}, s32[32,1,512]{2,1,0:T(1,128)S(1)}, s32[32,1,512]{2,1,0:T(1,128)S(1)}, s32[4,256]{1,0:T(4,128)S(1)}) custom-call(s32[256]{0:T(256)} %bitcast.12, s32[1,256]{1,0:T(1,128)} %bitcast.13, s32[64,256]{1,0:T(8,128)} %bitcast.11, s32[1,256]{1,0:T(1,128)} %bitcast.14, ...), custom_call_target="tpu_custom_call" | custom-call | tf_op jit(solution)/shard_map/pallas_call | solution.py:364
  18.8 6.6 %all-to-all-done = bf16[32,16,256]{2,1,0:T(8,128)(2,1)S(1)} async-done(((bf16[32,16,256]{2,1,0:T(8,128)(2,1)}), bf16[32,16,256]{2,1,0:T(8,128)(2,1)S(1)}, u32[]{:S(2)}, u32[]{:S(2)}) %all-to-all-start) | async-done | bytes 262176 | tf_op jit(solution)/shard_map/all_to_all | solution.py:389
  25.5 2.0 %shard_map.87 = f32[8,1,256]{2,1,0:T(1,128)S(1)} custom-call(s32[4,256]{1,0:T(4,128)S(1)} %get-tuple-element.11.info_ref, bf16[512,256]{1,0:T(8,128)(2,1)S(1)} %bitcast.9, s32[32,1,512]{2,1,0:T(1,128)S(1)} %get-tuple-element.12.ids_ref, s32[32,1,512]{2,1,0:T(1,128)S(1)} %get-tuple-element.13.ex_ref, bf16[5120,256]{1,0:T(8,128)(2,1)S(1)} %get-tuple-element.14.near_ref, ...), custom_call_target="tpu_custom_call" | custom-call | tf_op jit(solution)/shard_map/pallas_call | solution.py:364
  27.5 9.6 %all_to_all.15.parts_ref = f32[8,1,256]{2,1,0:T(1,128)S(1)} all-to-all(f32[8,1,256]{2,1,0:T(1,128)S(1)} %shard_map.87), channel_id=1, replica_groups=mesh['rows'=32,'feat'=8] {'feat'}, dimensions={0} | all-to-all | bytes 16384 | tf_op jit(solution)/shard_map/all_to_all | solution.py:430
  37.0 2.2 %shard_map.88 = bf16[32,40,128]{2,1,0:T(8,128)(2,1)S(1)} custom-call(s32[4,256]{1,0:T(4,128)S(1)} %get-tuple-element.11.info_ref, f32[8,1,256]{2,1,0:T(1,128)S(1)} %all_to_all.15.parts_ref, s32[32,1,512]{2,1,0:T(1,128)S(1)} %get-tuple-element.12.ids_ref, s32[32,1,512]{2,1,0:T(1,128)S(1)} %get-tuple-element.13.ex_ref, ...), custom_call_target="tpu_custom_call" | custom-call | tf_op jit(solution)/shard_map/pallas_call | solution.py:364
  39.2 19.6 %all_to_all.16.in_ref = bf16[32,40,128]{2,1,0:T(8,128)(2,1)S(1)} all-to-all(bf16[32,40,128]{2,1,0:T(8,128)(2,1)S(1)} %shard_map.88), channel_id=1, replica_groups=mesh['rows'=32,'feat'=8] {'rows'}, dimensions={0} | all-to-all | bytes 655360 | tf_op jit(solution)/shard_map/all_to_all | solution.py:446
  58.8 0.7 %shard_map.89 = (f32[32,128]{1,0:T(8,128)}, f32[1,256]{1,0:T(1,128)}, f32[1,1]{1,0:T(1,128)}) custom-call(bf16[32,40,128]{2,1,0:T(8,128)(2,1)S(1)} %all_to_all.16.in_ref), custom_call_target="tpu_custom_call" | custom-call | tf_op jit(solution)/shard_map/pallas_call | solution.py:364
Async XLA Ops:
  2.1 23.4 %all-to-all-start = ((bf16[32,16,256]{2,1,0:T(8,128)(2,1)}), bf16[32,16,256]{2,1,0:T(8,128)(2,1)S(1)}, u32[]{:S(2)}, u32[]{:S(2)}) async-start(bf16[32,16,256]{2,1,0:T(8,128)(2,1)} %shard_map.86), calls=%async_computation | async-start | bytes 524288 | tf_op jit(solution)/shard_map/all_to_all | solution.py:389

commit v7 on v6

--- a/solution.py
+++ b/solution.py
@@ -21,8 +21,9 @@
 CH = 512
 GCH = CH // GR
 NCH = NG // GCH
-KA = 10
+KA = 11
 KF = NCH - KA
+GROUP = 11
 XR = 8
 WIN = GCH + 8
 FUSED = 4
@@ -165,11 +166,13 @@
     near = jnp.minimum(chunks, KA)
 
     def widen_pair(i, carry):
-        for k in (2 * i, jnp.minimum(2 * i + 1, near - 1)):
-            widen(k, near_ref, k)
-        return carry
-
-    lax.fori_loop(0, lax.shift_right_logical(near + 1, 1), widen_pair, 0)
+        for k in (2 * i, 2 * i + 1):
+            k = jnp.minimum(k, full - 1)
+            widen(jnp.minimum(k, near - 1), near_ref, k)
+        return carry
+
+    full = groups(near) * GROUP
+    lax.fori_loop(0, lax.shift_right_logical(full + 1, 1), widen_pair, 0)
 
     def send(k):
         span = pl.ds(pl.multiple_of(k * CH, CH), CH)
@@ -186,6 +189,10 @@
 
     lax.fori_loop(0, chunks - KA, over, 0)
     lax.fori_loop(0, chunks - KA, arrive, 0)
+
+
+def groups(near):
+    return lax.div(near + (GROUP - 1), GROUP)
 
 
 def doubled(v, ids):
@@ -203,7 +210,11 @@
     return pl.multiple_of(lax.shift_right_logical(scalar(ex_ref[k]), 3) * 8, 8)
 
 
-def each_chunk(info_ref, near_ref, far_hbm, buf, sems, pair, single):
+def tiles(ref, k, n):
+    return ref[pl.ds(pl.multiple_of(k * CH, CH), n * CH), :]
+
+
+def each_chunk(info_ref, far_hbm, buf, sems, group, single):
     chunks = lax.shift_right_logical(scalar(info_ref[1:2, :]) + (GCH - 1), 6)
     near = jnp.minimum(chunks, KA)
 
@@ -217,20 +228,15 @@
 
     lax.fori_loop(0, chunks - KA, start, 0)
 
-    def tiles(ref, k):
-        return ref[pl.ds(pl.multiple_of(k * CH, CH), CH), :]
-
     def inner(i, carry):
-        k0 = 2 * i
-        k1 = jnp.minimum(k0 + 1, near - 1)
-        pair(k0, tiles(near_ref, k0), k1, tiles(near_ref, k1), k0 + 1 < near)
-        return carry
-
-    lax.fori_loop(0, lax.shift_right_logical(near + 1, 1), inner, 0)
+        group(i * GROUP, near)
+        return carry
+
+    lax.fori_loop(0, groups(near), inner, 0)
 
     def outer(k, carry):
         fetch(k).wait()
-        single(k + KA, tiles(buf, k))
+        single(k + KA, tiles(buf, k, 1))
         return carry
 
     lax.fori_loop(0, chunks - KA, outer, 0)
@@ -261,11 +267,11 @@
     def single(k, v):
         choose(k, nt(w_ref[...], v), True)
 
-    def pair(k0, v0, k1, v1, live):
-        choose(k0, nt(w_ref[...], v0), True)
-        choose(k1, nt(w_ref[...], v1), live)
-
-    each_chunk(info_ref, near_ref, far_hbm, buf, sems, pair, single)
+    def group(k, near):
+        for j in range(GROUP):
+            choose(jnp.minimum(k + j, near - 1), nt(w_ref[...], tiles(near_ref, k + j, 1)), k + j < near)
+
+    each_chunk(info_ref, far_hbm, buf, sems, group, single)
     folded = acc[0:E, 0:C]
     for i in range(1, CH // C):
         folded = folded + acc[0:E, C * i : C * i + C]
@@ -274,8 +280,7 @@
 
 
 def gradient_kernel(
-    info_ref, parts_ref, ids_ref, ex_ref, near_ref, far_hbm, out_ref, buf, acc, column_ref, hot0, hot1,
-    sems
+    info_ref, parts_ref, ids_ref, ex_ref, near_ref, far_hbm, out_ref, buf, acc, column_ref, hots, sems
 ):
     acc[...] = jnp.zeros_like(acc)
     margin = jnp.sum(parts_ref[...].reshape(F, E), axis=0, keepdims=True)
@@ -286,48 +291,6 @@
     half = resid.astype(BF16).astype(F32)
     column_ref[0:E, :] = jnp.broadcast_to(half, (C, E)).T
     column_ref[E : E + WIN, :] = jnp.zeros((WIN, C), F32)
-    rows = iota((WIN, CH), 0)
-    lo_rows = iota((16, CH), 0)
-
-    def prepare(k, hot, live):
-        ids = ids_ref[k]
-        base = window(ex_ref, k)
-        column = column_ref[pl.ds(base, WIN), :]
-        column = jnp.concatenate([column] * (CH // C), axis=1)
-        coef = jnp.sum(jnp.where(rows + base == ex_ref[k], column, 0.0), axis=0, keepdims=True)
-        coef = jnp.where((ids >= 0) & live, coef, 0.0)
-        hot[0:16, :] = jnp.where(lo_rows == (ids & 15), coef, 0.0).astype(BF16)
-        high = lax.shift_right_arithmetic(ids, 5).astype(F32)
-        hot[16:32, :] = jnp.broadcast_to(high, (16, CH)).astype(BF16)
-
-    def spread(hot):
-        low = hot[0:16, :]
-        high = hot[16:32, :]
-        zero = jnp.zeros((), BF16)
-        return jnp.concatenate([jnp.where(high == h, low, zero) for h in range(32)], axis=0)
-
-    def single(k, v):
-        prepare(k, hot0, True)
-        acc[...] += nn(spread(hot0), v)
-
-    chunks = lax.shift_right_logical(scalar(info_ref[1:2, :]) + (GCH - 1), 6)
-    near = jnp.minimum(chunks, KA)
-
-    def ahead(k):
-        for hot, j in ((hot0, k), (hot1, k + 1)):
-            prepare(jnp.minimum(j, near - 1), hot, j < near)
-
-    ahead(0)
-
-    def pair(k0, v0, k1, v1, live):
-        acc[...] += nn(spread(hot0), v0) + nn(spread(hot1), v1)
-        ahead(k0 + 2)
-
-    each_chunk(info_ref, near_ref, far_hbm, buf, sems, pair, single)
-    for i in range(2):
-        out_ref[:, 16 * i : 16 * i + 16, :] = (
-            acc[:, C * i : C * i + C].reshape(R, 16, C).astype(BF16)
-        )
 
     owner_hit = iota((R, E), 0) == info_ref[2:3, :]
     rank = info_ref[0:1, :]
@@ -341,6 +304,51 @@
     for i, piece in enumerate(split3(jnp.full((R, C), loss, F32))):
         extra = jnp.where(lane == 3 * OWN + i, piece, extra)
     out_ref[:, 32 : 32 + XR, :] = jnp.broadcast_to(extra[:, None, :], (R, XR, C)).astype(BF16)
+
+    rows = iota((WIN, CH), 0)
+    lo_rows = iota((16, CH), 0)
+
+    def prepare(k, j, live):
+        hot = hots.at[j]
+        ids = ids_ref[k]
+        base = window(ex_ref, k)
+        column = column_ref[pl.ds(base, WIN), :]
+        column = jnp.concatenate([column] * (CH // C), axis=1)
+        coef = jnp.sum(jnp.where(rows + base == ex_ref[k], column, 0.0), axis=0, keepdims=True)
+        coef = jnp.where((ids >= 0) & live, coef, 0.0)
+        hot[0:16, :] = jnp.where(lo_rows == (ids & 15), coef, 0.0).astype(BF16)
+        high = lax.shift_right_arithmetic(ids, 5).astype(F32)
+        hot[16:32, :] = jnp.broadcast_to(high, (16, CH)).astype(BF16)
+
+    def spread(j):
+        low = hots[j, 0:16, :]
+        high = hots[j, 16:32, :]
+        zero = jnp.zeros((), BF16)
+        return jnp.concatenate([jnp.where(high == h, low, zero) for h in range(32)], axis=0)
+
+    def single(k, v):
+        prepare(k, 0, True)
+        acc[...] += nn(spread(0), v)
+
+    chunks = lax.shift_right_logical(scalar(info_ref[1:2, :]) + (GCH - 1), 6)
+    near = jnp.minimum(chunks, KA)
+
+    def ahead(k):
+        for j in range(GROUP):
+            prepare(jnp.minimum(k + j, near - 1), j, k + j < near)
+
+    ahead(0)
+
+    def group(k, near):
+        hot = jnp.concatenate([spread(j) for j in range(GROUP)], axis=1)
+        acc[...] += nn(hot, tiles(near_ref, k, GROUP))
+        ahead(k + GROUP)
+
+    each_chunk(info_ref, far_hbm, buf, sems, group, single)
+    for i in range(2):
+        out_ref[:, 16 * i : 16 * i + 16, :] = (
+            acc[:, C * i : C * i + C].reshape(R, 16, C).astype(BF16)
+        )
 
 
 def finish_kernel(in_ref, grad_ref, owned_ref, loss_ref):
@@ -435,8 +443,7 @@
             pltpu.VMEM((KF * CH, 2 * C), BF16),
             pltpu.VMEM((B // 2, 2 * C), F32),
             pltpu.VMEM((E + WIN, C), F32),
-            pltpu.VMEM((32, CH), BF16),
-            pltpu.VMEM((32, CH), BF16),
+            pltpu.VMEM((GROUP, 32, CH), BF16),
             dma((KF,)),
         ],
         16,

time: 59.9 us -> 59.1 us (0.987)
  Pallas kernels: 11.8 us -> 13.7 us
  blocking collectives: 29.1 us -> 27.4 us
  waiting for transfers between devices: 6.64 us -> 5.78 us
    pallas_call x5, Pallas kernels: 11.8 us -> 13.7 us  [local(): pl.pallas_call(body, out_shape=out_shapes, in_specs=in_specs, out_specs=o...]
    all_to_all x1, blocking collectives: 19.6 us -> 17.8 us  [on_device(): arrived = lax.all_to_all(payload, 'rows', 0, 0, tiled=True)]
    all_to_all x1, waiting for transfers between devices: 6.64 us -> 5.78 us  [on_device(): lax.all_to_all(spread, 'rows', 0, 0, tiled=True).reshape(B // 2, 2 * C)]
  transfers between devices with their start and end apart: 1 -> 1, of which waited for: 1 -> 1; matrix products, arithmetic and copies ran while one was open for 0% -> 0% of each run, Pallas kernels for 9% -> 11%
where the time goes in v7:
time: 59.1 us; the launch traced here: 58.8 us
  blocking collectives  27.4 us (46%)
  Pallas kernels  13.7 us (23%)
  starting transfers between devices  11.2 us (19%)
  waiting for transfers between devices  5.78 us (10%)
  between operations  0.67 us (1%)
    all_to_all x1, blocking collectives, on_device(): arrived = lax.all_to_all(payload, 'rows', 0, 0, tiled=True)  17.8 us
    pallas_call x5, Pallas kernels, local(): pl.pallas_call(body, out_shape=out_shapes, in_specs=in_specs, out_specs=o...  13.7 us
    all_to_all x1, starting transfers between devices, on_device(): lax.all_to_all(spread, 'rows', 0, 0, tiled=True).reshape(B // 2, 2 * C)  11.2 us
    all_to_all x1, blocking collectives, on_device(): parts = lax.all_to_all(partial, 'feat', 0, 0, tiled=True)  9.58 us
    all_to_all x1, waiting for transfers between devices, on_device(): lax.all_to_all(spread, 'rows', 0, 0, tiled=True).reshape(B // 2, 2 * C)  5.78 us
  transfers between devices with their start and end apart: 1, of which 1 were waited for; matrix products, arithmetic and copies ran while one was open for 0% of the time, Pallas kernels for 11%

profile of v7, /device:TPU:32, one launch (start us, length us, event | category | flops | bytes accessed | tf_op | source)
XLA Modules:
  0.0 58.8 jit_solution(7353679432038247942)
XLA Ops:
  0.6 1.5 %shard_map.86 = bf16[32,16,256]{2,1,0:T(8,128)(2,1)} custom-call(f32[32,128]{1,0:T(8,128)} %w_hbm.1), custom_call_target="tpu_custom_call" | custom-call | tf_op jit(solution)/shard_map/pallas_call | solution.py:372
  2.1 11.2 %all-to-all-start = ((bf16[32,16,256]{2,1,0:T(8,128)(2,1)}), bf16[32,16,256]{2,1,0:T(8,128)(2,1)S(1)}, u32[]{:S(2)}, u32[]{:S(2)}) async-start(bf16[32,16,256]{2,1,0:T(8,128)(2,1)} %shard_map.86), calls=%async_computation | async-start | bytes 524288 | tf_op jit(solution)/shard_map/all_to_all | solution.py:397
  13.3 6.4 %shard_map.85 = (bf16[5632,256]{1,0:T(8,128)(2,1)S(1)}, bf16[10752,256]{1,0:T(8,128)(2,1)}, s32[32,1,512]{2,1,0:T(1,128)S(1)}, s32[32,1,512]{2,1,0:T(1,128)S(1)}, s32[4,256]{1,0:T(4,128)S(1)}) custom-call(s32[256]{0:T(256)} %bitcast.12, s32[1,256]{1,0:T(1,128)} %bitcast.13, s32[64,256]{1,0:T(8,128)} %bitcast.11, s32[1,256]{1,0:T(1,128)} %bitcast.14, ...), custom_call_target="tpu_custom_call" | custom-call | tf_op jit(solution)/shard_map/pallas_call | solution.py:372
  19.7 5.8 %all-to-all-done = bf16[32,16,256]{2,1,0:T(8,128)(2,1)S(1)} async-done(((bf16[32,16,256]{2,1,0:T(8,128)(2,1)}), bf16[32,16,256]{2,1,0:T(8,128)(2,1)S(1)}, u32[]{:S(2)}, u32[]{:S(2)}) %all-to-all-start) | async-done | bytes 262176 | tf_op jit(solution)/shard_map/all_to_all | solution.py:397
  25.5 2.4 %shard_map.87 = f32[8,1,256]{2,1,0:T(1,128)S(1)} custom-call(s32[4,256]{1,0:T(4,128)S(1)} %get-tuple-element.11.info_ref, bf16[512,256]{1,0:T(8,128)(2,1)S(1)} %bitcast.9, s32[32,1,512]{2,1,0:T(1,128)S(1)} %get-tuple-element.12.ids_ref, s32[32,1,512]{2,1,0:T(1,128)S(1)} %get-tuple-element.13.ex_ref, bf16[5632,256]{1,0:T(8,128)(2,1)S(1)} %get-tuple-element.14.near_ref, ...), custom_call_target="tpu_custom_call" | custom-call | tf_op jit(solution)/shard_map/pallas_call | solution.py:372
  27.9 9.6 %all_to_all.15.parts_ref = f32[8,1,256]{2,1,0:T(1,128)S(1)} all-to-all(f32[8,1,256]{2,1,0:T(1,128)S(1)} %shard_map.87), channel_id=1, replica_groups=mesh['rows'=32,'feat'=8] {'feat'}, dimensions={0} | all-to-all | bytes 16384 | tf_op jit(solution)/shard_map/all_to_all | solution.py:438
  37.5 2.7 %shard_map.88 = bf16[32,40,128]{2,1,0:T(8,128)(2,1)S(1)} custom-call(s32[4,256]{1,0:T(4,128)S(1)} %get-tuple-element.11.info_ref, f32[8,1,256]{2,1,0:T(1,128)S(1)} %all_to_all.15.parts_ref, s32[32,1,512]{2,1,0:T(1,128)S(1)} %get-tuple-element.12.ids_ref, s32[32,1,512]{2,1,0:T(1,128)S(1)} %get-tuple-element.13.ex_ref, ...), custom_call_target="tpu_custom_call" | custom-call | tf_op jit(solution)/shard_map/pallas_call | solution.py:372
  40.3 17.8 %all_to_all.16.in_ref = bf16[32,40,128]{2,1,0:T(8,128)(2,1)S(1)} all-to-all(bf16[32,40,128]{2,1,0:T(8,128)(2,1)S(1)} %shard_map.88), channel_id=1, replica_groups=mesh['rows'=32,'feat'=8] {'rows'}, dimensions={0} | all-to-all | bytes 655360 | tf_op jit(solution)/shard_map/all_to_all | solution.py:453
  58.1 0.7 %shard_map.89 = (f32[32,128]{1,0:T(8,128)}, f32[1,256]{1,0:T(1,128)}, f32[1,1]{1,0:T(1,128)}) custom-call(bf16[32,40,128]{2,1,0:T(8,128)(2,1)S(1)} %all_to_all.16.in_ref), custom_call_target="tpu_custom_call" | custom-call | tf_op jit(solution)/shard_map/pallas_call | solution.py:372
Async XLA Ops:
  2.1 23.4 %all-to-all-start = ((bf16[32,16,256]{2,1,0:T(8,128)(2,1)}), bf16[32,16,256]{2,1,0:T(8,128)(2,1)S(1)}, u32[]{:S(2)}, u32[]{:S(2)}) async-start(bf16[32,16,256]{2,1,0:T(8,128)(2,1)} %shard_map.86), calls=%async_computation | async-start | bytes 524288 | tf_op jit(solution)/shard_map/all_to_all | solution.py:397

commit v8 on v7

--- a/solution.py
+++ b/solution.py
@@ -280,7 +280,7 @@
 
 
 def gradient_kernel(
-    info_ref, parts_ref, ids_ref, ex_ref, near_ref, far_hbm, out_ref, buf, acc, column_ref, hots, sems
+    info_ref, parts_ref, ids_ref, ex_ref, near_ref, far_hbm, out_ref, buf, acc, column_ref, sems
 ):
     acc[...] = jnp.zeros_like(acc)
     margin = jnp.sum(parts_ref[...].reshape(F, E), axis=0, keepdims=True)
@@ -308,41 +308,25 @@
     rows = iota((WIN, CH), 0)
     lo_rows = iota((16, CH), 0)
 
-    def prepare(k, j, live):
-        hot = hots.at[j]
+    def spread(k, live):
         ids = ids_ref[k]
         base = window(ex_ref, k)
         column = column_ref[pl.ds(base, WIN), :]
         column = jnp.concatenate([column] * (CH // C), axis=1)
         coef = jnp.sum(jnp.where(rows + base == ex_ref[k], column, 0.0), axis=0, keepdims=True)
         coef = jnp.where((ids >= 0) & live, coef, 0.0)
-        hot[0:16, :] = jnp.where(lo_rows == (ids & 15), coef, 0.0).astype(BF16)
+        low = jnp.where(lo_rows == (ids & 15), coef, 0.0).astype(BF16)
         high = lax.shift_right_arithmetic(ids, 5).astype(F32)
-        hot[16:32, :] = jnp.broadcast_to(high, (16, CH)).astype(BF16)
-
-    def spread(j):
-        low = hots[j, 0:16, :]
-        high = hots[j, 16:32, :]
+        high = jnp.broadcast_to(high, (16, CH)).astype(BF16)
         zero = jnp.zeros((), BF16)
         return jnp.concatenate([jnp.where(high == h, low, zero) for h in range(32)], axis=0)
 
     def single(k, v):
-        prepare(k, 0, True)
-        acc[...] += nn(spread(0), v)
-
-    chunks = lax.shift_right_logical(scalar(info_ref[1:2, :]) + (GCH - 1), 6)
-    near = jnp.minimum(chunks, KA)
-
-    def ahead(k):
-        for j in range(GROUP):
-            prepare(jnp.minimum(k + j, near - 1), j, k + j < near)
-
-    ahead(0)
+        acc[...] += nn(spread(k, True), v)
 
     def group(k, near):
-        hot = jnp.concatenate([spread(j) for j in range(GROUP)], axis=1)
-        acc[...] += nn(hot, tiles(near_ref, k, GROUP))
-        ahead(k + GROUP)
+        hot = [spread(jnp.minimum(k + j, near - 1), k + j < near) for j in range(GROUP)]
+        acc[...] += nn(jnp.concatenate(hot, axis=1), tiles(near_ref, k, GROUP))
 
     each_chunk(info_ref, far_hbm, buf, sems, group, single)
     for i in range(2):
@@ -443,7 +427,6 @@
             pltpu.VMEM((KF * CH, 2 * C), BF16),
             pltpu.VMEM((B // 2, 2 * C), F32),
             pltpu.VMEM((E + WIN, C), F32),
-            pltpu.VMEM((GROUP, 32, CH), BF16),
             dma((KF,)),
         ],
         16,

time: 59.1 us -> 58.8 us (level)
  no operation moved by 1% of the time
where the time goes in v8:
time: 58.8 us; the launch traced here: 58.5 us
  blocking collectives  27.4 us (47%)
  Pallas kernels  13.4 us (23%)
  starting transfers between devices  11.2 us (19%)
  waiting for transfers between devices  5.78 us (10%)
  between operations  0.67 us (1%)
    all_to_all x1, blocking collectives, on_device(): arrived = lax.all_to_all(payload, 'rows', 0, 0, tiled=True)  17.8 us
    pallas_call x5, Pallas kernels, local(): pl.pallas_call(body, out_shape=out_shapes, in_specs=in_specs, out_specs=o...  13.4 us
    all_to_all x1, starting transfers between devices, on_device(): lax.all_to_all(spread, 'rows', 0, 0, tiled=True).reshape(B // 2, 2 * C)  11.2 us
    all_to_all x1, blocking collectives, on_device(): parts = lax.all_to_all(partial, 'feat', 0, 0, tiled=True)  9.59 us
    all_to_all x1, waiting for transfers between devices, on_device(): lax.all_to_all(spread, 'rows', 0, 0, tiled=True).reshape(B // 2, 2 * C)  5.78 us
  transfers between devices with their start and end apart: 1, of which 1 were waited for; matrix products, arithmetic and copies ran while one was open for 0% of the time, Pallas kernels for 11%

profile of v8, /device:TPU:32, one launch (start us, length us, event | category | flops | bytes accessed | tf_op | source)
XLA Modules:
  0.0 58.5 jit_solution(875758500927252575)
XLA Ops:
  0.6 1.5 %shard_map.86 = bf16[32,16,256]{2,1,0:T(8,128)(2,1)} custom-call(f32[32,128]{1,0:T(8,128)} %w_hbm.1), custom_call_target="tpu_custom_call" | custom-call | tf_op jit(solution)/shard_map/pallas_call | solution.py:356
  2.1 11.2 %all-to-all-start = ((bf16[32,16,256]{2,1,0:T(8,128)(2,1)}), bf16[32,16,256]{2,1,0:T(8,128)(2,1)S(1)}, u32[]{:S(2)}, u32[]{:S(2)}) async-start(bf16[32,16,256]{2,1,0:T(8,128)(2,1)} %shard_map.86), calls=%async_computation | async-start | bytes 524288 | tf_op jit(solution)/shard_map/all_to_all | solution.py:381
  13.3 6.4 %shard_map.85 = (bf16[5632,256]{1,0:T(8,128)(2,1)S(1)}, bf16[10752,256]{1,0:T(8,128)(2,1)}, s32[32,1,512]{2,1,0:T(1,128)S(1)}, s32[32,1,512]{2,1,0:T(1,128)S(1)}, s32[4,256]{1,0:T(4,128)S(1)}) custom-call(s32[256]{0:T(256)} %bitcast.12, s32[1,256]{1,0:T(1,128)} %bitcast.13, s32[64,256]{1,0:T(8,128)} %bitcast.11, s32[1,256]{1,0:T(1,128)} %bitcast.14, ...), custom_call_target="tpu_custom_call" | custom-call | tf_op jit(solution)/shard_map/pallas_call | solution.py:356
  19.7 5.8 %all-to-all-done = bf16[32,16,256]{2,1,0:T(8,128)(2,1)S(1)} async-done(((bf16[32,16,256]{2,1,0:T(8,128)(2,1)}), bf16[32,16,256]{2,1,0:T(8,128)(2,1)S(1)}, u32[]{:S(2)}, u32[]{:S(2)}) %all-to-all-start) | async-done | bytes 262176 | tf_op jit(solution)/shard_map/all_to_all | solution.py:381
  25.5 2.4 %shard_map.87 = f32[8,1,256]{2,1,0:T(1,128)S(1)} custom-call(s32[4,256]{1,0:T(4,128)S(1)} %get-tuple-element.11.info_ref, bf16[512,256]{1,0:T(8,128)(2,1)S(1)} %bitcast.9, s32[32,1,512]{2,1,0:T(1,128)S(1)} %get-tuple-element.12.ids_ref, s32[32,1,512]{2,1,0:T(1,128)S(1)} %get-tuple-element.13.ex_ref, bf16[5632,256]{1,0:T(8,128)(2,1)S(1)} %get-tuple-element.14.near_ref, ...), custom_call_target="tpu_custom_call" | custom-call | tf_op jit(solution)/shard_map/pallas_call | solution.py:356
  27.9 9.6 %all_to_all.15.parts_ref = f32[8,1,256]{2,1,0:T(1,128)S(1)} all-to-all(f32[8,1,256]{2,1,0:T(1,128)S(1)} %shard_map.87), channel_id=1, replica_groups=mesh['rows'=32,'feat'=8] {'feat'}, dimensions={0} | all-to-all | bytes 16384 | tf_op jit(solution)/shard_map/all_to_all | solution.py:422
  37.5 2.4 %shard_map.88 = bf16[32,40,128]{2,1,0:T(8,128)(2,1)S(1)} custom-call(s32[4,256]{1,0:T(4,128)S(1)} %get-tuple-element.11.info_ref, f32[8,1,256]{2,1,0:T(1,128)S(1)} %all_to_all.15.parts_ref, s32[32,1,512]{2,1,0:T(1,128)S(1)} %get-tuple-element.12.ids_ref, s32[32,1,512]{2,1,0:T(1,128)S(1)} %get-tuple-element.13.ex_ref, ...), custom_call_target="tpu_custom_call" | custom-call | tf_op jit(solution)/shard_map/pallas_call | solution.py:356
  39.9 17.8 %all_to_all.16.in_ref = bf16[32,40,128]{2,1,0:T(8,128)(2,1)S(1)} all-to-all(bf16[32,40,128]{2,1,0:T(8,128)(2,1)S(1)} %shard_map.88), channel_id=1, replica_groups=mesh['rows'=32,'feat'=8] {'rows'}, dimensions={0} | all-to-all | bytes 655360 | tf_op jit(solution)/shard_map/all_to_all | solution.py:436
  57.7 0.7 %shard_map.89 = (f32[32,128]{1,0:T(8,128)}, f32[1,256]{1,0:T(1,128)}, f32[1,1]{1,0:T(1,128)}) custom-call(bf16[32,40,128]{2,1,0:T(8,128)(2,1)S(1)} %all_to_all.16.in_ref), custom_call_target="tpu_custom_call" | custom-call | tf_op jit(solution)/shard_map/pallas_call | solution.py:356
Async XLA Ops:
  2.1 23.4 %all-to-all-start = ((bf16[32,16,256]{2,1,0:T(8,128)(2,1)}), bf16[32,16,256]{2,1,0:T(8,128)(2,1)S(1)}, u32[]{:S(2)}, u32[]{:S(2)}) async-start(bf16[32,16,256]{2,1,0:T(8,128)(2,1)} %shard_map.86), calls=%async_computation | async-start | bytes 524288 | tf_op jit(solution)/shard_map/all_to_all | solution.py:381

commit v9 on v8

--- a/solution.py
+++ b/solution.py
@@ -23,11 +23,10 @@
 NCH = NG // GCH
 KA = 11
 KF = NCH - KA
-GROUP = 11
 XR = 8
 WIN = GCH + 8
 FUSED = 4
-EARLY = 2
+EARLY = KA - 8
 LOADS = 4
 
 VMEM = pl.BlockSpec(memory_space=pltpu.VMEM)
@@ -140,17 +139,14 @@
             off = off + lax.shift_right_logical(counts_s[e] + (GR - 1), 3)
         return off
 
-    def place_two(i, carry):
-        place(2 * i, 0)
-        return place(2 * i + 1, carry)
-
     def place_and_put(i, off):
         place(EARLY + i, 0)
         for j in range(FUSED):
             off = put_eight(FUSED * i + j, off)
         return off
 
-    lax.fori_loop(0, EARLY // 2, place_two, 0)
+    for k in range(EARLY):
+        place(k, 0)
     for copy in loads:
         copy.wait()
     lax.fori_loop(0, E // (8 * FUSED), place_and_put, 0)
@@ -167,12 +163,12 @@
 
     def widen_pair(i, carry):
         for k in (2 * i, 2 * i + 1):
-            k = jnp.minimum(k, full - 1)
             widen(jnp.minimum(k, near - 1), near_ref, k)
         return carry
 
-    full = groups(near) * GROUP
-    lax.fori_loop(0, lax.shift_right_logical(full + 1, 1), widen_pair, 0)
+    lax.fori_loop(0, KA // 2, widen_pair, 0)
+    for k in range(KA // 2 * 2, KA):
+        widen(jnp.minimum(k, near - 1), near_ref, k)
 
     def send(k):
         span = pl.ds(pl.multiple_of(k * CH, CH), CH)
@@ -189,10 +185,6 @@
 
     lax.fori_loop(0, chunks - KA, over, 0)
     lax.fori_loop(0, chunks - KA, arrive, 0)
-
-
-def groups(near):
-    return lax.div(near + (GROUP - 1), GROUP)
 
 
 def doubled(v, ids):
@@ -211,12 +203,17 @@
 
 
 def tiles(ref, k, n):
+    if isinstance(k, int):
+        return ref[k * CH : (k + n) * CH, :]
     return ref[pl.ds(pl.multiple_of(k * CH, CH), n * CH), :]
 
 
-def each_chunk(info_ref, far_hbm, buf, sems, group, single):
+def fold(x):
+    return sum(x[:, C * i : C * i + C] for i in range(1, CH // C)) + x[:, 0:C]
+
+
+def far_chunks(info_ref, far_hbm, buf, sems, near_work, far_work):
     chunks = lax.shift_right_logical(scalar(info_ref[1:2, :]) + (GCH - 1), 6)
-    near = jnp.minimum(chunks, KA)
 
     def fetch(k):
         span = pl.ds(pl.multiple_of(k * CH, CH), CH)
@@ -226,19 +223,13 @@
         fetch(k).start()
         return carry
 
-    lax.fori_loop(0, chunks - KA, start, 0)
-
-    def inner(i, carry):
-        group(i * GROUP, near)
-        return carry
-
-    lax.fori_loop(0, groups(near), inner, 0)
-
     def outer(k, carry):
         fetch(k).wait()
-        single(k + KA, tiles(buf, k, 1))
-        return carry
-
+        far_work(k + KA, tiles(buf, k, 1))
+        return carry
+
+    near_work()
+    lax.fori_loop(0, chunks - KA, start, 0)
     lax.fori_loop(0, chunks - KA, outer, 0)
 
 
@@ -249,7 +240,7 @@
     rows = iota((WIN, CH), 0)
     sub8 = iota((8, CH), 0)
 
-    def choose(k, score, live):
+    def choose(k, score):
         ids = ids_ref[k]
         ids8 = jnp.broadcast_to(ids, (8, CH))
         pieces = [score[8 * i : 8 * i + 8, :] for i in range(B // 16)]
@@ -259,35 +250,33 @@
             pieces = [jnp.where(bit, b, a) for a, b in zip(pieces[0::2], pieces[1::2])]
             half = 32 if half == 8 else 2 * half
         pick = jnp.sum(jnp.where(sub8 == (ids8 & 7), pieces[0], 0.0), axis=0, keepdims=True)
-        pick = jnp.where((ids >= 0) & live, pick, 0.0)
+        pick = jnp.where(ids >= 0, pick, 0.0)
         base = window(ex_ref, k)
         span = pl.ds(base, WIN)
-        acc[span, :] += jnp.where(rows + base == ex_ref[k], pick, 0.0)
-
-    def single(k, v):
-        choose(k, nt(w_ref[...], v), True)
-
-    def group(k, near):
-        for j in range(GROUP):
-            choose(jnp.minimum(k + j, near - 1), nt(w_ref[...], tiles(near_ref, k + j, 1)), k + j < near)
-
-    each_chunk(info_ref, far_hbm, buf, sems, group, single)
-    folded = acc[0:E, 0:C]
-    for i in range(1, CH // C):
-        folded = folded + acc[0:E, C * i : C * i + C]
-    row = jnp.sum(folded.T, axis=0, keepdims=True)
+        mine = jnp.where(rows + base == ex_ref[k], pick, 0.0)
+        acc[span, :] += fold(mine)
+
+    def near_work():
+        for k in range(KA):
+            choose(k, nt(w_ref[...], tiles(near_ref, k, 1)))
+
+    def far_work(k, v):
+        choose(k, nt(w_ref[...], v))
+
+    far_chunks(info_ref, far_hbm, buf, sems, near_work, far_work)
+    row = jnp.sum(acc[0:E, :].T, axis=0, keepdims=True)
     out_ref[...] = jnp.broadcast_to(row[None], out_ref.shape)
 
 
 def gradient_kernel(
     info_ref, parts_ref, ids_ref, ex_ref, near_ref, far_hbm, out_ref, buf, acc, column_ref, sems
 ):
-    acc[...] = jnp.zeros_like(acc)
     margin = jnp.sum(parts_ref[...].reshape(F, E), axis=0, keepdims=True)
     small_exp = jnp.exp(-jnp.abs(margin))
     label = info_ref[3:4, :].astype(F32)
     resid = jax.nn.sigmoid(margin) - label
-    loss = jnp.sum(jnp.maximum(margin, 0.0) + jnp.log1p(small_exp) - label * margin)
+    loss = jnp.maximum(margin, 0.0) + jnp.log1p(small_exp) - label * margin
+    loss = jnp.broadcast_to(jnp.sum(loss, axis=1, keepdims=True), (R, C))
     half = resid.astype(BF16).astype(F32)
     column_ref[0:E, :] = jnp.broadcast_to(half, (C, E)).T
     column_ref[E : E + WIN, :] = jnp.zeros((WIN, C), F32)
@@ -301,34 +290,34 @@
         b = jnp.where(lane_row == rank + OWN * i, 1.0, 0.0).astype(BF16)
         extra = extra + nt(a, b)
     lane = iota((R, C), 1)
-    for i, piece in enumerate(split3(jnp.full((R, C), loss, F32))):
+    for i, piece in enumerate(split3(loss)):
         extra = jnp.where(lane == 3 * OWN + i, piece, extra)
     out_ref[:, 32 : 32 + XR, :] = jnp.broadcast_to(extra[:, None, :], (R, XR, C)).astype(BF16)
 
     rows = iota((WIN, CH), 0)
     lo_rows = iota((16, CH), 0)
 
-    def spread(k, live):
+    def spread(k):
         ids = ids_ref[k]
         base = window(ex_ref, k)
         column = column_ref[pl.ds(base, WIN), :]
         column = jnp.concatenate([column] * (CH // C), axis=1)
         coef = jnp.sum(jnp.where(rows + base == ex_ref[k], column, 0.0), axis=0, keepdims=True)
-        coef = jnp.where((ids >= 0) & live, coef, 0.0)
+        coef = jnp.where(ids >= 0, coef, 0.0)
         low = jnp.where(lo_rows == (ids & 15), coef, 0.0).astype(BF16)
         high = lax.shift_right_arithmetic(ids, 5).astype(F32)
         high = jnp.broadcast_to(high, (16, CH)).astype(BF16)
         zero = jnp.zeros((), BF16)
         return jnp.concatenate([jnp.where(high == h, low, zero) for h in range(32)], axis=0)
 
-    def single(k, v):
-        acc[...] += nn(spread(k, True), v)
-
-    def group(k, near):
-        hot = [spread(jnp.minimum(k + j, near - 1), k + j < near) for j in range(GROUP)]
-        acc[...] += nn(jnp.concatenate(hot, axis=1), tiles(near_ref, k, GROUP))
-
-    each_chunk(info_ref, far_hbm, buf, sems, group, single)
+    def near_work():
+        hot = jnp.concatenate([spread(k) for k in range(KA)], axis=1)
+        acc[...] = nn(hot, tiles(near_ref, 0, KA))
+
+    def far_work(k, v):
+        acc[...] += nn(spread(k), v)
+
+    far_chunks(info_ref, far_hbm, buf, sems, near_work, far_work)
     for i in range(2):
         out_ref[:, 16 * i : 16 * i + 16, :] = (
             acc[:, C * i : C * i + C].reshape(R, 16, C).astype(BF16)
@@ -413,7 +402,7 @@
         margins_kernel, pltpu.VMEM((F, 1, E), F32), [VMEM, VMEM, VMEM, VMEM, VMEM, ANY], VMEM,
         [
             pltpu.VMEM((KF * CH, 2 * C), BF16),
-            pltpu.VMEM((E + WIN, CH), F32),
+            pltpu.VMEM((E + WIN, C), F32),
             dma((KF,)),
         ],
         16,

time: 58.8 us -> 58.5 us (level)
  no operation moved by 1% of the time
where the time goes in v9:
time: 58.5 us; the launch traced here: 58.2 us
  blocking collectives  27.4 us (47%)
  Pallas kernels  13.1 us (22%)
  starting transfers between devices  11.2 us (19%)
  waiting for transfers between devices  5.78 us (10%)
  between operations  0.67 us (1%)
    all_to_all x1, blocking collectives, on_device(): arrived = lax.all_to_all(payload, 'rows', 0, 0, tiled=True)  17.8 us
    pallas_call x5, Pallas kernels, local(): pl.pallas_call(body, out_shape=out_shapes, in_specs=in_specs, out_specs=o...  13.1 us
    all_to_all x1, starting transfers between devices, on_device(): lax.all_to_all(spread, 'rows', 0, 0, tiled=True).reshape(B // 2, 2 * C)  11.2 us
    all_to_all x1, blocking collectives, on_device(): parts = lax.all_to_all(partial, 'feat', 0, 0, tiled=True)  9.57 us
    all_to_all x1, waiting for transfers between devices, on_device(): lax.all_to_all(spread, 'rows', 0, 0, tiled=True).reshape(B // 2, 2 * C)  5.78 us
  transfers between devices with their start and end apart: 1, of which 1 were waited for; matrix products, arithmetic and copies ran while one was open for 0% of the time, Pallas kernels for 11%

profile of v9, /device:TPU:32, one launch (start us, length us, event | category | flops | bytes accessed | tf_op | source)
XLA Modules:
  0.0 58.2 jit_solution(1542394861804514281)
XLA Ops:
  0.6 1.5 %shard_map.86 = bf16[32,16,256]{2,1,0:T(8,128)(2,1)} custom-call(f32[32,128]{1,0:T(8,128)} %w_hbm.1), custom_call_target="tpu_custom_call" | custom-call | tf_op jit(solution)/shard_map/pallas_call | solution.py:345
  2.1 11.2 %all-to-all-start = ((bf16[32,16,256]{2,1,0:T(8,128)(2,1)}), bf16[32,16,256]{2,1,0:T(8,128)(2,1)S(1)}, u32[]{:S(2)}, u32[]{:S(2)}) async-start(bf16[32,16,256]{2,1,0:T(8,128)(2,1)} %shard_map.86), calls=%async_computation | async-start | bytes 524288 | tf_op jit(solution)/shard_map/all_to_all | solution.py:370
  13.3 6.4 %shard_map.85 = (bf16[5632,256]{1,0:T(8,128)(2,1)S(1)}, bf16[10752,256]{1,0:T(8,128)(2,1)}, s32[32,1,512]{2,1,0:T(1,128)S(1)}, s32[32,1,512]{2,1,0:T(1,128)S(1)}, s32[4,256]{1,0:T(4,128)S(1)}) custom-call(s32[256]{0:T(256)} %bitcast.12, s32[1,256]{1,0:T(1,128)} %bitcast.13, s32[64,256]{1,0:T(8,128)} %bitcast.11, s32[1,256]{1,0:T(1,128)} %bitcast.14, ...), custom_call_target="tpu_custom_call" | custom-call | tf_op jit(solution)/shard_map/pallas_call | solution.py:345
  19.7 5.8 %all-to-all-done = bf16[32,16,256]{2,1,0:T(8,128)(2,1)S(1)} async-done(((bf16[32,16,256]{2,1,0:T(8,128)(2,1)}), bf16[32,16,256]{2,1,0:T(8,128)(2,1)S(1)}, u32[]{:S(2)}, u32[]{:S(2)}) %all-to-all-start) | async-done | bytes 262176 | tf_op jit(solution)/shard_map/all_to_all | solution.py:370
  25.5 2.3 %shard_map.87 = f32[8,1,256]{2,1,0:T(1,128)S(1)} custom-call(s32[4,256]{1,0:T(4,128)S(1)} %get-tuple-element.11.info_ref, bf16[512,256]{1,0:T(8,128)(2,1)S(1)} %bitcast.9, s32[32,1,512]{2,1,0:T(1,128)S(1)} %get-tuple-element.12.ids_ref, s32[32,1,512]{2,1,0:T(1,128)S(1)} %get-tuple-element.13.ex_ref, bf16[5632,256]{1,0:T(8,128)(2,1)S(1)} %get-tuple-element.14.near_ref, ...), custom_call_target="tpu_custom_call" | custom-call | tf_op jit(solution)/shard_map/pallas_call | solution.py:345
  27.8 9.6 %all_to_all.15.parts_ref = f32[8,1,256]{2,1,0:T(1,128)S(1)} all-to-all(f32[8,1,256]{2,1,0:T(1,128)S(1)} %shard_map.87), channel_id=1, replica_groups=mesh['rows'=32,'feat'=8] {'feat'}, dimensions={0} | all-to-all | bytes 16384 | tf_op jit(solution)/shard_map/all_to_all | solution.py:411
  37.3 2.3 %shard_map.88 = bf16[32,40,128]{2,1,0:T(8,128)(2,1)S(1)} custom-call(s32[4,256]{1,0:T(4,128)S(1)} %get-tuple-element.11.info_ref, f32[8,1,256]{2,1,0:T(1,128)S(1)} %all_to_all.15.parts_ref, s32[32,1,512]{2,1,0:T(1,128)S(1)} %get-tuple-element.12.ids_ref, s32[32,1,512]{2,1,0:T(1,128)S(1)} %get-tuple-element.13.ex_ref, ...), custom_call_target="tpu_custom_call" | custom-call | tf_op jit(solution)/shard_map/pallas_call | solution.py:345
  39.6 17.8 %all_to_all.16.in_ref = bf16[32,40,128]{2,1,0:T(8,128)(2,1)S(1)} all-to-all(bf16[32,40,128]{2,1,0:T(8,128)(2,1)S(1)} %shard_map.88), channel_id=1, replica_groups=mesh['rows'=32,'feat'=8] {'rows'}, dimensions={0} | all-to-all | bytes 655360 | tf_op jit(solution)/shard_map/all_to_all | solution.py:425
  57.4 0.7 %shard_map.89 = (f32[32,128]{1,0:T(8,128)}, f32[1,256]{1,0:T(1,128)}, f32[1,1]{1,0:T(1,128)}) custom-call(bf16[32,40,128]{2,1,0:T(8,128)(2,1)S(1)} %all_to_all.16.in_ref), custom_call_target="tpu_custom_call" | custom-call | tf_op jit(solution)/shard_map/pallas_call | solution.py:345
Async XLA Ops:
  2.1 23.4 %all-to-all-start = ((bf16[32,16,256]{2,1,0:T(8,128)(2,1)}), bf16[32,16,256]{2,1,0:T(8,128)(2,1)S(1)}, u32[]{:S(2)}, u32[]{:S(2)}) async-start(bf16[32,16,256]{2,1,0:T(8,128)(2,1)} %shard_map.86), calls=%async_computation | async-start | bytes 524288 | tf_op jit(solution)/shard_map/all_to_all | solution.py:370
